TPU v7x, 32 devices: a whole 2x2x4 slice. The times are simulated.
32 devices in a mesh: row: 4 (over x, core), col: 4 (over z), depth: 2 (over y).
Axes of the slice: x: 2, y: 2, z: 4, core: 2. Of those that a mesh axis runs over, the one named last changes fastest.
Arguments:
- acts: bfloat16 [256, 32768], P('depth', 'row'), may hold values from -6 to 6
- act_mask: int32 [256, 256], P('depth', 'row'), may hold values 0 or 1
- w1: bfloat16 [256, 32, 128, 128], P(('row', 'depth'), 'col'), may hold values from -0.09375 to 0.09375
- cols1: int32 [256, 32], P('row', 'col'), may hold values from 0 to 255, as said below
- bias1: float32 [32768], P('col'), may hold values from -3 to 3
- mask2: int32 [256, 256], P('depth', 'col'), may hold values 0 or 1
- w2: bfloat16 [256, 32, 128, 128], P(('col', 'depth'), 'row'), may hold values from -0.1875 to 0.1875
- cols2: int32 [256, 32], P('col', 'row'), may hold values from 0 to 255, as said below
- bias2: float32 [32768], P(('row', 'col')), may hold values from -3 to 3
Outputs:
- result: bfloat16 [256, 32768], P('depth', ('row', 'col'))
Inputs may be any that keep to these rules, and one draw needn't show every extreme that they name: `cols1`: in each of the 256 block rows the 32 entries name different block columns, and for every g the entries g * 8 to g * 8 + 7 lie among block columns g * 64 to g * 64 + 63. `cols2`: in each of the 256 block rows the 32 entries name different block columns, and for every g the entries g * 8 to g * 8 + 7 lie among block columns g * 64 to g * 64 + 63.
All inputs are finite; a program needn't handle non-finite values. No bound on the sum of `act_mask` or of `mask2` on one device may be relied on, other than what follows from the above.
Results may differ from a plain program's by a relative error of at most 0.0047.
Values may be sent and summed in bfloat16 or wider, within the bound.
No kernel may reach another device: no remote copies, remote signals or barrier semaphores. Data moves between devices by JAX's collectives and lax.ppermute only.
A program may use at most 128 MiB of HBM per device.

v0:
```python
import jax
import jax.numpy as jnp
from jax import lax
from jax.sharding import PartitionSpec as P


def fold_function(inputs, targets, stride):

    def add_tiles(running_total, tiles, first_row):

        def advance(number, total):
            offset = number * stride
            block_list = lax.dynamic_slice_in_dim(tiles, offset, stride, 0)
            incoming_rows = lax.dynamic_slice_in_dim(inputs, offset, stride, 1)
            wanted = lax.dynamic_slice_in_dim(targets, offset, stride, 0)
            product = jnp.einsum(
                "tws,wish->twih", incoming_rows, block_list, preferred_element_type=jnp.float32
            )
            flat_product = product.reshape(product.shape[0], -1, product.shape[-1])
            return total.at[:, wanted.reshape(-1)].add(flat_product)

        return lax.fori_loop(0, tiles.shape[0] // stride, advance, running_total)

    return add_tiles


def on_device(acts, act_mask, w1, cols1, bias1, mask2, w2, cols2, bias2):
    block = w1.shape[-1]
    rows_dev = acts.shape[0]
    row_blocks = act_mask.shape[1]
    col_blocks = mask2.shape[1]
    row_index = lax.axis_index("row")
    col_index = lax.axis_index("col")
    masked = acts.reshape(rows_dev, row_blocks, block) * act_mask[:, :, None].astype(jnp.bfloat16)
    first_layer_destinations = cols1 - col_index * col_blocks
    second_targets = cols2 - row_index * row_blocks
    first_offset_value = jnp.zeros((rows_dev, col_blocks, block), jnp.float32)
    first_fold = fold_function(masked, first_layer_destinations, w1.shape[0])
    first_sum = first_fold(
        first_offset_value, lax.all_gather(w1, "depth", axis=0, tiled=True), jnp.int32(0)
    )
    bias_blocks = bias1.reshape(col_blocks, block)
    share = col_blocks // lax.axis_size("row")
    part_sum = lax.psum_scatter(first_sum, "row", scatter_dimension=1, tiled=True)
    bias_part = lax.dynamic_slice_in_dim(bias_blocks, row_index * share, share, 0)
    mask_part = lax.dynamic_slice_in_dim(mask2, row_index * share, share, 1)
    hidden_part = jnp.maximum(part_sum + bias_part, 0.0) * mask_part[:, :, None].astype(jnp.float32)
    hidden = lax.all_gather(hidden_part.astype(jnp.bfloat16), "row", axis=1, tiled=True)
    second_start = jnp.zeros((rows_dev, row_blocks, block), jnp.float32)
    second_fold = fold_function(hidden, second_targets, w2.shape[0])
    second_sum = second_fold(
        second_start, lax.all_gather(w2, "depth", axis=0, tiled=True), jnp.int32(0)
    )
    outcome = lax.psum_scatter(second_sum, "col", scatter_dimension=1, tiled=True)
    bias_out = bias2.reshape(outcome.shape[1], block)
    return jnp.maximum(outcome + bias_out, 0.0).astype(jnp.bfloat16).reshape(rows_dev, -1)


def solution(mesh):
    return jax.shard_map(
        on_device,
        mesh=mesh,
        in_specs=(
            P("depth", "row"),
            P("depth", "row"),
            P(("row", "depth"), "col", None, None),
            P("row", "col"),
            P("col"),
            P("depth", "col"),
            P(("col", "depth"), "row", None, None),
            P("col", "row"),
            P(("row", "col")),
        ),
        out_specs=P("depth", ("row", "col")),
        check_vma=False,
    )
```

profile of v0, /device:TPU:0, one launch (start us, length us, event | category | flops | bytes accessed | tf_op | source)
XLA Modules:
  0.0 905.7 jit_solution(17120707963761237808)
XLA Ops:
  6.5 0.0 all-gather.6.cloned.1.call-start
  6.5 0.7 all-gather.6.cloned.1.call-update
  7.3 0.0 reduce-scatter.3.cloned.1.call-start
  7.3 0.1 copy.35
  7.4 0.7 copy-done.3
  8.1 2.4 copy.36
  10.6 1.7 broadcast_multiply_fusion
  12.3 198.1 %all-gather.6.cloned.1.call-done = bf16[64,8,128,128]{3,2,1,0:T(8,128)(2,1)} async-done(((bf16[32,8,128,128]{3,2,1,0:T(8,128)(2,1)}), bf16[64,8,128,128]{3,2,1,0:T(8,128)(2,1)}) %all-gather.6.cloned.1.call-update) | async-done | bytes 16777232 | tf_op jit(solution)/shard_map/all_gather | solution.py:40
  210.5 2.6 broadcast.65.clone
  213.1 161.8 %while.26 = (s32[]{:T(128)}, f32[128,64,128]{2,0,1:T(8,128)}, s32[64,8]{1,0:T(8,128)S(1)}, bf16[64,8,128,128]{3,2,1,0:T(8,128)(2,1)}, bf16[128,64,128]{0,2,1:T(8...) while((s32[]{:T(128)}, f32[128,64,128]{2,0,1:T(8,128)}, s32[64,8]{1,0:T(8,128)S(1)}, ...), condition=%wide.region_2.0_spmd, body=%wide.region_0.0_spmd.sunk | while | flops 1077936896 | bytes 110108816 | solution.py:22
  213.1 11.5 %fusion.18 = f32[32,8,128,128]{3,2,1,0:T(8,128)} fusion(bf16[64,8,128,128]{3,2,1,0:T(8,128)(2,1)} %get-tuple-element.323, s32[]{:T(128)S(6)} %select_n.58, bf16[128,64,128]{0,2,1:T(8,128)(2,1)S(1)} %get-tuple-element.324), kind=kOutput, calls=%fused_computation.2.clone.1 | convolution fusion | flops 1073741824 | bytes 26215424 | tf_op jit(solution)/shard_map/while/body/eval_jaxpr/tws,wish->twih/dot_general | solution.py:16
  224.6 17.4 %copy.51 = f32[128,256,128]{2,0,1:T(8,128)} copy(f32[128,256,128]{0,2,1:T(8,128)} %bitcast.44) | data formatting | bytes 33554432 | tf_op jit(solution)/shard_map/while/body/eval_jaxpr/reshape | solution.py:19
  242.0 0.1 reshape.128
  242.1 51.9 %scatter_fusion = f32[128,64,128]{2,0,1:T(8,128)} fusion(f32[128,64,128]{2,0,1:T(8,128)} %get-tuple-element.312, s32[256]{0:T(256)S(1)} %bitcast.48, f32[256,128,128]{2,1,0:T(8,128)} %bitcast.42), kind=kCustom, calls=%fused_computation.clone.1 | custom fusion | flops 4194304 | bytes 50332672 | tf_op jit(solution)/shard_map/while/body/eval_jaxpr/scatter-add | solution.py:20
  294.0 11.5 %fusion.18 = f32[32,8,128,128]{3,2,1,0:T(8,128)} fusion(bf16[64,8,128,128]{3,2,1,0:T(8,128)(2,1)} %get-tuple-element.323, s32[]{:T(128)S(6)} %select_n.58, bf16[128,64,128]{0,2,1:T(8,128)(2,1)S(1)} %get-tuple-element.324), kind=kOutput, calls=%fused_computation.2.clone.1 | convolution fusion | flops 1073741824 | bytes 26215424 | tf_op jit(solution)/shard_map/while/body/eval_jaxpr/tws,wish->twih/dot_general | solution.py:16
  305.5 17.4 %copy.51 = f32[128,256,128]{2,0,1:T(8,128)} copy(f32[128,256,128]{0,2,1:T(8,128)} %bitcast.44) | data formatting | bytes 33554432 | tf_op jit(solution)/shard_map/while/body/eval_jaxpr/reshape | solution.py:19
  323.0 0.1 reshape.128
  323.1 51.8 %scatter_fusion = f32[128,64,128]{2,0,1:T(8,128)} fusion(f32[128,64,128]{2,0,1:T(8,128)} %get-tuple-element.312, s32[256]{0:T(256)S(1)} %bitcast.48, f32[256,128,128]{2,1,0:T(8,128)} %bitcast.42), kind=kCustom, calls=%fused_computation.clone.1 | custom fusion | flops 4194304 | bytes 50332672 | tf_op jit(solution)/shard_map/while/body/eval_jaxpr/scatter-add | solution.py:20
  374.9 5.6 copy.39
  380.5 0.0 reduce-scatter.3.cloned.1.call-update
  380.5 0.0 copy-start.7
  380.5 0.0 all-gather.4.cloned.1.call-start
  380.6 0.7 all-gather.4.cloned.1.call-update
  381.3 0.0 all-gather.8.cloned.1.call-start
  381.4 0.7 dynamic-slice_convert_fusion
  382.1 43.1 %reduce-scatter.3.cloned.1.call-done = f32[128,16,128]{0,2,1:T(8,128)} async-done(((f32[128,64,128]{0,2,1:T(8,128)}), f32[128,16,128]{0,2,1:T(8,128)}) %reduce-scatter.3.cloned.1.call-update) | async-done | bytes 1048592 | tf_op jit(solution)/shard_map/reduce_scatter | solution.py:44
  425.2 1.6 multiply_convert_fusion
  426.8 1.0 copy.40
  427.8 0.0 all-gather.8.cloned.1.call-update
  427.8 0.0 reduce-scatter.5.cloned.1.call-start
  427.9 0.1 copy.34
  428.0 197.7 %all-gather.4.cloned.1.call-done = bf16[64,8,128,128]{3,2,1,0:T(8,128)(2,1)} async-done(((bf16[32,8,128,128]{3,2,1,0:T(8,128)(2,1)}), bf16[64,8,128,128]{3,2,1,0:T(8,128)(2,1)}) %all-gather.4.cloned.1.call-update) | async-done | bytes 16777232 | tf_op jit(solution)/shard_map/all_gather | solution.py:52
  625.6 24.0 %all-gather.8.cloned.1.call-done = bf16[128,64,128]{2,0,1:T(8,128)(2,1)} async-done(((bf16[128,16,128]{2,0,1:T(8,128)(2,1)}), bf16[128,64,128]{2,0,1:T(8,128)(2,1)}) %all-gather.8.cloned.1.call-update) | async-done | bytes 2097168 | tf_op jit(solution)/shard_map/all_gather | solution.py:48
  649.6 2.6 broadcast.65
  652.2 162.1 %while.27 = (s32[]{:T(128)}, f32[128,64,128]{2,0,1:T(8,128)}, s32[64,8]{1,0:T(8,128)S(1)}, bf16[64,8,128,128]{3,2,1,0:T(8,128)(2,1)}, bf16[128,64,128]{2,0,1:T(8...) while((s32[]{:T(128)}, f32[128,64,128]{2,0,1:T(8,128)}, s32[64,8]{1,0:T(8,128)S(1)}, ...), condition=%wide.region_6.0_spmd, body=%wide.region_4.0_spmd.sunk | while | flops 1077936896 | bytes 110108816 | solution.py:22
  652.2 11.5 %fusion.21 = f32[32,8,128,128]{3,2,1,0:T(8,128)} fusion(bf16[64,8,128,128]{3,2,1,0:T(8,128)(2,1)} %get-tuple-element.350, s32[]{:T(128)S(6)} %select_n.60, bf16[128,64,128]{2,0,1:T(8,128)(2,1)S(1)} %get-tuple-element.351), kind=kOutput, calls=%fused_computation.9.clone.1 | convolution fusion | flops 1073741824 | bytes 26215424 | tf_op jit(solution)/shard_map/while/body/eval_jaxpr/tws,wish->twih/dot_general | solution.py:16
  663.8 17.4 %copy.52 = f32[128,256,128]{2,0,1:T(8,128)} copy(f32[128,256,128]{0,2,1:T(8,128)} %bitcast.45) | data formatting | bytes 33554432 | tf_op jit(solution)/shard_map/while/body/eval_jaxpr/reshape | solution.py:19
  681.2 0.1 reshape.131
  681.3 51.9 %scatter_fusion.1 = f32[128,64,128]{2,0,1:T(8,128)} fusion(f32[128,64,128]{2,0,1:T(8,128)} %get-tuple-element.339, s32[256]{0:T(256)S(1)} %bitcast.49, f32[256,128,128]{2,1,0:T(8,128)} %bitcast.43), kind=kCustom, calls=%fused_computation.1.clone.1 | custom fusion | flops 4194304 | bytes 50332672 | tf_op jit(solution)/shard_map/while/body/eval_jaxpr/scatter-add | solution.py:20
  733.2 11.5 %fusion.21 = f32[32,8,128,128]{3,2,1,0:T(8,128)} fusion(bf16[64,8,128,128]{3,2,1,0:T(8,128)(2,1)} %get-tuple-element.350, s32[]{:T(128)S(6)} %select_n.60, bf16[128,64,128]{2,0,1:T(8,128)(2,1)S(1)} %get-tuple-element.351), kind=kOutput, calls=%fused_computation.9.clone.1 | convolution fusion | flops 1073741824 | bytes 26215424 | tf_op jit(solution)/shard_map/while/body/eval_jaxpr/tws,wish->twih/dot_general | solution.py:16
  744.8 17.4 %copy.52 = f32[128,256,128]{2,0,1:T(8,128)} copy(f32[128,256,128]{0,2,1:T(8,128)} %bitcast.45) | data formatting | bytes 33554432 | tf_op jit(solution)/shard_map/while/body/eval_jaxpr/reshape | solution.py:19
  762.2 0.1 reshape.131
  762.3 52.0 %scatter_fusion.1 = f32[128,64,128]{2,0,1:T(8,128)} fusion(f32[128,64,128]{2,0,1:T(8,128)} %get-tuple-element.339, s32[256]{0:T(256)S(1)} %bitcast.49, f32[256,128,128]{2,1,0:T(8,128)} %bitcast.43), kind=kCustom, calls=%fused_computation.1.clone.1 | custom fusion | flops 4194304 | bytes 50332672 | tf_op jit(solution)/shard_map/while/body/eval_jaxpr/scatter-add | solution.py:20
  814.3 5.6 copy.42
  819.9 0.0 reduce-scatter.5.cloned.1.call-update
  820.0 76.6 %reduce-scatter.5.cloned.1.call-done = f32[128,16,128]{0,2,1:T(8,128)} async-done(((f32[128,64,128]{0,2,1:T(8,128)}), f32[128,16,128]{0,2,1:T(8,128)}) %reduce-scatter.5.cloned.1.call-update) | async-done | bytes 1048592 | tf_op jit(solution)/shard_map/reduce_scatter | solution.py:54
  896.6 1.6 maximum_convert_fusion
  898.2 1.0 copy.43
  (26 shorter events, 0.1 us)
Async XLA Ops:
  6.5 374.8 %copy-start = (f32[8192]{0:T(1024)S(1)}, f32[8192]{0:T(1024)}, u32[]{:S(2)}) copy-start(f32[8192]{0:T(1024)} %param.17) | copy-start | bytes 98308
  6.5 0.8 copy-start.6
  6.5 1.6 copy-start.3
  6.5 203.9 %all-gather.6.cloned.1.call-start = ((), (), s32[]{:S(2)}) async-start(), calls=%async_computation.3 | async-start | bytes 25165824 | tf_op jit(solution)/shard_map/all_gather | solution.py:40
  7.3 3.3 copy-start.4
  7.3 417.9 %reduce-scatter.3.cloned.1.call-start = ((), (), s32[]{:S(2)}) async-start(), calls=%async_computation.4 | async-start | bytes 5242880 | tf_op jit(solution)/shard_map/reduce_scatter | solution.py:44
  380.5 47.3 %copy-start.7 = (s32[64,8]{0,1:T(8,128)S(1)}, s32[64,8]{0,1:T(8,128)}, u32[]{:S(2)}) copy-start(s32[64,8]{0,1:T(8,128)} %param.20) | copy-start | bytes 6148
  380.5 245.1 %all-gather.4.cloned.1.call-start = ((), (), s32[]{:S(2)}) async-start(), calls=%async_computation.2 | async-start | bytes 25165824 | tf_op jit(solution)/shard_map/all_gather | solution.py:52
  381.3 268.4 %all-gather.8.cloned.1.call-start = ((), (), s32[]{:S(2)}) async-start(), calls=%async_computation.5 | async-start | bytes 2621440 | tf_op jit(solution)/shard_map/all_gather | solution.py:48
  427.8 468.8 %reduce-scatter.5.cloned.1.call-start = ((), (), s32[]{:S(2)}) async-start(), calls=%async_computation.6 | async-start | bytes 5242880 | tf_op jit(solution)/shard_map/reduce_scatter | solution.py:54
  649.6 2.6 copy-start.2
  814.3 84.9 %copy-start.1 = (f32[8192]{0:T(1024)S(1)}, f32[8192]{0:T(1024)}, u32[]{:S(2)}) copy-start(f32[8192]{0:T(1024)} %param.17) | copy-start | bytes 98308
  819.9 76.7 %copy-start.5 = (f32[2048]{0:T(1024)S(1)}, f32[2048]{0:T(1024)}, u32[]{:S(2)}) copy-start(f32[2048]{0:T(1024)} %param.21) | copy-start | bytes 24580
Sparse Core Ops, SparseCore 0:
  8.9 201.5 all-gather.5
  380.7 44.5 reduce-scatter.2
  426.8 198.8 all-gather.3
  627.1 22.5 all-gather.7
  820.1 76.4 reduce-scatter.4
where the time goes:
time: 910 us; the launch traced here: 906 us
  waiting for transfers between devices  541 us (59%)
  other arithmetic  213 us (23%)
  local copies, waits for them, and re-layouts  91.9 us (10%)
  matrix products  46.1 us (5%)
  between operations  13.2 us (1%)
    scatter-add x4, other arithmetic, advance(): return total.at[:, wanted.reshape(-1)].add(flat_product)  208 us
    all_gather x1, waiting for transfers between devices, on_device(): lax.all_gather(w1, 'depth', axis=0, tiled=True)  198 us
    all_gather x1, waiting for transfers between devices, on_device(): lax.all_gather(w2, 'depth', axis=0, tiled=True)  198 us
    reduce_scatter x1, waiting for transfers between devices, on_device(): lax.psum_scatter(second_sum, 'col', scatter_dimension=1, tiled=True)  76.6 us
    reshape x4, local copies, waits for them, and re-layouts, advance(): flat_product = product.reshape(product.shape[0], -1, product.shape[-1])  69.7 us
    dot_general x4, matrix products, advance(): jnp.einsum('tws,wish->twih', incoming_rows, block_list, preferred_element...  46.1 us
    reduce_scatter x1, waiting for transfers between devices, on_device(): lax.psum_scatter(first_sum, 'row', scatter_dimension=1, tiled=True)  43.1 us
    all_gather x1, waiting for transfers between devices, on_device(): lax.all_gather(hidden_part.astype(jnp.bfloat16), 'row', axis=1, tiled=True)  24 us
  transfers between devices with their start and end apart: 5, of which 5 were waited for; matrix products, arithmetic and copies ran while one was open for 1% of the time, Pallas kernels for 0%

commit v1 on v0

--- a/solution.py
+++ b/solution.py
@@ -1,12 +1,267 @@
+import functools
+
 import jax
 import jax.numpy as jnp
+import numpy as np
 from jax import lax
+from jax.experimental import pallas as pl
+from jax.experimental.pallas import tpu as pltpu
 from jax.sharding import PartitionSpec as P
 
 
+UNROLL = 4
+VMEM_LIMIT = 8 * 1024 * 1024
+
+
+def mask_kernel(half_ref, acts_ref, live_ref, out_ref):
+    blocks, _, block = out_ref.shape
+    live = live_ref[...].astype(jnp.float32).T
+    for i in range(blocks):
+        x = acts_ref[:, i * block:(i + 1) * block].astype(jnp.float32)
+        out_ref[i] = (x * live[:, i:i + 1]).astype(jnp.bfloat16)
+
+
+def masked_half(acts, act_mask, half):
+    rows, width = acts.shape
+    blocks = act_mask.shape[1] // 2
+    block = width // act_mask.shape[1]
+    steps = 2
+    return pl.pallas_call(
+        mask_kernel,
+        out_shape=pltpu.VMEM((blocks, rows, block), jnp.bfloat16),
+        grid_spec=pltpu.PrefetchScalarGridSpec(
+            num_scalar_prefetch=1,
+            grid=(steps,),
+            in_specs=[
+                pl.BlockSpec((rows, width // 2 // steps), lambda s, h: (0, h[0] * steps + s)),
+                pl.BlockSpec((blocks // steps, rows), lambda s, h: (h[0] * steps + s, 0)),
+            ],
+            out_specs=pl.BlockSpec((blocks // steps, rows, block), lambda s, h: (s, 0, 0)),
+        ),
+        compiler_params=pltpu.CompilerParams(vmem_limit_bytes=VMEM_LIMIT),
+        cost_estimate=pl.CostEstimate(flops=rows * width, bytes_accessed=2 * rows * width, transcendentals=0),
+    )(half.reshape(1), pltpu.with_memory_space_constraint(acts, pltpu.HBM), act_mask.T)
+
+
+def clear(acc):
+
+    def body(i, carry):
+        acc[i] = jnp.zeros_like(acc[i])
+        return carry
+
+    lax.fori_loop(0, acc.shape[0], body, 0, unroll=4)
+
+
+def add_products(acc, x_ref, w_ref, place_ref, start, first, count):
+    _, entries, block, _ = w_ref.shape
+
+    def advance(step, carry):
+        for i in range(UNROLL):
+            at = first + step * UNROLL + i
+            row = start + at
+            x = x_ref[at]
+            for k in range(0, entries, 2):
+                pair = jnp.concatenate([w_ref[row, k], w_ref[row, k + 1]], axis=1)
+                product = jnp.dot(x, pair, preferred_element_type=jnp.float32)
+                for half in range(2):
+                    to = place_ref[row * entries + k + half]
+                    acc[to] = acc[to] + product[:, half * block:(half + 1) * block]
+        return carry
+
+    lax.fori_loop(0, count // UNROLL, advance, 0)
+
+
+def write_out(acc, outs):
+    start = 0
+    for out in outs:
+
+        def body(i, carry, out=out, start=start):
+            out[i] = acc[start + i].astype(out.dtype)
+            return carry
+
+        lax.fori_loop(0, out.shape[0], body, 0, unroll=4)
+        start += out.shape[0]
+
+
+def fold_kernel(parts, load, starts_ref, place_ref, *refs):
+    x_refs, w_ref, refs = refs[:parts], refs[parts], refs[parts + 1:]
+    copies = []
+    if load:
+        *refs, sems = refs
+        *outs, keep_ref, acc = refs
+        for part, x_ref in enumerate(x_refs):
+            for first in range(0, x_ref.shape[0], UNROLL):
+                rows = pl.ds(starts_ref[part] + first, UNROLL)
+                copies.append(pltpu.make_async_copy(w_ref.at[rows], keep_ref.at[rows], sems.at[len(copies)]))
+        w_ref = keep_ref
+    else:
+        *outs, acc = refs
+    for copy in copies:
+        copy.start()
+    clear(acc)
+    for part, x_ref in enumerate(x_refs):
+        if load:
+            for first in range(0, x_ref.shape[0], UNROLL):
+                copies.pop(0).wait()
+                add_products(acc, x_ref, w_ref, place_ref, starts_ref[part], first, UNROLL)
+        else:
+            add_products(acc, x_ref, w_ref, place_ref, starts_ref[part], 0, x_ref.shape[0])
+    write_out(acc, outs)
+
+
+def fold(xs, weights, places, starts, segments, load=False):
+    rows_in, entries, block, _ = weights.shape
+    rows = xs[0].shape[1]
+    total = sum(count for count, _ in segments)
+    smem = pl.BlockSpec(memory_space=pltpu.SMEM)
+    vmem = pl.BlockSpec(memory_space=pltpu.VMEM)
+    hbm = pl.BlockSpec(memory_space=pltpu.HBM)
+    in_vmem = functools.partial(pltpu.with_memory_space_constraint, memory_space=pltpu.VMEM)
+    in_hbm = functools.partial(pltpu.with_memory_space_constraint, memory_space=pltpu.HBM)
+    out_shape = [pltpu.VMEM((count, rows, block), kind) for count, kind in segments]
+    scratch = [pltpu.VMEM((total, rows, block), jnp.float32)]
+    if load:
+        out_shape.append(pltpu.VMEM(weights.shape, weights.dtype))
+        scratch.append(pltpu.SemaphoreType.DMA((rows_in // UNROLL,)))
+    elif len(segments) == 1:
+        scratch = []
+    return pl.pallas_call(
+        functools.partial(fold_kernel, len(xs), load),
+        out_shape=out_shape,
+        in_specs=[smem, smem] + [vmem] * len(xs) + [hbm if load else vmem],
+        out_specs=[vmem] * len(out_shape),
+        scratch_shapes=scratch,
+        compiler_params=pltpu.CompilerParams(vmem_limit_bytes=VMEM_LIMIT),
+        cost_estimate=pl.CostEstimate(
+            flops=2 * rows * rows_in * entries * block * block,
+            bytes_accessed=2 * weights.size,
+            transcendentals=0,
+        ),
+    )(jnp.stack(starts), places.reshape(-1), *map(in_vmem, xs), (in_hbm if load else in_vmem)(weights))
+
+
+def finish_kernel(own_ref, up_ref, down_ref, bias_ref, out_ref):
+    share, _, block = own_ref.shape
+    for i in range(share):
+        total = own_ref[i] + up_ref[i].astype(jnp.float32) + down_ref[i].astype(jnp.float32)
+        out_ref[:, i * block:(i + 1) * block] = jnp.maximum(total + bias_ref[i:i + 1, :], 0.0).astype(jnp.bfloat16)
+
+
+def line_orders(size):
+    order, right, left = [], [], []
+    for place in range(size):
+        sends = []
+        for step in range(size - 1):
+            up = place + size - 1 - step
+            if place < up < size:
+                sends.append((step, 0, up))
+            down = place - size + 1 + step
+            if 0 <= down < place:
+                sends.append((step, 1, down))
+        chunks = [s[2] for s in sends] + [place]
+        order.append(chunks)
+        right.append([next((i for i, s in enumerate(sends) if s[:2] == (step, 0)), 0) for step in range(size - 1)])
+        left.append([next((i for i, s in enumerate(sends) if s[:2] == (step, 1)), 0) for step in range(size - 1)])
+    slots = np.argsort(np.array(order), axis=1)
+    return slots.astype(np.int32), np.array(right, np.int32), np.array(left, np.int32)
+
+
+def exchange_plan(acts, act_mask, w1, cols1, bias1, mask2, w2, cols2, bias2):
+    bf16, f32 = jnp.bfloat16, jnp.float32
+    block = w1.shape[-1]
+    rows = acts.shape[0]
+    row_blocks = act_mask.shape[1]
+    col_blocks = mask2.shape[1]
+    half_in = row_blocks // 2
+    half_mid = col_blocks // 2
+    quarter = col_blocks // 4
+    size_row, size_col = lax.axis_size("row"), lax.axis_size("col")
+    r, c, d = lax.axis_index("row"), lax.axis_index("col"), lax.axis_index("depth")
+    core = lax.rem(r, 2)
+    over_depth = functools.partial(lax.ppermute, axis_name="depth", perm=[(0, 1), (1, 0)])
+    over_core = functools.partial(lax.ppermute, axis_name="row", perm=[(i, i ^ 1) for i in range(size_row)])
+    over_x = functools.partial(lax.ppermute, axis_name="row", perm=[(i, i ^ 2) for i in range(size_row)])
+    zero = jnp.int32(0)
+
+    other_x = over_depth(masked_half(acts, act_mask, 1 - d))
+    own_x = masked_half(acts, act_mask, d)
+    mask_own = lax.dynamic_slice_in_dim(mask2, d * half_mid + core * quarter, quarter, 1).astype(bf16)
+    mask_other = over_depth(
+        lax.dynamic_slice_in_dim(mask2, (1 - d) * half_mid + core * quarter, quarter, 1).astype(bf16)
+    )
+    bias_blocks = lax.dynamic_slice_in_dim(
+        bias1.reshape(col_blocks, 1, block), d * half_mid + core * quarter, quarter, 0
+    )
+
+    to1 = lax.dynamic_slice_in_dim(cols1, d * half_in, half_in, 0) - c * col_blocks
+    to_depth = to1 // half_mid
+    to_core = (to1 // quarter) % 2
+    same_core = 1 - (to_core ^ core)
+    same_depth = 1 - (to_depth ^ d)
+    place1 = same_core * half_mid + same_depth * quarter + to1 % quarter
+
+    slots, right, left = line_orders(size_col)
+
+    def mine_of(table):
+        return sum(jnp.where(c == i, int(v), 0) for i, v in enumerate(table))
+
+    to2 = lax.dynamic_slice_in_dim(cols2, d * half_mid, half_mid, 0) - r * row_blocks
+    share = row_blocks // size_col
+    chunk = to2 // share
+    slot = sum(jnp.where(chunk == i, mine_of(slots[:, i]), 0) for i in range(size_col))
+    place2 = slot * share + to2 % share
+    own_x, mask_other, place1, place2 = lax.optimization_barrier((own_x, mask_other, place1, place2))
+
+    segments = [(half_mid, bf16), (quarter, f32), (quarter, f32)]
+
+    def core_sums(low, send, keep):
+        low = over_core(low)
+        return (send + low[:quarter].astype(f32)).astype(bf16), keep + low[quarter:].astype(f32)
+
+    *sums, w1 = fold([own_x], w1, place1, [zero], segments, load=True)
+    send_own, keep_own = core_sums(*sums)
+    got_other = over_depth(send_own)
+    sums = fold([other_x], w1, place1, [zero], segments)
+    send_other, keep_other = core_sums(*sums)
+    got_own = over_depth(send_other)
+
+    def hidden(keep, got, mask):
+        part = keep + got.astype(f32)
+        z1 = part + over_x(part.astype(bf16)).astype(f32)
+        out = (jnp.maximum(z1 + bias_blocks, 0.0) * mask.astype(f32).T[:, :, None]).astype(bf16)
+        return [out, over_core(out)]
+
+    hidden_other = hidden(keep_other, got_other, mask_other)
+    hidden_own = hidden(keep_own, got_own, mask_own)
+    starts = [core * quarter, (1 - core) * quarter]
+    *for_other, w2 = fold(hidden_other, w2, place2, starts, [(share, bf16)] * size_col, load=True)
+    from_other = [over_depth(part) for part in for_other]
+    (mine,) = fold(hidden_own, w2, place2, starts, [(row_blocks, f32)])
+    total = [mine[i * share:(i + 1) * share] + f.astype(f32) for i, f in enumerate(from_other)]
+
+    up = down = None
+    for step in range(size_col - 1):
+
+        def send(table, got):
+            pick = mine_of(table[:, step])
+            value = total[0]
+            for i in range(1, step + 1):
+                value = jnp.where(pick == i, total[i], value)
+            return (value if got is None else value + got.astype(f32)).astype(bf16)
+
+        go_up, go_down = send(right, up), send(left, down)
+        up = lax.ppermute(go_up, "col", [(i, i + 1) for i in range(step + 1)])
+        down = lax.ppermute(go_down, "col", [(size_col - 1 - i, size_col - 2 - i) for i in range(step + 1)])
+    return pl.pallas_call(
+        finish_kernel,
+        out_shape=jax.ShapeDtypeStruct((rows, share * block), bf16),
+        compiler_params=pltpu.CompilerParams(vmem_limit_bytes=VMEM_LIMIT),
+    )(total[-1], up, down, bias2.reshape(share, block))
+
+
 def fold_function(inputs, targets, stride):
 
-    def add_tiles(running_total, tiles, first_row):
+    def add_tiles(running_total, tiles):
 
         def advance(number, total):
             offset = number * stride
@@ -24,7 +279,7 @@
     return add_tiles
 
 
-def on_device(acts, act_mask, w1, cols1, bias1, mask2, w2, cols2, bias2):
+def gather_plan(acts, act_mask, w1, cols1, bias1, mask2, w2, cols2, bias2):
     block = w1.shape[-1]
     rows_dev = acts.shape[0]
     row_blocks = act_mask.shape[1]
@@ -32,12 +287,11 @@
     row_index = lax.axis_index("row")
     col_index = lax.axis_index("col")
     masked = acts.reshape(rows_dev, row_blocks, block) * act_mask[:, :, None].astype(jnp.bfloat16)
-    first_layer_destinations = cols1 - col_index * col_blocks
+    first_targets = cols1 - col_index * col_blocks
     second_targets = cols2 - row_index * row_blocks
-    first_offset_value = jnp.zeros((rows_dev, col_blocks, block), jnp.float32)
-    first_fold = fold_function(masked, first_layer_destinations, w1.shape[0])
+    first_fold = fold_function(masked, first_targets, w1.shape[0])
     first_sum = first_fold(
-        first_offset_value, lax.all_gather(w1, "depth", axis=0, tiled=True), jnp.int32(0)
+        jnp.zeros((rows_dev, col_blocks, block), jnp.float32), lax.all_gather(w1, "depth", axis=0, tiled=True)
     )
     bias_blocks = bias1.reshape(col_blocks, block)
     share = col_blocks // lax.axis_size("row")
@@ -46,10 +300,9 @@
     mask_part = lax.dynamic_slice_in_dim(mask2, row_index * share, share, 1)
     hidden_part = jnp.maximum(part_sum + bias_part, 0.0) * mask_part[:, :, None].astype(jnp.float32)
     hidden = lax.all_gather(hidden_part.astype(jnp.bfloat16), "row", axis=1, tiled=True)
-    second_start = jnp.zeros((rows_dev, row_blocks, block), jnp.float32)
     second_fold = fold_function(hidden, second_targets, w2.shape[0])
     second_sum = second_fold(
-        second_start, lax.all_gather(w2, "depth", axis=0, tiled=True), jnp.int32(0)
+        jnp.zeros((rows_dev, row_blocks, block), jnp.float32), lax.all_gather(w2, "depth", axis=0, tiled=True)
     )
     outcome = lax.psum_scatter(second_sum, "col", scatter_dimension=1, tiled=True)
     bias_out = bias2.reshape(outcome.shape[1], block)
@@ -57,8 +310,10 @@
 
 
 def solution(mesh):
+    sizes = dict(mesh.shape)
+    pairs = sizes["depth"] == 2 and sizes["row"] == 4
     return jax.shard_map(
-        on_device,
+        exchange_plan if pairs else gather_plan,
         mesh=mesh,
         in_specs=(
             P("depth", "row"),

time: 910 us -> 172 us (0.19)
  waiting for transfers between devices: 541 us -> 96.5 us
  other arithmetic: 213 us -> 11.9 us
  local copies, waits for them, and re-layouts: 91.9 us -> 1.87 us
  matrix products: 46.1 us -> 0 us
  starting transfers between devices: 0.16 us -> 33.7 us
  Pallas kernels: 0 us -> 26.7 us
  between operations: 13.2 us -> 0.19 us
    all_gather x3 -> x0, waiting for transfers between devices: 420 us -> none  [the longest x1 198 us: on_device(): lax.all_gather(w1, 'depth', axis=0, tiled=True)]
    scatter-add x4 -> x0, other arithmetic: 208 us -> none  [advance(): return total.at[:, wanted.reshape(-1)].add(flat_product)]
    reduce_scatter x2 -> x0, waiting for transfers between devices: 120 us -> none  [the longest x1 76.6 us: on_device(): lax.psum_scatter(second_sum, 'col', scatter_dimension=1, tiled=True)]
    ppermute x0 -> x20, waiting for transfers between devices: none -> 96.5 us  [the longest x2 20.7 us: hidden(): z1 = part + over_x(part.astype(bf16)).astype(f32)]
    reshape x9 -> x2, local copies, waits for them, and re-layouts: 71.1 us -> 0.18 us  [fold(): places.reshape(-1)]
    dot_general x4 -> x0, matrix products: 46.1 us -> none  [advance(): jnp.einsum('tws,wish->twih', incoming_rows, block_list, preferred_element...]
    ppermute x0 -> x20, starting transfers between devices: none -> 33.7 us  [the longest x3 15.3 us: exchange_plan(): up = lax.ppermute(go_up, 'col', [(i, i + 1) for i in range(step + 1)])]
    pallas_call x0 -> x7, Pallas kernels: none -> 26.7 us  [the longest x4 20.8 us: fold(): pl.pallas_call(functools.partial(fold_kernel, len(xs), load), out_shape=o...]
  transfers between devices with their start and end apart: 5 -> 20, of which waited for: 5 -> 12; matrix products, arithmetic and copies ran while one was open for 1% -> 5% of each run, Pallas kernels for 0% -> 13%
where the time goes in v1:
time: 172 us; the launch traced here: 171 us
  waiting for transfers between devices  96.5 us (56%)
  starting transfers between devices  33.7 us (20%)
  Pallas kernels  26.7 us (16%)
  other arithmetic  11.9 us (7%)
  local copies, waits for them, and re-layouts  1.87 us (1%)
    pallas_call x4, Pallas kernels, fold(): pl.pallas_call(functools.partial(fold_kernel, len(xs), load), out_shape=o...  20.8 us
    ppermute x2, waiting for transfers between devices, hidden(): z1 = part + over_x(part.astype(bf16)).astype(f32)  20.7 us
    ppermute x1, waiting for transfers between devices, exchange_plan(): over_depth(lax.dynamic_slice_in_dim(mask2, (1 - d) * half_mid + core * qu...  19.1 us
    ppermute x4, waiting for transfers between devices, exchange_plan(): from_other = [over_depth(part) for part in for_other]  17.2 us
    ppermute x3, starting transfers between devices, exchange_plan(): up = lax.ppermute(go_up, 'col', [(i, i + 1) for i in range(step + 1)])  15.3 us
    ppermute x1, waiting for transfers between devices, exchange_plan(): got_other = over_depth(send_own)  12.2 us
    ppermute x1, waiting for transfers between devices, exchange_plan(): got_own = over_depth(send_other)  10.4 us
    ppermute x3, waiting for transfers between devices, exchange_plan(): up = lax.ppermute(go_up, 'col', [(i, i + 1) for i in range(step + 1)])  9.26 us
  transfers between devices with their start and end apart: 20, of which 12 were waited for; matrix products, arithmetic and copies ran while one was open for 5% of the time, Pallas kernels for 13%

profile of v1, /device:TPU:0, one launch (start us, length us, event | category | flops | bytes accessed | tf_op | source)
XLA Modules:
  0.0 170.9 jit_solution(3487902593204895113)
XLA Ops:
  0.0 0.8 copy-done.3
  0.8 2.8 %shard_map.93 = bf16[32,128,128]{2,1,0:T(8,128)(2,1)} custom-call(s32[1]{0:T(128)} %bitcast.4.half_ref, bf16[128,8192]{1,0:T(8,128)(2,1)} %acts_ref.3, s32[64,128]{1,0:T(8,128)S(1)} %bitcast.14), custom_call_target="tpu_custom_call" | custom-call | flops 1048576 | bytes 2097152 | tf_op jit(solution)/shard_map/pallas_call | solution.py:29
  3.6 3.0 %collective-permute-start.2 = (bf16[32,128,128]{2,1,0:T(8,128)(2,1)}, bf16[32,128,128]{2,1,0:T(8,128)(2,1)S(1)}, u32[]{:S(2)}, u32[]{:S(2)}) collective-permute-start(bf16[32,128,128]{2,1,0:T(8,128)(2,1)} %shard_map.93), channel_id=1, source_target_pairs={{0,1},{1,0},{2,3},{3,2},{4,5},{5,4},{6,7},{7,6},{8,9},{9,8},{10,11... | collective-permute-start | bytes 3145736 | tf_op jit(solution)/shard_map/ppermute | solution.py:186
  6.6 0.7 convert_bitcast_fusion.1
  7.3 0.8 fusion.7
  8.1 0.7 copy-done.4
  8.9 2.0 %shard_map.91.refs_0_ = bf16[32,128,128]{2,1,0:T(8,128)(2,1)S(1)} custom-call(s32[1]{0:T(128)} %bitcast.2.half_ref, bf16[128,8192]{1,0:T(8,128)(2,1)} %acts_ref.3, s32[64,128]{1,0:T(8,128)S(1)} %bitcast.15), custom_call_target="tpu_custom_call" | custom-call | flops 1048576 | bytes 2097152 | tf_op jit(solution)/shard_map/pallas_call | solution.py:29
  10.9 19.1 %collective-permute-done = bf16[128,16]{0,1:T(8,128)(2,1)S(1)} collective-permute-done((bf16[128,16]{0,1:T(8,128)(2,1)S(1)}, bf16[128,16]{0,1:T(8,128)(2,1)S(1)}, u32[]{:S(2)}, u32[]{:S(2)}) %collective-permute-start) | collective-permute-done | bytes 4128 | tf_op jit(solution)/shard_map/ppermute | solution.py:189
  30.1 0.1 reshape.24.place_ref
  30.2 5.8 %shard_map.92 = (bf16[32,128,128]{2,1,0:T(8,128)(2,1)S(1)}, f32[16,128,128]{2,1,0:T(8,128)S(1)}, f32[16,128,128]{2,1,0:T(8,128)S(1)}, bf16[32,8,128,128]{3,2,1,0:T(8,128)(2,1)S(1)}) custom-call(s32[1]{0:T(128)} %constant.89.clone.1.starts_ref, s32[256]{0:T(256)S(1)} %reshape.24.place_ref, bf16[32,128,128]{2,1,0:T(8,128)(2,1)S(1)} %shard_map.91.refs_0_, ...), custom_call_target="tpu_custom_call" | custom-call | flops 1073741824 | bytes 8388608 | tf_op jit(solution)/shard_map/pallas_call | solution.py:128
  36.1 4.8 %shard_map.94 = (bf16[32,128,128]{2,1,0:T(8,128)(2,1)S(1)}, f32[16,128,128]{2,1,0:T(8,128)S(1)}, f32[16,128,128]{2,1,0:T(8,128)S(1)}) custom-call(s32[1]{0:T(128)} %constant.89.clone.1.starts_ref, s32[256]{0:T(256)S(1)} %reshape.24.place_ref, bf16[32,128,128]{2,1,0:T(8,128)(2,1)S(1)} %collective-permute-done.2.refs_0_, ...), custom_call_target="tpu_custom_call" | custom-call | flops 1073741824 | bytes 8388608 | tf_op jit(solution)/shard_map/pallas_call | solution.py:128
  40.9 0.6 collective-permute-start.3
  41.5 0.1 add_convert_fusion.4
  41.7 1.8 %collective-permute-start.7 = (bf16[16,128,128]{2,1,0:T(8,128)(2,1)S(1)}, bf16[16,128,128]{2,1,0:T(8,128)(2,1)S(1)}, u32[]{:S(2)}, u32[]{:S(2)}) collective-permute-start(bf16[16,128,128]{2,1,0:T(8,128)(2,1)S(1)} %add_convert_fusion.4), channel_id=1, source_target_pairs={{0,1},{1,0},{2,3},{3,2},{4,5},{5,4},{6,7},{7,6},{8,9},{9,8},{10,11... | collective-permute-start | bytes 1572872 | tf_op jit(solution)/shard_map/ppermute | solution.py:223
  43.4 12.2 %collective-permute-done.7 = bf16[16,128,128]{2,1,0:T(8,128)(2,1)S(1)} collective-permute-done((bf16[16,128,128]{2,1,0:T(8,128)(2,1)S(1)}, bf16[16,128,128]{2,1,0:T(8,128)(2,1)S(1)}, u32[]{:S(2)}, u32[]{:S(2)}) %collective-permute-start.7) | collective-permute-done | bytes 524320 | tf_op jit(solution)/shard_map/ppermute | solution.py:223
  55.6 0.2 fusion.1
  55.8 1.8 %collective-permute-start.8 = (bf16[16,128,128]{2,1,0:T(8,128)(2,1)S(1)}, bf16[16,128,128]{2,1,0:T(8,128)(2,1)S(1)}, u32[]{:S(2)}, u32[]{:S(2)}) collective-permute-start(bf16[16,128,128]{2,1,0:T(8,128)(2,1)S(1)} %fusion.1), channel_id=1, source_target_pairs={{0,16},{8,24},{16,0},{24,8},{1,17},{9,25},{17,1},{25,9},{2,18},{10... | collective-permute-start | bytes 1572872 | tf_op jit(solution)/shard_map/ppermute | solution.py:230
  57.6 11.3 %collective-permute-done.8 = bf16[16,128,128]{2,1,0:T(8,128)(2,1)S(1)} collective-permute-done((bf16[16,128,128]{2,1,0:T(8,128)(2,1)S(1)}, bf16[16,128,128]{2,1,0:T(8,128)(2,1)S(1)}, u32[]{:S(2)}, u32[]{:S(2)}) %collective-permute-start.8) | collective-permute-done | bytes 524320 | tf_op jit(solution)/shard_map/ppermute | solution.py:230
  68.9 0.6 multiply_convert_fusion
  69.5 1.8 %collective-permute-start.4 = (bf16[16,128,128]{2,1,0:T(8,128)(2,1)S(1)}, bf16[16,128,128]{2,1,0:T(8,128)(2,1)S(1)}, u32[]{:S(2)}, u32[]{:S(2)}) collective-permute-start(bf16[16,128,128]{2,1,0:T(8,128)(2,1)S(1)} %get-tuple-element.43), channel_id=1, source_target_pairs={{0,1},{1,0},{2,3},{3,2},{4,5},{5,4},{6,7},{7,6},{8,9},{9,8},{10,11... | collective-permute-start | bytes 1572872 | tf_op jit(solution)/shard_map/ppermute | solution.py:226
  71.2 10.4 %collective-permute-done.4 = bf16[16,128,128]{2,1,0:T(8,128)(2,1)S(1)} collective-permute-done((bf16[16,128,128]{2,1,0:T(8,128)(2,1)S(1)}, bf16[16,128,128]{2,1,0:T(8,128)(2,1)S(1)}, u32[]{:S(2)}, u32[]{:S(2)}) %collective-permute-start.4) | collective-permute-done | bytes 524320 | tf_op jit(solution)/shard_map/ppermute | solution.py:226
  81.7 0.2 fusion
  81.9 1.8 %collective-permute-start.5 = (bf16[16,128,128]{2,1,0:T(8,128)(2,1)S(1)}, bf16[16,128,128]{2,1,0:T(8,128)(2,1)}, u32[]{:S(2)}, u32[]{:S(2)}) collective-permute-start(bf16[16,128,128]{2,1,0:T(8,128)(2,1)S(1)} %fusion), channel_id=1, source_target_pairs={{0,16},{8,24},{16,0},{24,8},{1,17},{9,25},{17,1},{25,9},{2,18},{10... | collective-permute-start | bytes 1572872 | tf_op jit(solution)/shard_map/ppermute | solution.py:230
  83.9 9.4 %collective-permute-done.5 = bf16[16,128,128]{2,1,0:T(8,128)(2,1)} collective-permute-done((bf16[16,128,128]{2,1,0:T(8,128)(2,1)S(1)}, bf16[16,128,128]{2,1,0:T(8,128)(2,1)}, u32[]{:S(2)}, u32[]{:S(2)}) %collective-permute-start.5) | collective-permute-done | bytes 524320 | tf_op jit(solution)/shard_map/ppermute | solution.py:230
  93.4 1.7 multiply_convert_fusion.1.refs_0_
  95.1 5.7 %shard_map.95 = (bf16[16,128,128]{2,1,0:T(8,128)(2,1)S(1)}, bf16[16,128,128]{2,1,0:T(8,128)(2,1)S(1)}, bf16[16,128,128]{2,1,0:T(8,128)(2,1)S(1)}, bf16[16,128,12...) custom-call(s32[2]{0:T(128)S(1)} %pad_add_fusion.starts_ref, s32[256]{0:T(256)S(1)} %reshape.23.place_ref, ...), custom_call_target="tpu_custom_call" | custom-call | flops 1073741824 | bytes 8388608 | tf_op jit(solution)/shard_map/pallas_call | solution.py:128
  100.9 1.8 %collective-permute-start.13 = (bf16[16,128,128]{2,1,0:T(8,128)(2,1)S(1)}, bf16[16,128,128]{2,1,0:T(8,128)(2,1)S(1)}, u32[]{:S(2)}, u32[]{:S(2)}) collective-permute-start(bf16[16,128,128]{2,1,0:T(8,128)(2,1)S(1)} %get-tuple-element.36), channel_id=1, source_target_pairs={{0,1},{1,0},{2,3},{3,2},{4,5},{5,4},{6,7},{7,6},{8,9},{9,8},{10,11... | collective-permute-start | bytes 1572872 | tf_op jit(solution)/shard_map/ppermute | solution.py:238
  102.6 0.3 collective-permute-start.12
  102.9 4.5 %shard_map.96 = f32[64,128,128]{2,1,0:T(8,128)S(1)} custom-call(s32[2]{0:T(128)S(1)} %pad_add_fusion.starts_ref, s32[256]{0:T(256)S(1)} %reshape.23.place_ref, bf16[16,128,128]{2,1,0:T(8,128)(2,1)S(1)} %multiply_convert_fusion.1.refs_0_, bf16[16,128,128]{2,1,0:T(8,128)(2,1)S(1)} %collective-permute-done.6.refs_1_, ...), custom_call_target="tpu_custom_call" | custom-call | flops 1073741824 | bytes 8388608 | tf_op jit(solution)/shard_map/pallas_call | solution.py:128
  107.5 8.2 %collective-permute-done.13 = bf16[16,128,128]{2,1,0:T(8,128)(2,1)S(1)} collective-permute-done((bf16[16,128,128]{2,1,0:T(8,128)(2,1)S(1)}, bf16[16,128,128]{2,1,0:T(8,128)(2,1)S(1)}, u32[]{:S(2)}, u32[]{:S(2)}) %collective-permute-start.13) | collective-permute-done | bytes 524320 | tf_op jit(solution)/shard_map/ppermute | solution.py:238
  115.7 1.0 fusion.18
  116.7 1.5 collective-permute-start.17
  118.2 4.4 %collective-permute-start.14 = (bf16[16,128,128]{2,1,0:T(8,128)(2,1)}, bf16[16,128,128]{2,1,0:T(8,128)(2,1)}, u32[]{:S(2)}, u32[]{:S(2)}) collective-permute-start(bf16[16,128,128]{2,1,0:T(8,128)(2,1)} %fusion.18), channel_id=1, source_target_pairs={{0,2},{1,3},{8,10},{9,11},{16,18},{17,19},{24,26},{25,27}} | collective-permute-start | bytes 1572872 | tf_op jit(solution)/shard_map/ppermute | solution.py:253
  122.6 1.5 collective-permute-start.10
  124.1 0.5 collective-permute-start.11
  124.6 2.3 %collective-permute-done.12 = bf16[16,128,128]{2,1,0:T(8,128)(2,1)S(1)} collective-permute-done((bf16[16,128,128]{2,1,0:T(8,128)(2,1)S(1)}, bf16[16,128,128]{2,1,0:T(8,128)(2,1)S(1)}, u32[]{:S(2)}, u32[]{:S(2)}) %collective-permute-start.12) | collective-permute-done | bytes 524320 | tf_op jit(solution)/shard_map/ppermute | solution.py:238
  127.0 5.6 %collective-permute-done.14 = bf16[16,128,128]{2,1,0:T(8,128)(2,1)} collective-permute-done((bf16[16,128,128]{2,1,0:T(8,128)(2,1)}, bf16[16,128,128]{2,1,0:T(8,128)(2,1)}, u32[]{:S(2)}, u32[]{:S(2)}) %collective-permute-start.14) | collective-permute-done | bytes 524320 | tf_op jit(solution)/shard_map/ppermute | solution.py:253
  132.6 3.3 %add_convert_fusion.1 = (bf16[16,128,128]{2,1,0:T(8,128)(2,1)}, bf16[16,128,128]{2,1,0:T(8,128)(2,1)}) fusion(bf16[16,128,128]{2,1,0:T(8,128)(2,1)} %collective-permute-done.17, pred[]{:T(512)S(6)} %eq.93, bf16[16,128,128]{2,1,0:T(8,128)(2,1)S(1)} %collective-permute-done.12, f32[64,128,128]{2,1,0:T(8,128)} %copy-done.2, ...), kind=kLoop, calls=%fused_computation.5 | loop fusion | flops 3145728 | bytes 5242882 | tf_op jit(solution)/shard_map/convert_element_type | solution.py:250
  135.9 0.7 collective-permute-start.18
  136.6 5.8 %collective-permute-start.15 = (bf16[16,128,128]{2,1,0:T(8,128)(2,1)}, bf16[16,128,128]{2,1,0:T(8,128)(2,1)}, u32[]{:S(2)}, u32[]{:S(2)}) collective-permute-start(bf16[16,128,128]{2,1,0:T(8,128)(2,1)} %get-tuple-element.40), channel_id=1, source_target_pairs={{0,2},{2,4},{1,3},{3,5},{8,10},{10,12},{9,11},{11,13},{16,18},{18,... | collective-permute-start | bytes 1572872 | tf_op jit(solution)/shard_map/ppermute | solution.py:253
  142.4 6.7 %collective-permute-done.11 = bf16[16,128,128]{2,1,0:T(8,128)(2,1)} collective-permute-done((bf16[16,128,128]{2,1,0:T(8,128)(2,1)S(1)}, bf16[16,128,128]{2,1,0:T(8,128)(2,1)}, u32[]{:S(2)}, u32[]{:S(2)}) %collective-permute-start.11) | collective-permute-done | bytes 524320 | tf_op jit(solution)/shard_map/ppermute | solution.py:238
  149.0 2.4 %collective-permute-done.15 = bf16[16,128,128]{2,1,0:T(8,128)(2,1)} collective-permute-done((bf16[16,128,128]{2,1,0:T(8,128)(2,1)}, bf16[16,128,128]{2,1,0:T(8,128)(2,1)}, u32[]{:S(2)}, u32[]{:S(2)}) %collective-permute-start.15) | collective-permute-done | bytes 524320 | tf_op jit(solution)/shard_map/ppermute | solution.py:253
  151.5 3.2 %add_convert_fusion = (bf16[16,128,128]{2,1,0:T(8,128)(2,1)S(1)}, bf16[16,128,128]{2,1,0:T(8,128)(2,1)S(1)}, f32[16,128,128]{2,1,0:T(8,128)S(1)}) fusion(bf16[16,128,128]{2,1,0:T(8,128)(2,1)S(1)} %collective-permute-done.18, bf16[16,128,128]{2,1,0:T(8,128)(2,1)} %collective-permute-done.11, f32[64,128,128]{2,1,0:T(8,128)} %copy-done.2, pred[]{:T(512)S(6)} %eq.92, ...), kind=kLoop, calls=%fused_computation.4 | loop fusion | flops 4718592 | bytes 9437188 | tf_op jit(solution)/shard_map/convert_element_type | solution.py:250
  154.7 1.3 collective-permute-start.19
  156.0 5.0 %collective-permute-start.16 = (bf16[16,128,128]{2,1,0:T(8,128)(2,1)S(1)}, bf16[16,128,128]{2,1,0:T(8,128)(2,1)S(1)}, u32[]{:S(2)}, u32[]{:S(2)}) collective-permute-start(bf16[16,128,128]{2,1,0:T(8,128)(2,1)S(1)} %get-tuple-element.38), channel_id=1, source_target_pairs={{0,2},{2,4},{4,6},{1,3},{3,5},{5,7},{8,10},{10,12},{12,14},{9,11},... | collective-permute-start | bytes 1572872 | tf_op jit(solution)/shard_map/ppermute | solution.py:253
  161.1 7.6 %collective-permute-done.19.down_ref = bf16[16,128,128]{2,1,0:T(8,128)(2,1)S(1)} collective-permute-done((bf16[16,128,128]{2,1,0:T(8,128)(2,1)S(1)}, bf16[16,128,128]{2,1,0:T(8,128)(2,1)S(1)}, u32[]{:S(2)}, u32[]{:S(2)}) %collective-permute-start.19) | collective-permute-done | bytes 524320 | tf_op jit(solution)/shard_map/ppermute | solution.py:254
  168.7 1.2 collective-permute-done.16.up_ref
  169.8 1.0 shard_map.97
  (30 shorter events, 0.5 us)
Async XLA Ops:
  0.0 57.6 %copy-start = (f32[8192]{0:T(1024)S(1)}, f32[8192]{0:T(1024)}, u32[]{:S(2)}) copy-start(f32[8192]{0:T(1024)} %param.13) | copy-start | bytes 98308
  0.0 0.8 copy-start.3
  3.6 32.5 %collective-permute-start.2 = (bf16[32,128,128]{2,1,0:T(8,128)(2,1)}, bf16[32,128,128]{2,1,0:T(8,128)(2,1)S(1)}, u32[]{:S(2)}, u32[]{:S(2)}) collective-permute-start(bf16[32,128,128]{2,1,0:T(8,128)(2,1)} %shard_map.93), channel_id=1, source_target_pairs={{0,1},{1,0},{2,3},{3,2},{4,5},{5,4},{6,7},{7,6},{8,9},{9,8},{10,11... | collective-permute-start | bytes 3145736 | tf_op jit(solution)/shard_map/ppermute | solution.py:186
  7.3 22.7 %collective-permute-start = (bf16[128,16]{0,1:T(8,128)(2,1)S(1)}, bf16[128,16]{0,1:T(8,128)(2,1)S(1)}, u32[]{:S(2)}, u32[]{:S(2)}) collective-permute-start(bf16[128,16]{0,1:T(8,128)(2,1)S(1)} %get-tuple-element.45), channel_id=1, source_target_pairs={{0,1},{1,0},{2,3},{3,2},{4,5},{5,4},{6,7},{7,6},{8,9},{9,8},{10,11... | collective-permute-start | bytes 12296 | tf_op jit(solution)/shard_map/ppermute | solution.py:189
  8.1 0.8 copy-start.4
  36.0 5.5 %collective-permute-start.1 = (bf16[32,128,128]{2,1,0:T(8,128)(2,1)S(1)}, bf16[32,128,128]{2,1,0:T(8,128)(2,1)S(1)}, u32[]{:S(2)}, u32[]{:S(2)}) collective-permute-start(bf16[32,128,128]{2,1,0:T(8,128)(2,1)S(1)} %get-tuple-element.25), channel_id=1, source_target_pairs={{0,8},{8,0},{16,24},{24,16},{1,9},{9,1},{17,25},{25,17},{2,10},{10... | collective-permute-start | bytes 3145736 | tf_op jit(solution)/shard_map/ppermute | solution.py:218
  40.9 14.7 %collective-permute-start.3 = (bf16[32,128,128]{2,1,0:T(8,128)(2,1)S(1)}, bf16[32,128,128]{2,1,0:T(8,128)(2,1)S(1)}, u32[]{:S(2)}, u32[]{:S(2)}) collective-permute-start(bf16[32,128,128]{2,1,0:T(8,128)(2,1)S(1)} %get-tuple-element.28), channel_id=1, source_target_pairs={{0,8},{8,0},{16,24},{24,16},{1,9},{9,1},{17,25},{25,17},{2,10},{10... | collective-permute-start | bytes 3145736 | tf_op jit(solution)/shard_map/ppermute | solution.py:218
  41.5 40.2 %copy-start.6 = (bf16[32,128,128]{2,1,0:T(8,128)(2,1)}, bf16[32,128,128]{2,1,0:T(8,128)(2,1)S(1)}, u32[]{:S(2)}) copy-start(bf16[32,128,128]{2,1,0:T(8,128)(2,1)S(1)} %collective-permute-done.1) | copy-start | bytes 3145732
  41.7 13.9 %collective-permute-start.7 = (bf16[16,128,128]{2,1,0:T(8,128)(2,1)S(1)}, bf16[16,128,128]{2,1,0:T(8,128)(2,1)S(1)}, u32[]{:S(2)}, u32[]{:S(2)}) collective-permute-start(bf16[16,128,128]{2,1,0:T(8,128)(2,1)S(1)} %add_convert_fusion.4), channel_id=1, source_target_pairs={{0,1},{1,0},{2,3},{3,2},{4,5},{5,4},{6,7},{7,6},{8,9},{9,8},{10,11... | collective-permute-start | bytes 1572872 | tf_op jit(solution)/shard_map/ppermute | solution.py:223
  55.8 13.1 %collective-permute-start.8 = (bf16[16,128,128]{2,1,0:T(8,128)(2,1)S(1)}, bf16[16,128,128]{2,1,0:T(8,128)(2,1)S(1)}, u32[]{:S(2)}, u32[]{:S(2)}) collective-permute-start(bf16[16,128,128]{2,1,0:T(8,128)(2,1)S(1)} %fusion.1), channel_id=1, source_target_pairs={{0,16},{8,24},{16,0},{24,8},{1,17},{9,25},{17,1},{25,9},{2,18},{10... | collective-permute-start | bytes 1572872 | tf_op jit(solution)/shard_map/ppermute | solution.py:230
  69.5 12.2 %collective-permute-start.4 = (bf16[16,128,128]{2,1,0:T(8,128)(2,1)S(1)}, bf16[16,128,128]{2,1,0:T(8,128)(2,1)S(1)}, u32[]{:S(2)}, u32[]{:S(2)}) collective-permute-start(bf16[16,128,128]{2,1,0:T(8,128)(2,1)S(1)} %get-tuple-element.43), channel_id=1, source_target_pairs={{0,1},{1,0},{2,3},{3,2},{4,5},{5,4},{6,7},{7,6},{8,9},{9,8},{10,11... | collective-permute-start | bytes 1572872 | tf_op jit(solution)/shard_map/ppermute | solution.py:226
  81.9 11.5 %collective-permute-start.5 = (bf16[16,128,128]{2,1,0:T(8,128)(2,1)S(1)}, bf16[16,128,128]{2,1,0:T(8,128)(2,1)}, u32[]{:S(2)}, u32[]{:S(2)}) collective-permute-start(bf16[16,128,128]{2,1,0:T(8,128)(2,1)S(1)} %fusion), channel_id=1, source_target_pairs={{0,16},{8,24},{16,0},{24,8},{1,17},{9,25},{17,1},{25,9},{2,18},{10... | collective-permute-start | bytes 1572872 | tf_op jit(solution)/shard_map/ppermute | solution.py:230
  83.7 11.4 %collective-permute-start.9 = (bf16[16,128,128]{2,1,0:T(8,128)(2,1)S(1)}, bf16[16,128,128]{2,1,0:T(8,128)(2,1)S(1)}, u32[]{:S(2)}, u32[]{:S(2)}) collective-permute-start(bf16[16,128,128]{2,1,0:T(8,128)(2,1)S(1)} %get-tuple-element.42.refs_0_), channel_id=1, source_target_pairs={{0,8},{8,0},{16,24},{24,16},{1,9},{9,1},{17,25},{25,17},{2,10},{10... | collective-permute-start | bytes 1572872 | tf_op jit(solution)/shard_map/ppermute | solution.py:232
  95.0 7.9 %collective-permute-start.6 = (bf16[16,128,128]{2,1,0:T(8,128)(2,1)S(1)}, bf16[16,128,128]{2,1,0:T(8,128)(2,1)S(1)}, u32[]{:S(2)}, u32[]{:S(2)}) collective-permute-start(bf16[16,128,128]{2,1,0:T(8,128)(2,1)S(1)} %multiply_convert_fusion.1.refs_0_), channel_id=1, source_target_pairs={{0,8},{8,0},{16,24},{24,16},{1,9},{9,1},{17,25},{25,17},{2,10},{10... | collective-permute-start | bytes 1572872 | tf_op jit(solution)/shard_map/ppermute | solution.py:232
  100.9 14.9 %collective-permute-start.13 = (bf16[16,128,128]{2,1,0:T(8,128)(2,1)S(1)}, bf16[16,128,128]{2,1,0:T(8,128)(2,1)S(1)}, u32[]{:S(2)}, u32[]{:S(2)}) collective-permute-start(bf16[16,128,128]{2,1,0:T(8,128)(2,1)S(1)} %get-tuple-element.36), channel_id=1, source_target_pairs={{0,1},{1,0},{2,3},{3,2},{4,5},{5,4},{6,7},{7,6},{8,9},{9,8},{10,11... | collective-permute-start | bytes 1572872 | tf_op jit(solution)/shard_map/ppermute | solution.py:238
  102.6 24.3 %collective-permute-start.12 = (bf16[16,128,128]{2,1,0:T(8,128)(2,1)S(1)}, bf16[16,128,128]{2,1,0:T(8,128)(2,1)S(1)}, u32[]{:S(2)}, u32[]{:S(2)}) collective-permute-start(bf16[16,128,128]{2,1,0:T(8,128)(2,1)S(1)} %get-tuple-element.35), channel_id=1, source_target_pairs={{0,1},{1,0},{2,3},{3,2},{4,5},{5,4},{6,7},{7,6},{8,9},{9,8},{10,11... | collective-permute-start | bytes 1572872 | tf_op jit(solution)/shard_map/ppermute | solution.py:238
  107.5 8.3 %copy-start.2 = (f32[64,128,128]{2,1,0:T(8,128)}, f32[64,128,128]{2,1,0:T(8,128)S(1)}, u32[]{:S(2)}) copy-start(f32[64,128,128]{2,1,0:T(8,128)S(1)} %shard_map.96) | copy-start | bytes 12582916
  116.7 10.3 %collective-permute-start.17 = (bf16[16,128,128]{2,1,0:T(8,128)(2,1)}, bf16[16,128,128]{2,1,0:T(8,128)(2,1)}, u32[]{:S(2)}, u32[]{:S(2)}) collective-permute-start(bf16[16,128,128]{2,1,0:T(8,128)(2,1)} %fusion.18), channel_id=1, source_target_pairs={{6,4},{7,5},{14,12},{15,13},{22,20},{23,21},{30,28},{31,29}} | collective-permute-start | bytes 1572872 | tf_op jit(solution)/shard_map/ppermute | solution.py:254
  118.2 14.4 %collective-permute-start.14 = (bf16[16,128,128]{2,1,0:T(8,128)(2,1)}, bf16[16,128,128]{2,1,0:T(8,128)(2,1)}, u32[]{:S(2)}, u32[]{:S(2)}) collective-permute-start(bf16[16,128,128]{2,1,0:T(8,128)(2,1)} %fusion.18), channel_id=1, source_target_pairs={{0,2},{1,3},{8,10},{9,11},{16,18},{17,19},{24,26},{25,27}} | collective-permute-start | bytes 1572872 | tf_op jit(solution)/shard_map/ppermute | solution.py:253
  122.6 19.8 %collective-permute-start.10 = (bf16[16,128,128]{2,1,0:T(8,128)(2,1)S(1)}, bf16[16,128,128]{2,1,0:T(8,128)(2,1)S(1)}, u32[]{:S(2)}, u32[]{:S(2)}) collective-permute-start(bf16[16,128,128]{2,1,0:T(8,128)(2,1)S(1)} %get-tuple-element.33), channel_id=1, source_target_pairs={{0,1},{1,0},{2,3},{3,2},{4,5},{5,4},{6,7},{7,6},{8,9},{9,8},{10,11... | collective-permute-start | bytes 1572872 | tf_op jit(solution)/shard_map/ppermute | solution.py:238
  124.1 24.9 %collective-permute-start.11 = (bf16[16,128,128]{2,1,0:T(8,128)(2,1)S(1)}, bf16[16,128,128]{2,1,0:T(8,128)(2,1)}, u32[]{:S(2)}, u32[]{:S(2)}) collective-permute-start(bf16[16,128,128]{2,1,0:T(8,128)(2,1)S(1)} %get-tuple-element.34), channel_id=1, source_target_pairs={{0,1},{1,0},{2,3},{3,2},{4,5},{5,4},{6,7},{7,6},{8,9},{9,8},{10,11... | collective-permute-start | bytes 1572872 | tf_op jit(solution)/shard_map/ppermute | solution.py:238
  135.9 13.2 %collective-permute-start.18 = (bf16[16,128,128]{2,1,0:T(8,128)(2,1)}, bf16[16,128,128]{2,1,0:T(8,128)(2,1)S(1)}, u32[]{:S(2)}, u32[]{:S(2)}) collective-permute-start(bf16[16,128,128]{2,1,0:T(8,128)(2,1)} %get-tuple-element.39), channel_id=1, source_target_pairs={{6,4},{4,2},{7,5},{5,3},{14,12},{12,10},{15,13},{13,11},{22,20},{2... | collective-permute-start | bytes 1572872 | tf_op jit(solution)/shard_map/ppermute | solution.py:254
  136.6 14.9 %collective-permute-start.15 = (bf16[16,128,128]{2,1,0:T(8,128)(2,1)}, bf16[16,128,128]{2,1,0:T(8,128)(2,1)}, u32[]{:S(2)}, u32[]{:S(2)}) collective-permute-start(bf16[16,128,128]{2,1,0:T(8,128)(2,1)} %get-tuple-element.40), channel_id=1, source_target_pairs={{0,2},{2,4},{1,3},{3,5},{8,10},{10,12},{9,11},{11,13},{16,18},{18,... | collective-permute-start | bytes 1572872 | tf_op jit(solution)/shard_map/ppermute | solution.py:253
  142.4 28.5 %copy-start.1 = (f32[8192]{0:T(1024)S(1)}, f32[8192]{0:T(1024)}, u32[]{:S(2)}) copy-start(f32[8192]{0:T(1024)} %param.13) | copy-start | bytes 98308
  142.4 27.5 %copy-start.5 = (f32[2048]{0:T(1024)S(1)}, f32[2048]{0:T(1024)}, u32[]{:S(2)}) copy-start(f32[2048]{0:T(1024)} %param.17) | copy-start | bytes 24580
  154.7 13.9 %collective-permute-start.19 = (bf16[16,128,128]{2,1,0:T(8,128)(2,1)S(1)}, bf16[16,128,128]{2,1,0:T(8,128)(2,1)S(1)}, u32[]{:S(2)}, u32[]{:S(2)}) collective-permute-start(bf16[16,128,128]{2,1,0:T(8,128)(2,1)S(1)} %get-tuple-element.37), channel_id=1, source_target_pairs={{6,4},{4,2},{2,0},{7,5},{5,3},{3,1},{14,12},{12,10},{10,8},{15,13}... | collective-permute-start | bytes 1572872 | tf_op jit(solution)/shard_map/ppermute | solution.py:254
  156.0 13.8 %collective-permute-start.16 = (bf16[16,128,128]{2,1,0:T(8,128)(2,1)S(1)}, bf16[16,128,128]{2,1,0:T(8,128)(2,1)S(1)}, u32[]{:S(2)}, u32[]{:S(2)}) collective-permute-start(bf16[16,128,128]{2,1,0:T(8,128)(2,1)S(1)} %get-tuple-element.38), channel_id=1, source_target_pairs={{0,2},{2,4},{4,6},{1,3},{3,5},{5,7},{8,10},{10,12},{12,14},{9,11},... | collective-permute-start | bytes 1572872 | tf_op jit(solution)/shard_map/ppermute | solution.py:253

commit v2 on v1

--- a/solution.py
+++ b/solution.py
@@ -2,7 +2,6 @@
 
 import jax
 import jax.numpy as jnp
-import numpy as np
 from jax import lax
 from jax.experimental import pallas as pl
 from jax.experimental.pallas import tpu as pltpu
@@ -11,6 +10,9 @@
 
 UNROLL = 4
 VMEM_LIMIT = 8 * 1024 * 1024
+
+in_vmem = functools.partial(pltpu.with_memory_space_constraint, memory_space=pltpu.VMEM)
+in_hbm = functools.partial(pltpu.with_memory_space_constraint, memory_space=pltpu.HBM)
 
 
 def mask_kernel(half_ref, acts_ref, live_ref, out_ref):
@@ -40,7 +42,7 @@
         ),
         compiler_params=pltpu.CompilerParams(vmem_limit_bytes=VMEM_LIMIT),
         cost_estimate=pl.CostEstimate(flops=rows * width, bytes_accessed=2 * rows * width, transcendentals=0),
-    )(half.reshape(1), pltpu.with_memory_space_constraint(acts, pltpu.HBM), act_mask.T)
+    )(half.reshape(1), in_hbm(acts), in_hbm(act_mask.T))
 
 
 def clear(acc):
@@ -116,8 +118,6 @@
     smem = pl.BlockSpec(memory_space=pltpu.SMEM)
     vmem = pl.BlockSpec(memory_space=pltpu.VMEM)
     hbm = pl.BlockSpec(memory_space=pltpu.HBM)
-    in_vmem = functools.partial(pltpu.with_memory_space_constraint, memory_space=pltpu.VMEM)
-    in_hbm = functools.partial(pltpu.with_memory_space_constraint, memory_space=pltpu.HBM)
     out_shape = [pltpu.VMEM((count, rows, block), kind) for count, kind in segments]
     scratch = [pltpu.VMEM((total, rows, block), jnp.float32)]
     if load:
@@ -140,30 +140,39 @@
     )(jnp.stack(starts), places.reshape(-1), *map(in_vmem, xs), (in_hbm if load else in_vmem)(weights))
 
 
-def finish_kernel(own_ref, up_ref, down_ref, bias_ref, out_ref):
-    share, _, block = own_ref.shape
+def add_kernel(*refs):
+    *parts, out_ref = refs
+
+    def body(i, carry):
+        total = parts[0][i]
+        for part in parts[1:]:
+            total = total + part[i].astype(jnp.float32)
+        out_ref[i] = total.astype(jnp.bfloat16)
+        return carry
+
+    lax.fori_loop(0, out_ref.shape[0], body, 0, unroll=2)
+
+
+def add(parts):
+    vmem = pl.BlockSpec(memory_space=pltpu.VMEM)
+    return pl.pallas_call(
+        add_kernel,
+        out_shape=pltpu.VMEM(parts[0].shape, jnp.bfloat16),
+        in_specs=[vmem] * len(parts),
+        out_specs=vmem,
+        compiler_params=pltpu.CompilerParams(vmem_limit_bytes=VMEM_LIMIT),
+    )(*map(in_vmem, parts))
+
+
+def finish_kernel(*refs):
+    *parts, bias_ref, out_ref = refs
+    share, _, block = parts[0].shape
     for i in range(share):
-        total = own_ref[i] + up_ref[i].astype(jnp.float32) + down_ref[i].astype(jnp.float32)
-        out_ref[:, i * block:(i + 1) * block] = jnp.maximum(total + bias_ref[i:i + 1, :], 0.0).astype(jnp.bfloat16)
-
-
-def line_orders(size):
-    order, right, left = [], [], []
-    for place in range(size):
-        sends = []
-        for step in range(size - 1):
-            up = place + size - 1 - step
-            if place < up < size:
-                sends.append((step, 0, up))
-            down = place - size + 1 + step
-            if 0 <= down < place:
-                sends.append((step, 1, down))
-        chunks = [s[2] for s in sends] + [place]
-        order.append(chunks)
-        right.append([next((i for i, s in enumerate(sends) if s[:2] == (step, 0)), 0) for step in range(size - 1)])
-        left.append([next((i for i, s in enumerate(sends) if s[:2] == (step, 1)), 0) for step in range(size - 1)])
-    slots = np.argsort(np.array(order), axis=1)
-    return slots.astype(np.int32), np.array(right, np.int32), np.array(left, np.int32)
+        total = parts[0][i]
+        for part in parts[1:]:
+            total = total + part[i].astype(jnp.float32)
+        total = jnp.maximum(total + bias_ref[i:i + 1, :], 0.0)
+        out_ref[:, i * block:(i + 1) * block] = total.astype(jnp.bfloat16)
 
 
 def exchange_plan(acts, act_mask, w1, cols1, bias1, mask2, w2, cols2, bias2):
@@ -200,23 +209,21 @@
     same_depth = 1 - (to_depth ^ d)
     place1 = same_core * half_mid + same_depth * quarter + to1 % quarter
 
-    slots, right, left = line_orders(size_col)
-
-    def mine_of(table):
-        return sum(jnp.where(c == i, int(v), 0) for i, v in enumerate(table))
-
     to2 = lax.dynamic_slice_in_dim(cols2, d * half_mid, half_mid, 0) - r * row_blocks
     share = row_blocks // size_col
     chunk = to2 // share
-    slot = sum(jnp.where(chunk == i, mine_of(slots[:, i]), 0) for i in range(size_col))
+    far = jnp.where(c < size_col // 2, size_col - 1, 0)
+    slot = jnp.where(chunk == far, 0, jnp.where(chunk == (far ^ 1), 1, jnp.where(chunk == (c ^ 1), 2, 3)))
     place2 = slot * share + to2 % share
-    own_x, mask_other, place1, place2 = lax.optimization_barrier((own_x, mask_other, place1, place2))
+    own_x, place1, place2 = lax.optimization_barrier((own_x, place1, place2))
 
     segments = [(half_mid, bf16), (quarter, f32), (quarter, f32)]
 
     def core_sums(low, send, keep):
         low = over_core(low)
-        return (send + low[:quarter].astype(f32)).astype(bf16), keep + low[quarter:].astype(f32)
+        return lax.optimization_barrier(
+            ((send + low[:quarter].astype(f32)).astype(bf16), keep + low[quarter:].astype(f32))
+        )
 
     *sums, w1 = fold([own_x], w1, place1, [zero], segments, load=True)
     send_own, keep_own = core_sums(*sums)
@@ -225,38 +232,42 @@
     send_other, keep_other = core_sums(*sums)
     got_own = over_depth(send_other)
 
-    def hidden(keep, got, mask):
+    def x_sums(keep, got):
         part = keep + got.astype(f32)
-        z1 = part + over_x(part.astype(bf16)).astype(f32)
+        part, low = lax.optimization_barrier((part, part.astype(bf16)))
+        return part, over_x(low)
+
+    def hidden(part, low, mask):
+        z1 = part + low.astype(f32)
         out = (jnp.maximum(z1 + bias_blocks, 0.0) * mask.astype(f32).T[:, :, None]).astype(bf16)
+        out = lax.optimization_barrier(out)
         return [out, over_core(out)]
 
-    hidden_other = hidden(keep_other, got_other, mask_other)
-    hidden_own = hidden(keep_own, got_own, mask_own)
+    sums_other = x_sums(keep_other, got_other)
+    sums_own = x_sums(keep_own, got_own)
+    hidden_other = hidden(*sums_other, mask_other)
     starts = [core * quarter, (1 - core) * quarter]
     *for_other, w2 = fold(hidden_other, w2, place2, starts, [(share, bf16)] * size_col, load=True)
-    from_other = [over_depth(part) for part in for_other]
-    (mine,) = fold(hidden_own, w2, place2, starts, [(row_blocks, f32)])
-    total = [mine[i * share:(i + 1) * share] + f.astype(f32) for i, f in enumerate(from_other)]
-
-    up = down = None
-    for step in range(size_col - 1):
-
-        def send(table, got):
-            pick = mine_of(table[:, step])
-            value = total[0]
-            for i in range(1, step + 1):
-                value = jnp.where(pick == i, total[i], value)
-            return (value if got is None else value + got.astype(f32)).astype(bf16)
-
-        go_up, go_down = send(right, up), send(left, down)
-        up = lax.ppermute(go_up, "col", [(i, i + 1) for i in range(step + 1)])
-        down = lax.ppermute(go_down, "col", [(size_col - 1 - i, size_col - 2 - i) for i in range(step + 1)])
+    got = []
+    for part in for_other:
+        got.append(over_depth(part))
+    part_own, low_own, w2 = lax.optimization_barrier((*sums_own, w2))
+    hidden_own = hidden(part_own, low_own, mask_own)
+    mine = fold(hidden_own, w2, place2, starts, [(share, f32)] * size_col)
+
+    over_col = functools.partial(lax.ppermute, axis_name="col")
+    ends = [(0, 1), (3, 2)]
+    ends0 = over_col(add([mine[0], got[0]]), perm=ends)
+    ends1 = over_col(add([mine[1], got[1]]), perm=ends)
+    cross0 = over_col(add([mine[0], got[0], ends0]), perm=[(1, 3), (2, 0)])
+    near = over_col(add([mine[2], got[2]]), perm=[(i, i ^ 1) for i in range(size_col)])
+    cross1 = over_col(add([mine[1], got[1], ends1]), perm=[(1, 2), (2, 1)])
+    parts = [mine[3], got[3], cross0, near, cross1]
     return pl.pallas_call(
         finish_kernel,
         out_shape=jax.ShapeDtypeStruct((rows, share * block), bf16),
         compiler_params=pltpu.CompilerParams(vmem_limit_bytes=VMEM_LIMIT),
-    )(total[-1], up, down, bias2.reshape(share, block))
+    )(*map(in_vmem, parts), bias2.reshape(share, block))
 
 
 def fold_function(inputs, targets, stride):
@@ -311,7 +322,7 @@
 
 def solution(mesh):
     sizes = dict(mesh.shape)
-    pairs = sizes["depth"] == 2 and sizes["row"] == 4
+    pairs = sizes["depth"] == 2 and sizes["row"] == 4 and sizes["col"] == 4
     return jax.shard_map(
         exchange_plan if pairs else gather_plan,
         mesh=mesh,

time: 172 us -> 145 us (0.84)
  waiting for transfers between devices: 96.5 us -> 83.3 us
  starting transfers between devices: 33.7 us -> 25.2 us
  other arithmetic: 11.9 us -> 6.92 us
    ppermute x1, waiting for transfers between devices: 19.1 us -> 1.62 us  [exchange_plan(): over_depth(lax.dynamic_slice_in_dim(mask2, (1 - d) * half_mid + core * qu...]
    ppermute x1, waiting for transfers between devices: 0.01 us -> 13.5 us  [exchange_plan(): other_x = over_depth(masked_half(acts, act_mask, 1 - d))]
    ppermute x12 -> x11, starting transfers between devices: 26.4 us -> 18.1 us  [the longest x4 5.14 us: exchange_plan(): got.append(over_depth(part))]
    ppermute x1, waiting for transfers between devices: 10.4 us -> 2.49 us  [exchange_plan(): got_own = over_depth(send_other)]
    convert_element_type x6 -> x2, other arithmetic: 8.01 us -> 1.21 us  [x_sums(): part, low = lax.optimization_barrier((part, part.astype(bf16)))]
    add x0 -> x3, other arithmetic: none -> 3.11 us  [the longest x2 2.33 us: core_sums(): keep + low[quarter:].astype(f32)]
    ppermute x12 -> x11, waiting for transfers between devices: 54.8 us -> 54.2 us  [the longest x4 25.3 us: exchange_plan(): got.append(over_depth(part))]
  transfers between devices with their start and end apart: 20 -> 19, of which waited for: 12 -> 12; matrix products, arithmetic and copies ran while one was open for 5% -> 4% of each run, Pallas kernels for 13% -> 17%
where the time goes in v2:
time: 145 us; the launch traced here: 143 us
  waiting for transfers between devices  83.3 us (57%)
  Pallas kernels  27.1 us (19%)
  starting transfers between devices  25.2 us (17%)
  other arithmetic  6.92 us (5%)
    ppermute x4, waiting for transfers between devices, exchange_plan(): got.append(over_depth(part))  25.3 us
    pallas_call x4, Pallas kernels, fold(): pl.pallas_call(functools.partial(fold_kernel, len(xs), load), out_shape=o...  21.1 us
    ppermute x2, waiting for transfers between devices, x_sums(): return (part, over_x(low))  13.9 us
    ppermute x1, waiting for transfers between devices, exchange_plan(): over_col(add([mine[2], got[2]]), perm=[(i, i ^ 1) for i in range(size_col)])  13.6 us
    ppermute x1, waiting for transfers between devices, exchange_plan(): other_x = over_depth(masked_half(acts, act_mask, 1 - d))  13.5 us
    ppermute x1, waiting for transfers between devices, exchange_plan(): got_other = over_depth(send_own)  11.5 us
    ppermute x4, starting transfers between devices, exchange_plan(): got.append(over_depth(part))  5.14 us
    pallas_call x2, Pallas kernels, masked_half(): pl.pallas_call(mask_kernel, out_shape=pltpu.VMEM((blocks, rows, block), j...  4.06 us
  transfers between devices with their start and end apart: 19, of which 12 were waited for; matrix products, arithmetic and copies ran while one was open for 4% of the time, Pallas kernels for 17%

profile of v2, /device:TPU:0, one launch (start us, length us, event | category | flops | bytes accessed | tf_op | source)
XLA Modules:
  0.0 143.0 jit_solution(9636851508026175175)
XLA Ops:
  0.0 2.0 %shard_map.93 = bf16[32,128,128]{2,1,0:T(8,128)(2,1)S(1)} custom-call(s32[1]{0:T(128)} %bitcast.4.half_ref, bf16[128,8192]{1,0:T(8,128)(2,1)} %acts_ref.3, s32[64,128]{1,0:T(8,128)} %bitcast.15), custom_call_target="tpu_custom_call" | custom-call | flops 1048576 | bytes 2097152 | tf_op jit(solution)/shard_map/pallas_call | solution.py:31
  2.0 3.1 %collective-permute-start.1 = (bf16[32,128,128]{2,1,0:T(8,128)(2,1)S(1)}, bf16[32,128,128]{2,1,0:T(8,128)(2,1)S(1)}, u32[]{:S(2)}, u32[]{:S(2)}) collective-permute-start(bf16[32,128,128]{2,1,0:T(8,128)(2,1)S(1)} %shard_map.93), channel_id=1, source_target_pairs={{0,1},{1,0},{2,3},{3,2},{4,5},{5,4},{6,7},{7,6},{8,9},{9,8},{10,11... | collective-permute-start | bytes 3145736 | tf_op jit(solution)/shard_map/ppermute | solution.py:195
  5.1 2.0 %shard_map.91.refs_0_ = bf16[32,128,128]{2,1,0:T(8,128)(2,1)S(1)} custom-call(s32[1]{0:T(128)} %bitcast.2.half_ref, bf16[128,8192]{1,0:T(8,128)(2,1)} %acts_ref.3, s32[64,128]{1,0:T(8,128)} %bitcast.16), custom_call_target="tpu_custom_call" | custom-call | flops 1048576 | bytes 2097152 | tf_op jit(solution)/shard_map/pallas_call | solution.py:31
  7.1 0.8 fusion.5
  7.9 0.8 fusion.10
  8.8 0.1 reshape.24.place_ref
  8.9 5.8 %shard_map.92 = (bf16[32,128,128]{2,1,0:T(8,128)(2,1)S(1)}, f32[16,128,128]{2,1,0:T(8,128)S(1)}, f32[16,128,128]{2,1,0:T(8,128)S(1)}, bf16[32,8,128,128]{3,2,1,0:T(8,128)(2,1)S(1)}) custom-call(s32[1]{0:T(128)} %constant.86.clone.1.starts_ref, s32[256]{0:T(256)S(1)} %reshape.24.place_ref, bf16[32,128,128]{2,1,0:T(8,128)(2,1)S(1)} %shard_map.91.refs_0_, ...), custom_call_target="tpu_custom_call" | custom-call | flops 1073741824 | bytes 8388608 | tf_op jit(solution)/shard_map/pallas_call | solution.py:128
  14.7 13.5 %collective-permute-done.1.refs_0_ = bf16[32,128,128]{2,1,0:T(8,128)(2,1)S(1)} collective-permute-done((bf16[32,128,128]{2,1,0:T(8,128)(2,1)S(1)}, bf16[32,128,128]{2,1,0:T(8,128)(2,1)S(1)}, u32[]{:S(2)}, u32[]{:S(2)}) %collective-permute-start.1) | collective-permute-done | bytes 1048608 | tf_op jit(solution)/shard_map/ppermute | solution.py:195
  28.3 4.7 %shard_map.94 = (bf16[32,128,128]{2,1,0:T(8,128)(2,1)S(1)}, f32[16,128,128]{2,1,0:T(8,128)S(1)}, f32[16,128,128]{2,1,0:T(8,128)S(1)}) custom-call(s32[1]{0:T(128)} %constant.86.clone.1.starts_ref, s32[256]{0:T(256)S(1)} %reshape.24.place_ref, bf16[32,128,128]{2,1,0:T(8,128)(2,1)S(1)} %collective-permute-done.1.refs_0_, ...), custom_call_target="tpu_custom_call" | custom-call | flops 1073741824 | bytes 8388608 | tf_op jit(solution)/shard_map/pallas_call | solution.py:128
  33.1 1.3 convert_add_fusion.3
  34.4 1.7 %collective-permute-start.5 = (bf16[16,128,128]{2,1,0:T(8,128)(2,1)S(1)}, bf16[16,128,128]{2,1,0:T(8,128)(2,1)S(1)}, u32[]{:S(2)}, u32[]{:S(2)}) collective-permute-start(bf16[16,128,128]{2,1,0:T(8,128)(2,1)S(1)} %get-tuple-element.50), channel_id=1, source_target_pairs={{0,1},{1,0},{2,3},{3,2},{4,5},{5,4},{6,7},{7,6},{8,9},{9,8},{10,11... | collective-permute-start | bytes 1572872 | tf_op jit(solution)/shard_map/ppermute | solution.py:230
  36.1 1.1 convert_add_fusion.2
  37.2 11.5 %collective-permute-done.5 = bf16[16,128,128]{2,1,0:T(8,128)(2,1)S(1)} collective-permute-done((bf16[16,128,128]{2,1,0:T(8,128)(2,1)S(1)}, bf16[16,128,128]{2,1,0:T(8,128)(2,1)S(1)}, u32[]{:S(2)}, u32[]{:S(2)}) %collective-permute-start.5) | collective-permute-done | bytes 524320 | tf_op jit(solution)/shard_map/ppermute | solution.py:230
  48.7 0.2 fusion.16
  48.9 1.8 %collective-permute-start.6 = (bf16[16,128,128]{2,1,0:T(8,128)(2,1)S(1)}, bf16[16,128,128]{2,1,0:T(8,128)(2,1)S(1)}, u32[]{:S(2)}, u32[]{:S(2)}) collective-permute-start(bf16[16,128,128]{2,1,0:T(8,128)(2,1)S(1)} %get-tuple-element.52), channel_id=1, source_target_pairs={{0,16},{8,24},{16,0},{24,8},{1,17},{9,25},{17,1},{25,9},{2,18},{10... | collective-permute-start | bytes 1572872 | tf_op jit(solution)/shard_map/ppermute | solution.py:238
  50.7 1.5 %collective-permute-start.7 = (bf16[128,16]{0,1:T(8,128)(2,1)S(1)}, bf16[128,16]{0,1:T(8,128)(2,1)S(1)}, u32[]{:S(2)}, u32[]{:S(2)}) collective-permute-start(bf16[128,16]{0,1:T(8,128)(2,1)S(1)} %get-tuple-element.74), channel_id=1, source_target_pairs={{0,1},{1,0},{2,3},{3,2},{4,5},{5,4},{6,7},{7,6},{8,9},{9,8},{10,11... | collective-permute-start | bytes 12296 | tf_op jit(solution)/shard_map/ppermute | solution.py:198
  52.2 0.5 collective-permute-start.3
  52.7 1.6 %collective-permute-done.7 = bf16[128,16]{0,1:T(8,128)(2,1)S(1)} collective-permute-done((bf16[128,16]{0,1:T(8,128)(2,1)S(1)}, bf16[128,16]{0,1:T(8,128)(2,1)S(1)}, u32[]{:S(2)}, u32[]{:S(2)}) %collective-permute-start.7) | collective-permute-done | bytes 4128 | tf_op jit(solution)/shard_map/ppermute | solution.py:198
  54.3 8.1 %collective-permute-done.6 = bf16[16,128,128]{2,1,0:T(8,128)(2,1)S(1)} collective-permute-done((bf16[16,128,128]{2,1,0:T(8,128)(2,1)S(1)}, bf16[16,128,128]{2,1,0:T(8,128)(2,1)S(1)}, u32[]{:S(2)}, u32[]{:S(2)}) %collective-permute-start.6) | collective-permute-done | bytes 524320 | tf_op jit(solution)/shard_map/ppermute | solution.py:238
  62.4 0.4 multiply_convert_fusion.1.refs_0_
  62.9 2.5 %collective-permute-done.3 = bf16[16,128,128]{2,1,0:T(8,128)(2,1)S(1)} collective-permute-done((bf16[16,128,128]{2,1,0:T(8,128)(2,1)}, bf16[16,128,128]{2,1,0:T(8,128)(2,1)S(1)}, u32[]{:S(2)}, u32[]{:S(2)}) %collective-permute-start.3) | collective-permute-done | bytes 524320 | tf_op jit(solution)/shard_map/ppermute | solution.py:233
  65.4 1.0 fusion.17
  66.4 0.5 collective-permute-start.4
  67.1 5.8 %shard_map.95 = (bf16[16,128,128]{2,1,0:T(8,128)(2,1)S(1)}, bf16[16,128,128]{2,1,0:T(8,128)(2,1)S(1)}, bf16[16,128,128]{2,1,0:T(8,128)(2,1)S(1)}, bf16[16,128,12...) custom-call(s32[2]{0:T(128)S(1)} %pad_add_fusion.starts_ref, s32[256]{0:T(256)S(1)} %reshape.23.place_ref, ...), custom_call_target="tpu_custom_call" | custom-call | flops 1073741824 | bytes 8388608 | tf_op jit(solution)/shard_map/pallas_call | solution.py:128
  72.9 5.8 %collective-permute-done.4 = bf16[16,128,128]{2,1,0:T(8,128)(2,1)} collective-permute-done((bf16[16,128,128]{2,1,0:T(8,128)(2,1)}, bf16[16,128,128]{2,1,0:T(8,128)(2,1)}, u32[]{:S(2)}, u32[]{:S(2)}) %collective-permute-start.4) | collective-permute-done | bytes 524320 | tf_op jit(solution)/shard_map/ppermute | solution.py:238
  78.8 1.4 multiply_convert_fusion.refs_0_
  80.2 1.6 %collective-permute-start.11 = (bf16[16,128,128]{2,1,0:T(8,128)(2,1)S(1)}, bf16[16,128,128]{2,1,0:T(8,128)(2,1)S(1)}, u32[]{:S(2)}, u32[]{:S(2)}) collective-permute-start(bf16[16,128,128]{2,1,0:T(8,128)(2,1)S(1)} %get-tuple-element.60), channel_id=1, source_target_pairs={{0,1},{1,0},{2,3},{3,2},{4,5},{5,4},{6,7},{7,6},{8,9},{9,8},{10,11... | collective-permute-start | bytes 1572872 | tf_op jit(solution)/shard_map/ppermute | solution.py:253
  81.8 0.5 collective-permute-start.16
  82.3 1.5 %collective-permute-start.14 = (bf16[16,128,128]{2,1,0:T(8,128)(2,1)S(1)}, bf16[16,128,128]{2,1,0:T(8,128)(2,1)S(1)}, u32[]{:S(2)}, u32[]{:S(2)}) collective-permute-start(bf16[16,128,128]{2,1,0:T(8,128)(2,1)S(1)} %get-tuple-element.62), channel_id=1, source_target_pairs={{0,1},{1,0},{2,3},{3,2},{4,5},{5,4},{6,7},{7,6},{8,9},{9,8},{10,11... | collective-permute-start | bytes 1572872 | tf_op jit(solution)/shard_map/ppermute | solution.py:253
  83.8 4.8 %shard_map.96 = (f32[16,128,128]{2,1,0:T(8,128)S(1)}, f32[16,128,128]{2,1,0:T(8,128)S(1)}, f32[16,128,128]{2,1,0:T(8,128)S(1)}, f32[16,128,128]{2,1,0:T(8,128)S(1)}) custom-call(s32[2]{0:T(128)S(1)} %pad_add_fusion.starts_ref, s32[256]{0:T(256)S(1)} %reshape.23.place_ref, bf16[16,128,128]{2,1,0:T(8,128)(2,1)S(1)} %multiply_convert_fusion.refs_0_, ...), custom_call_target="tpu_custom_call" | custom-call | flops 1073741824 | bytes 8388608 | tf_op jit(solution)/shard_map/pallas_call | solution.py:128
  88.6 6.5 %collective-permute-done.11.refs_1_ = bf16[16,128,128]{2,1,0:T(8,128)(2,1)S(1)} collective-permute-done((bf16[16,128,128]{2,1,0:T(8,128)(2,1)S(1)}, bf16[16,128,128]{2,1,0:T(8,128)(2,1)S(1)}, u32[]{:S(2)}, u32[]{:S(2)}) %collective-permute-start.11) | collective-permute-done | bytes 524320 | tf_op jit(solution)/shard_map/ppermute | solution.py:253
  95.1 0.1 shard_map.97
  95.2 3.5 %collective-permute-start.12 = (bf16[16,128,128]{2,1,0:T(8,128)(2,1)S(1)}, bf16[16,128,128]{2,1,0:T(8,128)(2,1)S(1)}, u32[]{:S(2)}, u32[]{:S(2)}) collective-permute-start(bf16[16,128,128]{2,1,0:T(8,128)(2,1)S(1)} %shard_map.97), channel_id=1, source_target_pairs={{0,2},{6,4},{1,3},{7,5},{8,10},{14,12},{9,11},{15,13},{16,18},{22,... | collective-permute-start | bytes 1572872 | tf_op jit(solution)/shard_map/ppermute | solution.py:260
  98.7 7.6 %collective-permute-done.16.refs_1_ = bf16[16,128,128]{2,1,0:T(8,128)(2,1)S(1)} collective-permute-done((bf16[16,128,128]{2,1,0:T(8,128)(2,1)S(1)}, bf16[16,128,128]{2,1,0:T(8,128)(2,1)S(1)}, u32[]{:S(2)}, u32[]{:S(2)}) %collective-permute-start.16) | collective-permute-done | bytes 524320 | tf_op jit(solution)/shard_map/ppermute | solution.py:253
  106.3 0.1 shard_map.100
  106.5 3.5 %collective-permute-start.17 = (bf16[16,128,128]{2,1,0:T(8,128)(2,1)S(1)}, bf16[16,128,128]{2,1,0:T(8,128)(2,1)S(1)}, u32[]{:S(2)}, u32[]{:S(2)}) collective-permute-start(bf16[16,128,128]{2,1,0:T(8,128)(2,1)S(1)} %shard_map.100), channel_id=1, source_target_pairs={{0,2},{6,4},{1,3},{7,5},{8,10},{14,12},{9,11},{15,13},{16,18},{22,... | collective-permute-start | bytes 1572872 | tf_op jit(solution)/shard_map/ppermute | solution.py:261
  110.0 1.6 %collective-permute-start.10 = (bf16[16,128,128]{2,1,0:T(8,128)(2,1)S(1)}, bf16[16,128,128]{2,1,0:T(8,128)(2,1)S(1)}, u32[]{:S(2)}, u32[]{:S(2)}) collective-permute-start(bf16[16,128,128]{2,1,0:T(8,128)(2,1)S(1)} %get-tuple-element.58), channel_id=1, source_target_pairs={{0,1},{1,0},{2,3},{3,2},{4,5},{5,4},{6,7},{7,6},{8,9},{9,8},{10,11... | collective-permute-start | bytes 1572872 | tf_op jit(solution)/shard_map/ppermute | solution.py:253
  111.5 6.0 %collective-permute-done.14.refs_1_ = bf16[16,128,128]{2,1,0:T(8,128)(2,1)S(1)} collective-permute-done((bf16[16,128,128]{2,1,0:T(8,128)(2,1)S(1)}, bf16[16,128,128]{2,1,0:T(8,128)(2,1)S(1)}, u32[]{:S(2)}, u32[]{:S(2)}) %collective-permute-start.14) | collective-permute-done | bytes 524320 | tf_op jit(solution)/shard_map/ppermute | solution.py:253
  117.6 0.1 shard_map.99
  117.7 1.6 %collective-permute-start.15 = (bf16[16,128,128]{2,1,0:T(8,128)(2,1)S(1)}, bf16[16,128,128]{2,1,0:T(8,128)(2,1)S(1)}, u32[]{:S(2)}, u32[]{:S(2)}) collective-permute-start(bf16[16,128,128]{2,1,0:T(8,128)(2,1)S(1)} %shard_map.99), channel_id=1, source_target_pairs={{0,2},{2,0},{4,6},{6,4},{1,3},{3,1},{5,7},{7,5},{8,10},{10,8},{12,... | collective-permute-start | bytes 1572872 | tf_op jit(solution)/shard_map/ppermute | solution.py:263
  119.3 0.2 shard_map.98
  119.5 1.3 collective-permute-start.13
  120.8 1.3 collective-permute-done.17.refs_2_
  122.1 0.2 shard_map.101
  122.3 0.7 collective-permute-start.18
  123.0 5.2 %collective-permute-done.10.refs_1_ = bf16[16,128,128]{2,1,0:T(8,128)(2,1)S(1)} collective-permute-done((bf16[16,128,128]{2,1,0:T(8,128)(2,1)S(1)}, bf16[16,128,128]{2,1,0:T(8,128)(2,1)S(1)}, u32[]{:S(2)}, u32[]{:S(2)}) %collective-permute-start.10) | collective-permute-done | bytes 524320 | tf_op jit(solution)/shard_map/ppermute | solution.py:253
  128.3 13.6 %collective-permute-done.15.refs_3_ = bf16[16,128,128]{2,1,0:T(8,128)(2,1)S(1)} collective-permute-done((bf16[16,128,128]{2,1,0:T(8,128)(2,1)S(1)}, bf16[16,128,128]{2,1,0:T(8,128)(2,1)S(1)}, u32[]{:S(2)}, u32[]{:S(2)}) %collective-permute-start.15) | collective-permute-done | bytes 524320 | tf_op jit(solution)/shard_map/ppermute | solution.py:263
  141.9 1.2 shard_map.102
  (26 shorter events, 0.6 us)
Async XLA Ops:
  0.0 52.7 %copy-start = (f32[8192]{0:T(1024)S(1)}, f32[8192]{0:T(1024)}, u32[]{:S(2)}) copy-start(f32[8192]{0:T(1024)} %param.13) | copy-start | bytes 98308
  2.0 26.2 %collective-permute-start.1 = (bf16[32,128,128]{2,1,0:T(8,128)(2,1)S(1)}, bf16[32,128,128]{2,1,0:T(8,128)(2,1)S(1)}, u32[]{:S(2)}, u32[]{:S(2)}) collective-permute-start(bf16[32,128,128]{2,1,0:T(8,128)(2,1)S(1)} %shard_map.93), channel_id=1, source_target_pairs={{0,1},{1,0},{2,3},{3,2},{4,5},{5,4},{6,7},{7,6},{8,9},{9,8},{10,11... | collective-permute-start | bytes 3145736 | tf_op jit(solution)/shard_map/ppermute | solution.py:195
  14.7 18.4 %collective-permute-start = (bf16[32,128,128]{2,1,0:T(8,128)(2,1)S(1)}, bf16[32,128,128]{2,1,0:T(8,128)(2,1)S(1)}, u32[]{:S(2)}, u32[]{:S(2)}) collective-permute-start(bf16[32,128,128]{2,1,0:T(8,128)(2,1)S(1)} %get-tuple-element.39), channel_id=1, source_target_pairs={{0,8},{8,0},{16,24},{24,16},{1,9},{9,1},{17,25},{25,17},{2,10},{10... | collective-permute-start | bytes 3145736 | tf_op jit(solution)/shard_map/ppermute | solution.py:223
  33.0 17.7 %copy-start.3 = (s32[128,64]{0,1:T(8,128)S(1)}, s32[128,64]{0,1:T(8,128)}, u32[]{:S(2)}) copy-start(s32[128,64]{0,1:T(8,128)} %param.14) | copy-start | bytes 98308
  33.0 3.1 %collective-permute-start.2 = (bf16[32,128,128]{2,1,0:T(8,128)(2,1)S(1)}, bf16[32,128,128]{2,1,0:T(8,128)(2,1)S(1)}, u32[]{:S(2)}, u32[]{:S(2)}) collective-permute-start(bf16[32,128,128]{2,1,0:T(8,128)(2,1)S(1)} %get-tuple-element.44), channel_id=1, source_target_pairs={{0,8},{8,0},{16,24},{24,16},{1,9},{9,1},{17,25},{25,17},{2,10},{10... | collective-permute-start | bytes 3145736 | tf_op jit(solution)/shard_map/ppermute | solution.py:223
  34.4 14.3 %collective-permute-start.5 = (bf16[16,128,128]{2,1,0:T(8,128)(2,1)S(1)}, bf16[16,128,128]{2,1,0:T(8,128)(2,1)S(1)}, u32[]{:S(2)}, u32[]{:S(2)}) collective-permute-start(bf16[16,128,128]{2,1,0:T(8,128)(2,1)S(1)} %get-tuple-element.50), channel_id=1, source_target_pairs={{0,1},{1,0},{2,3},{3,2},{4,5},{5,4},{6,7},{7,6},{8,9},{9,8},{10,11... | collective-permute-start | bytes 1572872 | tf_op jit(solution)/shard_map/ppermute | solution.py:230
  36.1 29.2 %copy-start.2 = (f32[16,128,128]{2,1,0:T(8,128)S(1)}, f32[16,128,128]{2,1,0:T(8,128)}, u32[]{:S(2)}) copy-start(f32[16,128,128]{2,1,0:T(8,128)} %get-tuple-element.41) | copy-start | bytes 3145732
  48.9 13.5 %collective-permute-start.6 = (bf16[16,128,128]{2,1,0:T(8,128)(2,1)S(1)}, bf16[16,128,128]{2,1,0:T(8,128)(2,1)S(1)}, u32[]{:S(2)}, u32[]{:S(2)}) collective-permute-start(bf16[16,128,128]{2,1,0:T(8,128)(2,1)S(1)} %get-tuple-element.52), channel_id=1, source_target_pairs={{0,16},{8,24},{16,0},{24,8},{1,17},{9,25},{17,1},{25,9},{2,18},{10... | collective-permute-start | bytes 1572872 | tf_op jit(solution)/shard_map/ppermute | solution.py:238
  50.7 3.6 %collective-permute-start.7 = (bf16[128,16]{0,1:T(8,128)(2,1)S(1)}, bf16[128,16]{0,1:T(8,128)(2,1)S(1)}, u32[]{:S(2)}, u32[]{:S(2)}) collective-permute-start(bf16[128,16]{0,1:T(8,128)(2,1)S(1)} %get-tuple-element.74), channel_id=1, source_target_pairs={{0,1},{1,0},{2,3},{3,2},{4,5},{5,4},{6,7},{7,6},{8,9},{9,8},{10,11... | collective-permute-start | bytes 12296 | tf_op jit(solution)/shard_map/ppermute | solution.py:198
  52.2 13.2 %collective-permute-start.3 = (bf16[16,128,128]{2,1,0:T(8,128)(2,1)}, bf16[16,128,128]{2,1,0:T(8,128)(2,1)S(1)}, u32[]{:S(2)}, u32[]{:S(2)}) collective-permute-start(bf16[16,128,128]{2,1,0:T(8,128)(2,1)} %get-tuple-element.46), channel_id=1, source_target_pairs={{0,1},{1,0},{2,3},{3,2},{4,5},{5,4},{6,7},{7,6},{8,9},{9,8},{10,11... | collective-permute-start | bytes 1572872 | tf_op jit(solution)/shard_map/ppermute | solution.py:233
  62.8 4.3 %collective-permute-start.8 = (bf16[16,128,128]{2,1,0:T(8,128)(2,1)S(1)}, bf16[16,128,128]{2,1,0:T(8,128)(2,1)S(1)}, u32[]{:S(2)}, u32[]{:S(2)}) collective-permute-start(bf16[16,128,128]{2,1,0:T(8,128)(2,1)S(1)} %multiply_convert_fusion.1.refs_0_), channel_id=1, source_target_pairs={{0,8},{8,0},{16,24},{24,16},{1,9},{9,1},{17,25},{25,17},{2,10},{10... | collective-permute-start | bytes 1572872 | tf_op jit(solution)/shard_map/ppermute | solution.py:244
  66.4 12.4 %collective-permute-start.4 = (bf16[16,128,128]{2,1,0:T(8,128)(2,1)}, bf16[16,128,128]{2,1,0:T(8,128)(2,1)}, u32[]{:S(2)}, u32[]{:S(2)}) collective-permute-start(bf16[16,128,128]{2,1,0:T(8,128)(2,1)} %get-tuple-element.48), channel_id=1, source_target_pairs={{0,16},{8,24},{16,0},{24,8},{1,17},{9,25},{17,1},{25,9},{2,18},{10... | collective-permute-start | bytes 1572872 | tf_op jit(solution)/shard_map/ppermute | solution.py:238
  80.1 3.7 %collective-permute-start.9 = (bf16[16,128,128]{2,1,0:T(8,128)(2,1)S(1)}, bf16[16,128,128]{2,1,0:T(8,128)(2,1)S(1)}, u32[]{:S(2)}, u32[]{:S(2)}) collective-permute-start(bf16[16,128,128]{2,1,0:T(8,128)(2,1)S(1)} %multiply_convert_fusion.refs_0_), channel_id=1, source_target_pairs={{0,8},{8,0},{16,24},{24,16},{1,9},{9,1},{17,25},{25,17},{2,10},{10... | collective-permute-start | bytes 1572872 | tf_op jit(solution)/shard_map/ppermute | solution.py:244
  80.2 14.9 %collective-permute-start.11 = (bf16[16,128,128]{2,1,0:T(8,128)(2,1)S(1)}, bf16[16,128,128]{2,1,0:T(8,128)(2,1)S(1)}, u32[]{:S(2)}, u32[]{:S(2)}) collective-permute-start(bf16[16,128,128]{2,1,0:T(8,128)(2,1)S(1)} %get-tuple-element.60), channel_id=1, source_target_pairs={{0,1},{1,0},{2,3},{3,2},{4,5},{5,4},{6,7},{7,6},{8,9},{9,8},{10,11... | collective-permute-start | bytes 1572872 | tf_op jit(solution)/shard_map/ppermute | solution.py:253
  81.8 24.5 %collective-permute-start.16 = (bf16[16,128,128]{2,1,0:T(8,128)(2,1)S(1)}, bf16[16,128,128]{2,1,0:T(8,128)(2,1)S(1)}, u32[]{:S(2)}, u32[]{:S(2)}) collective-permute-start(bf16[16,128,128]{2,1,0:T(8,128)(2,1)S(1)} %get-tuple-element.64), channel_id=1, source_target_pairs={{0,1},{1,0},{2,3},{3,2},{4,5},{5,4},{6,7},{7,6},{8,9},{9,8},{10,11... | collective-permute-start | bytes 1572872 | tf_op jit(solution)/shard_map/ppermute | solution.py:253
  82.3 59.5 %copy-start.1 = (f32[2048]{0:T(1024)S(1)}, f32[2048]{0:T(1024)}, u32[]{:S(2)}) copy-start(f32[2048]{0:T(1024)} %param.17) | copy-start | bytes 24580
  82.3 35.2 %collective-permute-start.14 = (bf16[16,128,128]{2,1,0:T(8,128)(2,1)S(1)}, bf16[16,128,128]{2,1,0:T(8,128)(2,1)S(1)}, u32[]{:S(2)}, u32[]{:S(2)}) collective-permute-start(bf16[16,128,128]{2,1,0:T(8,128)(2,1)S(1)} %get-tuple-element.62), channel_id=1, source_target_pairs={{0,1},{1,0},{2,3},{3,2},{4,5},{5,4},{6,7},{7,6},{8,9},{9,8},{10,11... | collective-permute-start | bytes 1572872 | tf_op jit(solution)/shard_map/ppermute | solution.py:253
  95.2 24.1 %collective-permute-start.12 = (bf16[16,128,128]{2,1,0:T(8,128)(2,1)S(1)}, bf16[16,128,128]{2,1,0:T(8,128)(2,1)S(1)}, u32[]{:S(2)}, u32[]{:S(2)}) collective-permute-start(bf16[16,128,128]{2,1,0:T(8,128)(2,1)S(1)} %shard_map.97), channel_id=1, source_target_pairs={{0,2},{6,4},{1,3},{7,5},{8,10},{14,12},{9,11},{15,13},{16,18},{22,... | collective-permute-start | bytes 1572872 | tf_op jit(solution)/shard_map/ppermute | solution.py:260
  106.5 15.7 %collective-permute-start.17 = (bf16[16,128,128]{2,1,0:T(8,128)(2,1)S(1)}, bf16[16,128,128]{2,1,0:T(8,128)(2,1)S(1)}, u32[]{:S(2)}, u32[]{:S(2)}) collective-permute-start(bf16[16,128,128]{2,1,0:T(8,128)(2,1)S(1)} %shard_map.100), channel_id=1, source_target_pairs={{0,2},{6,4},{1,3},{7,5},{8,10},{14,12},{9,11},{15,13},{16,18},{22,... | collective-permute-start | bytes 1572872 | tf_op jit(solution)/shard_map/ppermute | solution.py:261
  110.0 18.3 %collective-permute-start.10 = (bf16[16,128,128]{2,1,0:T(8,128)(2,1)S(1)}, bf16[16,128,128]{2,1,0:T(8,128)(2,1)S(1)}, u32[]{:S(2)}, u32[]{:S(2)}) collective-permute-start(bf16[16,128,128]{2,1,0:T(8,128)(2,1)S(1)} %get-tuple-element.58), channel_id=1, source_target_pairs={{0,1},{1,0},{2,3},{3,2},{4,5},{5,4},{6,7},{7,6},{8,9},{9,8},{10,11... | collective-permute-start | bytes 1572872 | tf_op jit(solution)/shard_map/ppermute | solution.py:253
  117.7 24.2 %collective-permute-start.15 = (bf16[16,128,128]{2,1,0:T(8,128)(2,1)S(1)}, bf16[16,128,128]{2,1,0:T(8,128)(2,1)S(1)}, u32[]{:S(2)}, u32[]{:S(2)}) collective-permute-start(bf16[16,128,128]{2,1,0:T(8,128)(2,1)S(1)} %shard_map.99), channel_id=1, source_target_pairs={{0,2},{2,0},{4,6},{6,4},{1,3},{3,1},{5,7},{7,5},{8,10},{10,8},{12,... | collective-permute-start | bytes 1572872 | tf_op jit(solution)/shard_map/ppermute | solution.py:263
  119.5 22.3 %collective-permute-start.13 = (bf16[16,128,128]{2,1,0:T(8,128)(2,1)S(1)}, bf16[16,128,128]{2,1,0:T(8,128)(2,1)S(1)}, u32[]{:S(2)}, u32[]{:S(2)}) collective-permute-start(bf16[16,128,128]{2,1,0:T(8,128)(2,1)S(1)} %shard_map.98), channel_id=1, source_target_pairs={{2,6},{4,0},{3,7},{5,1},{10,14},{12,8},{11,15},{13,9},{18,22},{20,... | collective-permute-start | bytes 1572872 | tf_op jit(solution)/shard_map/ppermute | solution.py:262
  122.3 19.5 %collective-permute-start.18 = (bf16[16,128,128]{2,1,0:T(8,128)(2,1)S(1)}, bf16[16,128,128]{2,1,0:T(8,128)(2,1)S(1)}, u32[]{:S(2)}, u32[]{:S(2)}) collective-permute-start(bf16[16,128,128]{2,1,0:T(8,128)(2,1)S(1)} %shard_map.101), channel_id=1, source_target_pairs={{2,4},{4,2},{3,5},{5,3},{10,12},{12,10},{11,13},{13,11},{18,20},{2... | collective-permute-start | bytes 1572872 | tf_op jit(solution)/shard_map/ppermute | solution.py:264

commit v3 on v2

--- a/solution.py
+++ b/solution.py
@@ -23,11 +23,10 @@
         out_ref[i] = (x * live[:, i:i + 1]).astype(jnp.bfloat16)
 
 
-def masked_half(acts, act_mask, half):
+def masked(acts, act_mask, first, blocks, steps=1):
     rows, width = acts.shape
-    blocks = act_mask.shape[1] // 2
     block = width // act_mask.shape[1]
-    steps = 2
+    unit = blocks // steps
     return pl.pallas_call(
         mask_kernel,
         out_shape=pltpu.VMEM((blocks, rows, block), jnp.bfloat16),
@@ -35,14 +34,14 @@
             num_scalar_prefetch=1,
             grid=(steps,),
             in_specs=[
-                pl.BlockSpec((rows, width // 2 // steps), lambda s, h: (0, h[0] * steps + s)),
-                pl.BlockSpec((blocks // steps, rows), lambda s, h: (h[0] * steps + s, 0)),
+                pl.BlockSpec((rows, unit * block), lambda s, f: (0, f[0] + s)),
+                pl.BlockSpec((unit, rows), lambda s, f: (f[0] + s, 0)),
             ],
-            out_specs=pl.BlockSpec((blocks // steps, rows, block), lambda s, h: (s, 0, 0)),
+            out_specs=pl.BlockSpec((unit, rows, block), lambda s, f: (s, 0, 0)),
         ),
         compiler_params=pltpu.CompilerParams(vmem_limit_bytes=VMEM_LIMIT),
-        cost_estimate=pl.CostEstimate(flops=rows * width, bytes_accessed=2 * rows * width, transcendentals=0),
-    )(half.reshape(1), in_hbm(acts), in_hbm(act_mask.T))
+        cost_estimate=pl.CostEstimate(flops=rows * blocks, bytes_accessed=4 * rows * blocks * block, transcendentals=0),
+    )(first.reshape(1), in_hbm(acts), in_hbm(act_mask.T))
 
 
 def clear(acc):
@@ -89,13 +88,12 @@
     x_refs, w_ref, refs = refs[:parts], refs[parts], refs[parts + 1:]
     copies = []
     if load:
-        *refs, sems = refs
-        *outs, keep_ref, acc = refs
+        *outs, held_ref, acc, sems = refs
         for part, x_ref in enumerate(x_refs):
             for first in range(0, x_ref.shape[0], UNROLL):
                 rows = pl.ds(starts_ref[part] + first, UNROLL)
-                copies.append(pltpu.make_async_copy(w_ref.at[rows], keep_ref.at[rows], sems.at[len(copies)]))
-        w_ref = keep_ref
+                copies.append(pltpu.make_async_copy(w_ref.at[rows], held_ref.at[rows], sems.at[len(copies)]))
+        w_ref = held_ref
     else:
         *outs, acc = refs
     for copy in copies:
@@ -111,7 +109,7 @@
     write_out(acc, outs)
 
 
-def fold(xs, weights, places, starts, segments, load=False):
+def fold(xs, weights, places, starts, segments, load=False, keep=False):
     rows_in, entries, block, _ = weights.shape
     rows = xs[0].shape[1]
     total = sum(count for count, _ in segments)
@@ -120,18 +118,22 @@
     hbm = pl.BlockSpec(memory_space=pltpu.HBM)
     out_shape = [pltpu.VMEM((count, rows, block), kind) for count, kind in segments]
     scratch = [pltpu.VMEM((total, rows, block), jnp.float32)]
+    held = pltpu.VMEM(weights.shape, weights.dtype)
+    limit = VMEM_LIMIT
     if load:
-        out_shape.append(pltpu.VMEM(weights.shape, weights.dtype))
         scratch.append(pltpu.SemaphoreType.DMA((rows_in // UNROLL,)))
-    elif len(segments) == 1:
-        scratch = []
+        if keep:
+            out_shape.append(held)
+        else:
+            scratch.insert(0, held)
+            limit += weights.size * weights.dtype.itemsize
     return pl.pallas_call(
         functools.partial(fold_kernel, len(xs), load),
         out_shape=out_shape,
         in_specs=[smem, smem] + [vmem] * len(xs) + [hbm if load else vmem],
         out_specs=[vmem] * len(out_shape),
         scratch_shapes=scratch,
-        compiler_params=pltpu.CompilerParams(vmem_limit_bytes=VMEM_LIMIT),
+        compiler_params=pltpu.CompilerParams(vmem_limit_bytes=limit),
         cost_estimate=pl.CostEstimate(
             flops=2 * rows * rows_in * entries * block * block,
             bytes_accessed=2 * weights.size,
@@ -164,13 +166,14 @@
     )(*map(in_vmem, parts))
 
 
-def finish_kernel(*refs):
-    *parts, bias_ref, out_ref = refs
-    share, _, block = parts[0].shape
+def finish_kernel(mine_ref, got_ref, near_ref, *refs):
+    cross_refs, bias_ref, out_ref = refs[:-2], refs[-2], refs[-1]
+    share, _, block = mine_ref.shape
+    size = cross_refs[0].shape[0]
     for i in range(share):
-        total = parts[0][i]
-        for part in parts[1:]:
-            total = total + part[i].astype(jnp.float32)
+        total = mine_ref[i] + got_ref[i].astype(jnp.float32) + near_ref[i].astype(jnp.float32)
+        for cross_ref in cross_refs[i // size::share // size]:
+            total = total + cross_ref[i % size].astype(jnp.float32)
         total = jnp.maximum(total + bias_ref[i:i + 1, :], 0.0)
         out_ref[:, i * block:(i + 1) * block] = total.astype(jnp.bfloat16)
 
@@ -192,8 +195,14 @@
     over_x = functools.partial(lax.ppermute, axis_name="row", perm=[(i, i ^ 2) for i in range(size_row)])
     zero = jnp.int32(0)
 
-    other_x = over_depth(masked_half(acts, act_mask, 1 - d))
-    own_x = masked_half(acts, act_mask, d)
+    side = lax.rem(c, 2)
+    eighth, fourth = half_in // 4, half_in // 2
+    part_x = over_depth(masked(acts, act_mask, (1 - d) * 4 + side, eighth))
+    rest_x = over_depth(masked(acts, act_mask, (1 - d) * 2 + 1, fourth))
+    own_x = masked(acts, act_mask, d * 2, half_in, steps=2)
+    swapped_x = lax.ppermute(part_x, "col", [(i, i ^ 1) for i in range(size_col)])
+    other_x = [part_x, swapped_x, rest_x]
+    other_starts = [side * eighth, (1 - side) * eighth, jnp.int32(fourth)]
     mask_own = lax.dynamic_slice_in_dim(mask2, d * half_mid + core * quarter, quarter, 1).astype(bf16)
     mask_other = over_depth(
         lax.dynamic_slice_in_dim(mask2, (1 - d) * half_mid + core * quarter, quarter, 1).astype(bf16)
@@ -225,10 +234,10 @@
             ((send + low[:quarter].astype(f32)).astype(bf16), keep + low[quarter:].astype(f32))
         )
 
-    *sums, w1 = fold([own_x], w1, place1, [zero], segments, load=True)
+    sums = fold([own_x], w1, place1, [zero], segments, load=True)
     send_own, keep_own = core_sums(*sums)
     got_other = over_depth(send_own)
-    sums = fold([other_x], w1, place1, [zero], segments)
+    sums = fold(other_x, w1, place1, other_starts, segments, load=True)
     send_other, keep_other = core_sums(*sums)
     got_own = over_depth(send_other)
 
@@ -247,22 +256,25 @@
     sums_own = x_sums(keep_own, got_own)
     hidden_other = hidden(*sums_other, mask_other)
     starts = [core * quarter, (1 - core) * quarter]
-    *for_other, w2 = fold(hidden_other, w2, place2, starts, [(share, bf16)] * size_col, load=True)
+    cuts = [share // 2] * 4 + [share] * 2
+    *for_other, w2 = fold(hidden_other, w2, place2, starts, [(n, bf16) for n in cuts], load=True, keep=True)
     got = []
     for part in for_other:
         got.append(over_depth(part))
     part_own, low_own, w2 = lax.optimization_barrier((*sums_own, w2))
     hidden_own = hidden(part_own, low_own, mask_own)
-    mine = fold(hidden_own, w2, place2, starts, [(share, f32)] * size_col)
-
-    over_col = functools.partial(lax.ppermute, axis_name="col")
-    ends = [(0, 1), (3, 2)]
-    ends0 = over_col(add([mine[0], got[0]]), perm=ends)
-    ends1 = over_col(add([mine[1], got[1]]), perm=ends)
-    cross0 = over_col(add([mine[0], got[0], ends0]), perm=[(1, 3), (2, 0)])
-    near = over_col(add([mine[2], got[2]]), perm=[(i, i ^ 1) for i in range(size_col)])
-    cross1 = over_col(add([mine[1], got[1], ends1]), perm=[(1, 2), (2, 1)])
-    parts = [mine[3], got[3], cross0, near, cross1]
+    mine = fold(hidden_own, w2, place2, starts, [(n, f32) for n in cuts])
+
+    def over_col(parts, perm):
+        return lax.ppermute(add(parts), "col", perm)
+
+    cross = []
+    for i in range(4):
+        total = [mine[i], got[i]]
+        total.append(over_col(total, [(0, 1), (3, 2)]))
+        cross.append(over_col(total, [(1, 3), (2, 0)] if i < 2 else [(1, 2), (2, 1)]))
+    near = over_col([mine[4], got[4]], [(i, i ^ 1) for i in range(size_col)])
+    parts = [mine[5], got[5], near, *cross]
     return pl.pallas_call(
         finish_kernel,
         out_shape=jax.ShapeDtypeStruct((rows, share * block), bf16),

time: 145 us -> 159 us (1.097); the launches traced: 143 us -> 159 us
  starting transfers between devices: 25.2 us -> 31.5 us
  Pallas kernels: 27.1 us -> 31.9 us
  waiting for transfers between devices: 83.3 us -> 85.7 us
  local copies, waits for them, and re-layouts: 0.35 us -> 2 us
    ppermute x6 -> x12, starting transfers between devices: 13.7 us -> 19 us  [the longest x9 13.9 us: over_col(): return lax.ppermute(add(parts), 'col', perm)]
    ppermute x6 -> x12, waiting for transfers between devices: 28.4 us -> 33 us  [the longest x9 26.2 us: over_col(): return lax.ppermute(add(parts), 'col', perm)]
    ppermute x4 -> x6, waiting for transfers between devices: 25.3 us -> 22.5 us  [exchange_plan(): got.append(over_depth(part))]
    pallas_call x4, Pallas kernels: 21.1 us -> 23.5 us  [fold(): pl.pallas_call(functools.partial(fold_kernel, len(xs), load), out_shape=o...]
    pallas_call x2 -> x3, Pallas kernels: 4.06 us -> 6.33 us  [masked(): pl.pallas_call(mask_kernel, out_shape=pltpu.VMEM((blocks, rows, block), j...]
    unnamed x8 -> x12, local copies, waits for them, and re-layouts: 0.02 us -> 1.67 us
    ppermute x4 -> x6, starting transfers between devices: 5.14 us -> 6.21 us  [exchange_plan(): got.append(over_depth(part))]
  transfers between devices with their start and end apart: 19 -> 27, of which waited for: 12 -> 13; matrix products, arithmetic and copies ran while one was open for 4% -> 5% of each run, Pallas kernels for 17% -> 18%
where the time goes in v3:
time: 159 us
  waiting for transfers between devices  85.7 us (54%)
  Pallas kernels  31.9 us (20%)
  starting transfers between devices  31.5 us (20%)
  other arithmetic  7.39 us (5%)
  local copies, waits for them, and re-layouts  2 us (1%)
    ppermute x9, waiting for transfers between devices, over_col(): return lax.ppermute(add(parts), 'col', perm)  26.2 us
    pallas_call x4, Pallas kernels, fold(): pl.pallas_call(functools.partial(fold_kernel, len(xs), load), out_shape=o...  23.5 us
    ppermute x6, waiting for transfers between devices, exchange_plan(): got.append(over_depth(part))  22.5 us
    ppermute x2, waiting for transfers between devices, x_sums(): return (part, over_x(low))  15.1 us
    ppermute x9, starting transfers between devices, over_col(): return lax.ppermute(add(parts), 'col', perm)  13.9 us
    ppermute x1, waiting for transfers between devices, exchange_plan(): got_other = over_depth(send_own)  12.3 us
    ppermute x1, waiting for transfers between devices, exchange_plan(): lax.ppermute(part_x, 'col', [(i, i ^ 1) for i in range(size_col)])  6.82 us
    pallas_call x3, Pallas kernels, masked(): pl.pallas_call(mask_kernel, out_shape=pltpu.VMEM((blocks, rows, block), j...  6.33 us
  transfers between devices with their start and end apart: 27, of which 13 were waited for; matrix products, arithmetic and copies ran while one was open for 5% of the time, Pallas kernels for 18%

profile of v3, /device:TPU:0, one launch (start us, length us, event | category | flops | bytes accessed | tf_op | source)
XLA Modules:
  0.0 158.9 jit_solution(7653660789260777458)
XLA Ops:
  0.0 2.0 %shard_map.93 = bf16[8,128,128]{2,1,0:T(8,128)(2,1)} custom-call(s32[1]{0:T(128)} %bitcast.6.half_ref, bf16[128,8192]{1,0:T(8,128)(2,1)} %acts_ref.5, s32[64,128]{1,0:T(8,128)} %bitcast.18), custom_call_target="tpu_custom_call" | custom-call | flops 1024 | bytes 524288 | tf_op jit(solution)/shard_map/pallas_call | solution.py:30
  2.0 3.0 %collective-permute-start.1 = (bf16[8,128,128]{2,1,0:T(8,128)(2,1)}, bf16[8,128,128]{2,1,0:T(8,128)(2,1)S(1)}, u32[]{:S(2)}, u32[]{:S(2)}) collective-permute-start(bf16[8,128,128]{2,1,0:T(8,128)(2,1)} %shard_map.93), channel_id=1, source_target_pairs={{0,1},{1,0},{2,3},{3,2},{4,5},{5,4},{6,7},{7,6},{8,9},{9,8},{10,11... | collective-permute-start | bytes 786440 | tf_op jit(solution)/shard_map/ppermute | solution.py:200
  5.0 2.3 %shard_map.94 = bf16[16,128,128]{2,1,0:T(8,128)(2,1)} custom-call(s32[1]{0:T(128)} %bitcast.7.half_ref, bf16[128,8192]{1,0:T(8,128)(2,1)} %acts_ref.5, s32[64,128]{1,0:T(8,128)} %bitcast.19), custom_call_target="tpu_custom_call" | custom-call | flops 2048 | bytes 1048576 | tf_op jit(solution)/shard_map/pallas_call | solution.py:30
  7.3 2.0 %shard_map.91.refs_0_ = bf16[32,128,128]{2,1,0:T(8,128)(2,1)S(1)} custom-call(s32[1]{0:T(128)} %bitcast.2.half_ref, bf16[128,8192]{1,0:T(8,128)(2,1)} %acts_ref.5, s32[64,128]{1,0:T(8,128)} %bitcast.20), custom_call_target="tpu_custom_call" | custom-call | flops 4096 | bytes 2097152 | tf_op jit(solution)/shard_map/pallas_call | solution.py:30
  9.3 0.8 fusion.5
  10.1 0.8 fusion.10
  11.1 6.7 %shard_map.92 = (bf16[32,128,128]{2,1,0:T(8,128)(2,1)}, f32[16,128,128]{2,1,0:T(8,128)S(1)}, f32[16,128,128]{2,1,0:T(8,128)S(1)}) custom-call(s32[1]{0:T(128)} %constant.91.clone.1.starts_ref, s32[256]{0:T(256)S(1)} %reshape.27.place_ref, bf16[32,128,128]{2,1,0:T(8,128)(2,1)S(1)} %shard_map.91.refs_0_, bf16[32,8,128,128]{3,2,1,0:T(8,128)(2,1)} %refs_3_.1), custom_call_target="tpu_custom_call" | custom-call | flops 1073741824 | bytes 8388608 | tf_op jit(solution)/shard_map/pallas_call | solution.py:130
  17.9 2.1 %collective-permute-start.2 = (bf16[8,128,128]{2,1,0:T(8,128)(2,1)S(1)}, bf16[8,128,128]{2,1,0:T(8,128)(2,1)S(1)}, u32[]{:S(2)}, u32[]{:S(2)}) collective-permute-start(bf16[8,128,128]{2,1,0:T(8,128)(2,1)S(1)} %collective-permute-done.1.refs_0_), channel_id=1, source_target_pairs={{0,2},{2,0},{4,6},{6,4},{1,3},{3,1},{5,7},{7,5},{8,10},{10,8},{12,... | collective-permute-start | bytes 786440 | tf_op jit(solution)/shard_map/ppermute | solution.py:203
  20.1 6.8 %collective-permute-done.2.refs_1_ = bf16[8,128,128]{2,1,0:T(8,128)(2,1)S(1)} collective-permute-done((bf16[8,128,128]{2,1,0:T(8,128)(2,1)S(1)}, bf16[8,128,128]{2,1,0:T(8,128)(2,1)S(1)}, u32[]{:S(2)}, u32[]{:S(2)}) %collective-permute-start.2) | collective-permute-done | bytes 262176 | tf_op jit(solution)/shard_map/ppermute | solution.py:203
  26.9 0.7 copy-done.1
  27.6 0.9 copy-done.2
  28.6 6.3 %shard_map.95 = (bf16[32,128,128]{2,1,0:T(8,128)(2,1)S(1)}, f32[16,128,128]{2,1,0:T(8,128)S(1)}, f32[16,128,128]{2,1,0:T(8,128)S(1)}) custom-call(s32[3]{0:T(128)S(1)} %pad_add_fusion.1.starts_ref, s32[256]{0:T(256)S(1)} %reshape.27.place_ref, bf16[8,128,128]{2,1,0:T(8,128)(2,1)S(1)} %collective-permute-done.1.refs_0_, bf16[8,128,128]{2,1,0:T(8,128)(2,1)S(1)} %copy-done.2, ...), custom_call_target="tpu_custom_call" | custom-call | flops 1073741824 | bytes 8388608 | tf_op jit(solution)/shard_map/pallas_call | solution.py:130
  35.0 2.4 %convert_add_fusion.3 = (f32[16,128,128]{2,1,0:T(8,128)}, bf16[16,128,128]{2,1,0:T(8,128)(2,1)S(1)}) fusion(f32[16,128,128]{2,1,0:T(8,128)S(1)} %get-tuple-element.43, bf16[32,128,128]{2,1,0:T(8,128)(2,1)} %collective-permute-done, f32[16,128,128]{2,1,0:T(8,128)S(1)} %get-tuple-element.41), kind=kLoop, calls=%fused_computation.6 | loop fusion | flops 1310720 | bytes 4718592 | tf_op jit(solution)/shard_map/add | solution.py:234
  37.4 1.7 %collective-permute-start.7 = (bf16[16,128,128]{2,1,0:T(8,128)(2,1)S(1)}, bf16[16,128,128]{2,1,0:T(8,128)(2,1)S(1)}, u32[]{:S(2)}, u32[]{:S(2)}) collective-permute-start(bf16[16,128,128]{2,1,0:T(8,128)(2,1)S(1)} %get-tuple-element.52), channel_id=1, source_target_pairs={{0,1},{1,0},{2,3},{3,2},{4,5},{5,4},{6,7},{7,6},{8,9},{9,8},{10,11... | collective-permute-start | bytes 1572872 | tf_op jit(solution)/shard_map/ppermute | solution.py:239
  39.4 12.3 %collective-permute-done.7 = bf16[16,128,128]{2,1,0:T(8,128)(2,1)S(1)} collective-permute-done((bf16[16,128,128]{2,1,0:T(8,128)(2,1)S(1)}, bf16[16,128,128]{2,1,0:T(8,128)(2,1)S(1)}, u32[]{:S(2)}, u32[]{:S(2)}) %collective-permute-start.7) | collective-permute-done | bytes 524320 | tf_op jit(solution)/shard_map/ppermute | solution.py:239
  51.9 1.7 %collective-permute-start.8 = (bf16[16,128,128]{2,1,0:T(8,128)(2,1)S(1)}, bf16[16,128,128]{2,1,0:T(8,128)(2,1)}, u32[]{:S(2)}, u32[]{:S(2)}) collective-permute-start(bf16[16,128,128]{2,1,0:T(8,128)(2,1)S(1)} %get-tuple-element.54), channel_id=1, source_target_pairs={{0,16},{8,24},{16,0},{24,8},{1,17},{9,25},{17,1},{25,9},{2,18},{10... | collective-permute-start | bytes 1572872 | tf_op jit(solution)/shard_map/ppermute | solution.py:247
  53.6 1.5 collective-permute-start.9
  55.2 0.5 collective-permute-start.5
  55.7 1.6 %collective-permute-done.9 = bf16[128,16]{0,1:T(8,128)(2,1)S(1)} collective-permute-done((bf16[128,16]{0,1:T(8,128)(2,1)S(1)}, bf16[128,16]{0,1:T(8,128)(2,1)S(1)}, u32[]{:S(2)}, u32[]{:S(2)}) %collective-permute-start.9) | collective-permute-done | bytes 4128 | tf_op jit(solution)/shard_map/ppermute | solution.py:207
  57.3 8.3 %collective-permute-done.8 = bf16[16,128,128]{2,1,0:T(8,128)(2,1)} collective-permute-done((bf16[16,128,128]{2,1,0:T(8,128)(2,1)S(1)}, bf16[16,128,128]{2,1,0:T(8,128)(2,1)}, u32[]{:S(2)}, u32[]{:S(2)}) %collective-permute-start.8) | collective-permute-done | bytes 524320 | tf_op jit(solution)/shard_map/ppermute | solution.py:247
  65.5 1.4 multiply_convert_fusion.1.refs_0_
  67.0 1.1 collective-permute-done.5
  68.1 1.0 fusion.17
  69.1 0.6 collective-permute-start.6
  69.9 5.8 %shard_map.96 = (bf16[8,128,128]{2,1,0:T(8,128)(2,1)S(1)}, bf16[8,128,128]{2,1,0:T(8,128)(2,1)S(1)}, bf16[8,128,128]{2,1,0:T(8,128)(2,1)S(1)}, bf16[8,128,128]{2...) custom-call(s32[2]{0:T(128)S(1)} %pad_add_fusion.starts_ref, ...), custom_call_target="tpu_custom_call" | custom-call | flops 1073741824 | bytes 8388608 | tf_op jit(solution)/shard_map/pallas_call | solution.py:130
  75.7 6.8 %collective-permute-done.6 = bf16[16,128,128]{2,1,0:T(8,128)(2,1)S(1)} collective-permute-done((bf16[16,128,128]{2,1,0:T(8,128)(2,1)}, bf16[16,128,128]{2,1,0:T(8,128)(2,1)S(1)}, u32[]{:S(2)}, u32[]{:S(2)}) %collective-permute-start.6) | collective-permute-done | bytes 524320 | tf_op jit(solution)/shard_map/ppermute | solution.py:247
  82.6 0.4 multiply_convert_fusion.refs_0_
  83.0 1.7 %collective-permute-start.24 = (bf16[8,128,128]{2,1,0:T(8,128)(2,1)S(1)}, bf16[8,128,128]{2,1,0:T(8,128)(2,1)S(1)}, u32[]{:S(2)}, u32[]{:S(2)}) collective-permute-start(bf16[8,128,128]{2,1,0:T(8,128)(2,1)S(1)} %get-tuple-element.70), channel_id=1, source_target_pairs={{0,1},{1,0},{2,3},{3,2},{4,5},{5,4},{6,7},{7,6},{8,9},{9,8},{10,11... | collective-permute-start | bytes 786440 | tf_op jit(solution)/shard_map/ppermute | solution.py:263
  85.1 1.7 %collective-permute-start.21 = (bf16[8,128,128]{2,1,0:T(8,128)(2,1)S(1)}, bf16[8,128,128]{2,1,0:T(8,128)(2,1)S(1)}, u32[]{:S(2)}, u32[]{:S(2)}) collective-permute-start(bf16[8,128,128]{2,1,0:T(8,128)(2,1)S(1)} %get-tuple-element.68), channel_id=1, source_target_pairs={{0,1},{1,0},{2,3},{3,2},{4,5},{5,4},{6,7},{7,6},{8,9},{9,8},{10,11... | collective-permute-start | bytes 786440 | tf_op jit(solution)/shard_map/ppermute | solution.py:263
  87.1 1.7 %collective-permute-start.18 = (bf16[8,128,128]{2,1,0:T(8,128)(2,1)S(1)}, bf16[8,128,128]{2,1,0:T(8,128)(2,1)S(1)}, u32[]{:S(2)}, u32[]{:S(2)}) collective-permute-start(bf16[8,128,128]{2,1,0:T(8,128)(2,1)S(1)} %get-tuple-element.66), channel_id=1, source_target_pairs={{0,1},{1,0},{2,3},{3,2},{4,5},{5,4},{6,7},{7,6},{8,9},{9,8},{10,11... | collective-permute-start | bytes 786440 | tf_op jit(solution)/shard_map/ppermute | solution.py:263
  88.8 4.8 %shard_map.97 = (f32[8,128,128]{2,1,0:T(8,128)S(1)}, f32[8,128,128]{2,1,0:T(8,128)S(1)}, f32[8,128,128]{2,1,0:T(8,128)S(1)}, f32[8,128,128]{2,1,0:T(8,128)S(1)},...) custom-call(s32[2]{0:T(128)S(1)} %pad_add_fusion.starts_ref, s32[256]{0:T(256)S(1)} %reshape.26.place_ref, ...), custom_call_target="tpu_custom_call" | custom-call | flops 1073741824 | bytes 8388608 | tf_op jit(solution)/shard_map/pallas_call | solution.py:130
  93.6 0.4 collective-permute-start.12
  94.1 15.0 %collective-permute-done.21.refs_1_ = bf16[8,128,128]{2,1,0:T(8,128)(2,1)S(1)} collective-permute-done((bf16[8,128,128]{2,1,0:T(8,128)(2,1)S(1)}, bf16[8,128,128]{2,1,0:T(8,128)(2,1)S(1)}, u32[]{:S(2)}, u32[]{:S(2)}) %collective-permute-start.21) | collective-permute-done | bytes 262176 | tf_op jit(solution)/shard_map/ppermute | solution.py:263
  109.1 3.6 %collective-permute-start.25 = (bf16[8,128,128]{2,1,0:T(8,128)(2,1)S(1)}, bf16[8,128,128]{2,1,0:T(8,128)(2,1)S(1)}, u32[]{:S(2)}, u32[]{:S(2)}) collective-permute-start(bf16[8,128,128]{2,1,0:T(8,128)(2,1)S(1)} %shard_map.105), channel_id=1, source_target_pairs={{0,2},{6,4},{1,3},{7,5},{8,10},{14,12},{9,11},{15,13},{16,18},{22,... | collective-permute-start | bytes 786440 | tf_op jit(solution)/shard_map/ppermute | solution.py:269
  112.9 7.5 %collective-permute-done.18.refs_1_ = bf16[8,128,128]{2,1,0:T(8,128)(2,1)S(1)} collective-permute-done((bf16[8,128,128]{2,1,0:T(8,128)(2,1)S(1)}, bf16[8,128,128]{2,1,0:T(8,128)(2,1)S(1)}, u32[]{:S(2)}, u32[]{:S(2)}) %collective-permute-start.18) | collective-permute-done | bytes 262176 | tf_op jit(solution)/shard_map/ppermute | solution.py:263
  120.4 3.6 %collective-permute-start.22 = (bf16[8,128,128]{2,1,0:T(8,128)(2,1)S(1)}, bf16[8,128,128]{2,1,0:T(8,128)(2,1)S(1)}, u32[]{:S(2)}, u32[]{:S(2)}) collective-permute-start(bf16[8,128,128]{2,1,0:T(8,128)(2,1)S(1)} %shard_map.103), channel_id=1, source_target_pairs={{0,2},{6,4},{1,3},{7,5},{8,10},{14,12},{9,11},{15,13},{16,18},{22,... | collective-permute-start | bytes 786440 | tf_op jit(solution)/shard_map/ppermute | solution.py:269
  124.1 1.3 collective-permute-start.19
  125.5 1.3 collective-permute-start.16
  127.2 3.5 %collective-permute-done.22.refs_2_ = bf16[8,128,128]{2,1,0:T(8,128)(2,1)S(1)} collective-permute-done((bf16[8,128,128]{2,1,0:T(8,128)(2,1)S(1)}, bf16[8,128,128]{2,1,0:T(8,128)(2,1)S(1)}, u32[]{:S(2)}, u32[]{:S(2)}) %collective-permute-start.22) | collective-permute-done | bytes 262176 | tf_op jit(solution)/shard_map/ppermute | solution.py:269
  130.7 0.7 collective-permute-start.26
  131.5 4.8 %collective-permute-done.19.refs_2_ = bf16[8,128,128]{2,1,0:T(8,128)(2,1)S(1)} collective-permute-done((bf16[8,128,128]{2,1,0:T(8,128)(2,1)S(1)}, bf16[8,128,128]{2,1,0:T(8,128)(2,1)S(1)}, u32[]{:S(2)}, u32[]{:S(2)}) %collective-permute-start.19) | collective-permute-done | bytes 262176 | tf_op jit(solution)/shard_map/ppermute | solution.py:269
  136.3 0.7 collective-permute-start.23
  137.1 4.8 %collective-permute-done.16.refs_2_ = bf16[8,128,128]{2,1,0:T(8,128)(2,1)S(1)} collective-permute-done((bf16[8,128,128]{2,1,0:T(8,128)(2,1)S(1)}, bf16[8,128,128]{2,1,0:T(8,128)(2,1)S(1)}, u32[]{:S(2)}, u32[]{:S(2)}) %collective-permute-start.16) | collective-permute-done | bytes 262176 | tf_op jit(solution)/shard_map/ppermute | solution.py:269
  141.9 1.3 collective-permute-start.20
  143.3 1.3 collective-permute-start.17
  144.6 10.1 %collective-permute-done.20.refs_1_ = bf16[8,128,128]{2,1,0:T(8,128)(2,1)S(1)} collective-permute-done((bf16[8,128,128]{2,1,0:T(8,128)(2,1)S(1)}, bf16[8,128,128]{2,1,0:T(8,128)(2,1)S(1)}, u32[]{:S(2)}, u32[]{:S(2)}) %collective-permute-start.20) | collective-permute-done | bytes 262176 | tf_op jit(solution)/shard_map/ppermute | solution.py:269
  154.8 2.9 %collective-permute-done.17.refs_0_ = bf16[8,128,128]{2,1,0:T(8,128)(2,1)S(1)} collective-permute-done((bf16[8,128,128]{2,1,0:T(8,128)(2,1)S(1)}, bf16[8,128,128]{2,1,0:T(8,128)(2,1)S(1)}, u32[]{:S(2)}, u32[]{:S(2)}) %collective-permute-start.17) | collective-permute-done | bytes 262176 | tf_op jit(solution)/shard_map/ppermute | solution.py:269
  157.7 1.2 shard_map.107
  (52 shorter events, 3.0 us)
Async XLA Ops:
  0.0 55.7 %copy-start = (f32[8192]{0:T(1024)S(1)}, f32[8192]{0:T(1024)}, u32[]{:S(2)}) copy-start(f32[8192]{0:T(1024)} %param.13) | copy-start | bytes 98308
  2.0 15.9 %collective-permute-start.1 = (bf16[8,128,128]{2,1,0:T(8,128)(2,1)}, bf16[8,128,128]{2,1,0:T(8,128)(2,1)S(1)}, u32[]{:S(2)}, u32[]{:S(2)}) collective-permute-start(bf16[8,128,128]{2,1,0:T(8,128)(2,1)} %shard_map.93), channel_id=1, source_target_pairs={{0,1},{1,0},{2,3},{3,2},{4,5},{5,4},{6,7},{7,6},{8,9},{9,8},{10,11... | collective-permute-start | bytes 786440 | tf_op jit(solution)/shard_map/ppermute | solution.py:200
  7.3 20.3 %collective-permute-start.3 = (bf16[16,128,128]{2,1,0:T(8,128)(2,1)}, bf16[16,128,128]{2,1,0:T(8,128)(2,1)}, u32[]{:S(2)}, u32[]{:S(2)}) collective-permute-start(bf16[16,128,128]{2,1,0:T(8,128)(2,1)} %shard_map.94), channel_id=1, source_target_pairs={{0,1},{1,0},{2,3},{3,2},{4,5},{5,4},{6,7},{7,6},{8,9},{9,8},{10,11... | collective-permute-start | bytes 1572872 | tf_op jit(solution)/shard_map/ppermute | solution.py:201
  17.8 17.2 %collective-permute-start = (bf16[32,128,128]{2,1,0:T(8,128)(2,1)}, bf16[32,128,128]{2,1,0:T(8,128)(2,1)}, u32[]{:S(2)}, u32[]{:S(2)}) collective-permute-start(bf16[32,128,128]{2,1,0:T(8,128)(2,1)} %get-tuple-element.42), channel_id=1, source_target_pairs={{0,8},{8,0},{16,24},{24,16},{1,9},{9,1},{17,25},{25,17},{2,10},{10... | collective-permute-start | bytes 3145736 | tf_op jit(solution)/shard_map/ppermute | solution.py:232
  17.9 9.0 %collective-permute-start.2 = (bf16[8,128,128]{2,1,0:T(8,128)(2,1)S(1)}, bf16[8,128,128]{2,1,0:T(8,128)(2,1)S(1)}, u32[]{:S(2)}, u32[]{:S(2)}) collective-permute-start(bf16[8,128,128]{2,1,0:T(8,128)(2,1)S(1)} %collective-permute-done.1.refs_0_), channel_id=1, source_target_pairs={{0,2},{2,0},{4,6},{6,4},{1,3},{3,1},{5,7},{7,5},{8,10},{10,8},{12,... | collective-permute-start | bytes 786440 | tf_op jit(solution)/shard_map/ppermute | solution.py:203
  26.9 0.7 copy-start.1
  27.6 1.0 copy-start.2
  34.9 18.8 %copy-start.5 = (s32[128,64]{0,1:T(8,128)S(1)}, s32[128,64]{0,1:T(8,128)}, u32[]{:S(2)}) copy-start(s32[128,64]{0,1:T(8,128)} %param.14) | copy-start | bytes 98308
  34.9 4.2 %collective-permute-start.4 = (bf16[32,128,128]{2,1,0:T(8,128)(2,1)S(1)}, bf16[32,128,128]{2,1,0:T(8,128)(2,1)S(1)}, u32[]{:S(2)}, u32[]{:S(2)}) collective-permute-start(bf16[32,128,128]{2,1,0:T(8,128)(2,1)S(1)} %get-tuple-element.46), channel_id=1, source_target_pairs={{0,8},{8,0},{16,24},{24,16},{1,9},{9,1},{17,25},{25,17},{2,10},{10... | collective-permute-start | bytes 3145736 | tf_op jit(solution)/shard_map/ppermute | solution.py:232
  37.4 30.7 %copy-start.4 = (f32[16,128,128]{2,1,0:T(8,128)S(1)}, f32[16,128,128]{2,1,0:T(8,128)}, u32[]{:S(2)}) copy-start(f32[16,128,128]{2,1,0:T(8,128)} %get-tuple-element.44) | copy-start | bytes 3145732
  37.4 14.3 %collective-permute-start.7 = (bf16[16,128,128]{2,1,0:T(8,128)(2,1)S(1)}, bf16[16,128,128]{2,1,0:T(8,128)(2,1)S(1)}, u32[]{:S(2)}, u32[]{:S(2)}) collective-permute-start(bf16[16,128,128]{2,1,0:T(8,128)(2,1)S(1)} %get-tuple-element.52), channel_id=1, source_target_pairs={{0,1},{1,0},{2,3},{3,2},{4,5},{5,4},{6,7},{7,6},{8,9},{9,8},{10,11... | collective-permute-start | bytes 1572872 | tf_op jit(solution)/shard_map/ppermute | solution.py:239
  51.9 13.6 %collective-permute-start.8 = (bf16[16,128,128]{2,1,0:T(8,128)(2,1)S(1)}, bf16[16,128,128]{2,1,0:T(8,128)(2,1)}, u32[]{:S(2)}, u32[]{:S(2)}) collective-permute-start(bf16[16,128,128]{2,1,0:T(8,128)(2,1)S(1)} %get-tuple-element.54), channel_id=1, source_target_pairs={{0,16},{8,24},{16,0},{24,8},{1,17},{9,25},{17,1},{25,9},{2,18},{10... | collective-permute-start | bytes 1572872 | tf_op jit(solution)/shard_map/ppermute | solution.py:247
  53.6 3.6 %collective-permute-start.9 = (bf16[128,16]{0,1:T(8,128)(2,1)S(1)}, bf16[128,16]{0,1:T(8,128)(2,1)S(1)}, u32[]{:S(2)}, u32[]{:S(2)}) collective-permute-start(bf16[128,16]{0,1:T(8,128)(2,1)S(1)} %get-tuple-element.80), channel_id=1, source_target_pairs={{0,1},{1,0},{2,3},{3,2},{4,5},{5,4},{6,7},{7,6},{8,9},{9,8},{10,11... | collective-permute-start | bytes 12296 | tf_op jit(solution)/shard_map/ppermute | solution.py:207
  55.2 12.9 %collective-permute-start.5 = (bf16[16,128,128]{2,1,0:T(8,128)(2,1)S(1)}, bf16[16,128,128]{2,1,0:T(8,128)(2,1)S(1)}, u32[]{:S(2)}, u32[]{:S(2)}) collective-permute-start(bf16[16,128,128]{2,1,0:T(8,128)(2,1)S(1)} %get-tuple-element.48), channel_id=1, source_target_pairs={{0,1},{1,0},{2,3},{3,2},{4,5},{5,4},{6,7},{7,6},{8,9},{9,8},{10,11... | collective-permute-start | bytes 1572872 | tf_op jit(solution)/shard_map/ppermute | solution.py:242
  66.9 3.0 %collective-permute-start.10 = (bf16[16,128,128]{2,1,0:T(8,128)(2,1)S(1)}, bf16[16,128,128]{2,1,0:T(8,128)(2,1)S(1)}, u32[]{:S(2)}, u32[]{:S(2)}) collective-permute-start(bf16[16,128,128]{2,1,0:T(8,128)(2,1)S(1)} %multiply_convert_fusion.1.refs_0_), channel_id=1, source_target_pairs={{0,8},{8,0},{16,24},{24,16},{1,9},{9,1},{17,25},{25,17},{2,10},{10... | collective-permute-start | bytes 1572872 | tf_op jit(solution)/shard_map/ppermute | solution.py:253
  69.1 13.4 %collective-permute-start.6 = (bf16[16,128,128]{2,1,0:T(8,128)(2,1)}, bf16[16,128,128]{2,1,0:T(8,128)(2,1)S(1)}, u32[]{:S(2)}, u32[]{:S(2)}) collective-permute-start(bf16[16,128,128]{2,1,0:T(8,128)(2,1)} %get-tuple-element.50), channel_id=1, source_target_pairs={{0,16},{8,24},{16,0},{24,8},{1,17},{9,25},{17,1},{25,9},{2,18},{10... | collective-permute-start | bytes 1572872 | tf_op jit(solution)/shard_map/ppermute | solution.py:247
  82.9 4.2 %collective-permute-start.11 = (bf16[16,128,128]{2,1,0:T(8,128)(2,1)S(1)}, bf16[16,128,128]{2,1,0:T(8,128)(2,1)S(1)}, u32[]{:S(2)}, u32[]{:S(2)}) collective-permute-start(bf16[16,128,128]{2,1,0:T(8,128)(2,1)S(1)} %multiply_convert_fusion.refs_0_), channel_id=1, source_target_pairs={{0,8},{8,0},{16,24},{24,16},{1,9},{9,1},{17,25},{25,17},{2,10},{10... | collective-permute-start | bytes 1572872 | tf_op jit(solution)/shard_map/ppermute | solution.py:253
  83.0 10.6 %collective-permute-start.24 = (bf16[8,128,128]{2,1,0:T(8,128)(2,1)S(1)}, bf16[8,128,128]{2,1,0:T(8,128)(2,1)S(1)}, u32[]{:S(2)}, u32[]{:S(2)}) collective-permute-start(bf16[8,128,128]{2,1,0:T(8,128)(2,1)S(1)} %get-tuple-element.70), channel_id=1, source_target_pairs={{0,1},{1,0},{2,3},{3,2},{4,5},{5,4},{6,7},{7,6},{8,9},{9,8},{10,11... | collective-permute-start | bytes 786440 | tf_op jit(solution)/shard_map/ppermute | solution.py:263
  84.8 40.7 %collective-permute-start.13 = (bf16[16,128,128]{2,1,0:T(8,128)(2,1)S(1)}, bf16[16,128,128]{2,1,0:T(8,128)(2,1)S(1)}, u32[]{:S(2)}, u32[]{:S(2)}) collective-permute-start(bf16[16,128,128]{2,1,0:T(8,128)(2,1)S(1)} %get-tuple-element.62), channel_id=1, source_target_pairs={{0,1},{1,0},{2,3},{3,2},{4,5},{5,4},{6,7},{7,6},{8,9},{9,8},{10,11... | collective-permute-start | bytes 1572872 | tf_op jit(solution)/shard_map/ppermute | solution.py:263
  85.1 24.0 %collective-permute-start.21 = (bf16[8,128,128]{2,1,0:T(8,128)(2,1)S(1)}, bf16[8,128,128]{2,1,0:T(8,128)(2,1)S(1)}, u32[]{:S(2)}, u32[]{:S(2)}) collective-permute-start(bf16[8,128,128]{2,1,0:T(8,128)(2,1)S(1)} %get-tuple-element.68), channel_id=1, source_target_pairs={{0,1},{1,0},{2,3},{3,2},{4,5},{5,4},{6,7},{7,6},{8,9},{9,8},{10,11... | collective-permute-start | bytes 786440 | tf_op jit(solution)/shard_map/ppermute | solution.py:263
  86.8 37.3 %collective-permute-start.15 = (bf16[8,128,128]{2,1,0:T(8,128)(2,1)S(1)}, bf16[8,128,128]{2,1,0:T(8,128)(2,1)S(1)}, u32[]{:S(2)}, u32[]{:S(2)}) collective-permute-start(bf16[8,128,128]{2,1,0:T(8,128)(2,1)S(1)} %get-tuple-element.64), channel_id=1, source_target_pairs={{0,1},{1,0},{2,3},{3,2},{4,5},{5,4},{6,7},{7,6},{8,9},{9,8},{10,11... | collective-permute-start | bytes 786440 | tf_op jit(solution)/shard_map/ppermute | solution.py:263
  87.1 70.6 %copy-start.3 = (f32[2048]{0:T(1024)S(1)}, f32[2048]{0:T(1024)}, u32[]{:S(2)}) copy-start(f32[2048]{0:T(1024)} %param.17) | copy-start | bytes 24580
  87.1 33.2 %collective-permute-start.18 = (bf16[8,128,128]{2,1,0:T(8,128)(2,1)S(1)}, bf16[8,128,128]{2,1,0:T(8,128)(2,1)S(1)}, u32[]{:S(2)}, u32[]{:S(2)}) collective-permute-start(bf16[8,128,128]{2,1,0:T(8,128)(2,1)S(1)} %get-tuple-element.66), channel_id=1, source_target_pairs={{0,1},{1,0},{2,3},{3,2},{4,5},{5,4},{6,7},{7,6},{8,9},{9,8},{10,11... | collective-permute-start | bytes 786440 | tf_op jit(solution)/shard_map/ppermute | solution.py:263
  93.6 49.7 %collective-permute-start.12 = (bf16[16,128,128]{2,1,0:T(8,128)(2,1)S(1)}, bf16[16,128,128]{2,1,0:T(8,128)(2,1)S(1)}, u32[]{:S(2)}, u32[]{:S(2)}) collective-permute-start(bf16[16,128,128]{2,1,0:T(8,128)(2,1)S(1)} %get-tuple-element.60), channel_id=1, source_target_pairs={{0,1},{1,0},{2,3},{3,2},{4,5},{5,4},{6,7},{7,6},{8,9},{9,8},{10,11... | collective-permute-start | bytes 1572872 | tf_op jit(solution)/shard_map/ppermute | solution.py:263
  109.1 17.8 %collective-permute-start.25 = (bf16[8,128,128]{2,1,0:T(8,128)(2,1)S(1)}, bf16[8,128,128]{2,1,0:T(8,128)(2,1)S(1)}, u32[]{:S(2)}, u32[]{:S(2)}) collective-permute-start(bf16[8,128,128]{2,1,0:T(8,128)(2,1)S(1)} %shard_map.105), channel_id=1, source_target_pairs={{0,2},{6,4},{1,3},{7,5},{8,10},{14,12},{9,11},{15,13},{16,18},{22,... | collective-permute-start | bytes 786440 | tf_op jit(solution)/shard_map/ppermute | solution.py:269
  120.4 10.3 %collective-permute-start.22 = (bf16[8,128,128]{2,1,0:T(8,128)(2,1)S(1)}, bf16[8,128,128]{2,1,0:T(8,128)(2,1)S(1)}, u32[]{:S(2)}, u32[]{:S(2)}) collective-permute-start(bf16[8,128,128]{2,1,0:T(8,128)(2,1)S(1)} %shard_map.103), channel_id=1, source_target_pairs={{0,2},{6,4},{1,3},{7,5},{8,10},{14,12},{9,11},{15,13},{16,18},{22,... | collective-permute-start | bytes 786440 | tf_op jit(solution)/shard_map/ppermute | solution.py:269
  124.1 12.2 %collective-permute-start.19 = (bf16[8,128,128]{2,1,0:T(8,128)(2,1)S(1)}, bf16[8,128,128]{2,1,0:T(8,128)(2,1)S(1)}, u32[]{:S(2)}, u32[]{:S(2)}) collective-permute-start(bf16[8,128,128]{2,1,0:T(8,128)(2,1)S(1)} %shard_map.101), channel_id=1, source_target_pairs={{0,2},{6,4},{1,3},{7,5},{8,10},{14,12},{9,11},{15,13},{16,18},{22,... | collective-permute-start | bytes 786440 | tf_op jit(solution)/shard_map/ppermute | solution.py:269
  125.5 16.4 %collective-permute-start.16 = (bf16[8,128,128]{2,1,0:T(8,128)(2,1)S(1)}, bf16[8,128,128]{2,1,0:T(8,128)(2,1)S(1)}, u32[]{:S(2)}, u32[]{:S(2)}) collective-permute-start(bf16[8,128,128]{2,1,0:T(8,128)(2,1)S(1)} %shard_map.99), channel_id=1, source_target_pairs={{0,2},{6,4},{1,3},{7,5},{8,10},{14,12},{9,11},{15,13},{16,18},{22,... | collective-permute-start | bytes 786440 | tf_op jit(solution)/shard_map/ppermute | solution.py:269
  127.0 30.7 %collective-permute-start.14 = (bf16[16,128,128]{2,1,0:T(8,128)(2,1)S(1)}, bf16[16,128,128]{2,1,0:T(8,128)(2,1)S(1)}, u32[]{:S(2)}, u32[]{:S(2)}) collective-permute-start(bf16[16,128,128]{2,1,0:T(8,128)(2,1)S(1)} %shard_map.98), channel_id=1, source_target_pairs={{0,2},{2,0},{4,6},{6,4},{1,3},{3,1},{5,7},{7,5},{8,10},{10,8},{12,... | collective-permute-start | bytes 1572872 | tf_op jit(solution)/shard_map/ppermute | solution.py:269
  130.7 13.9 %collective-permute-start.26 = (bf16[8,128,128]{2,1,0:T(8,128)(2,1)S(1)}, bf16[8,128,128]{2,1,0:T(8,128)(2,1)S(1)}, u32[]{:S(2)}, u32[]{:S(2)}) collective-permute-start(bf16[8,128,128]{2,1,0:T(8,128)(2,1)S(1)} %shard_map.106), channel_id=1, source_target_pairs={{2,4},{4,2},{3,5},{5,3},{10,12},{12,10},{11,13},{13,11},{18,20},{2... | collective-permute-start | bytes 786440 | tf_op jit(solution)/shard_map/ppermute | solution.py:269
  136.3 8.3 %collective-permute-start.23 = (bf16[8,128,128]{2,1,0:T(8,128)(2,1)S(1)}, bf16[8,128,128]{2,1,0:T(8,128)(2,1)S(1)}, u32[]{:S(2)}, u32[]{:S(2)}) collective-permute-start(bf16[8,128,128]{2,1,0:T(8,128)(2,1)S(1)} %shard_map.104), channel_id=1, source_target_pairs={{2,4},{4,2},{3,5},{5,3},{10,12},{12,10},{11,13},{13,11},{18,20},{2... | collective-permute-start | bytes 786440 | tf_op jit(solution)/shard_map/ppermute | solution.py:269
  141.9 12.9 %collective-permute-start.20 = (bf16[8,128,128]{2,1,0:T(8,128)(2,1)S(1)}, bf16[8,128,128]{2,1,0:T(8,128)(2,1)S(1)}, u32[]{:S(2)}, u32[]{:S(2)}) collective-permute-start(bf16[8,128,128]{2,1,0:T(8,128)(2,1)S(1)} %shard_map.102), channel_id=1, source_target_pairs={{2,6},{4,0},{3,7},{5,1},{10,14},{12,8},{11,15},{13,9},{18,22},{20,... | collective-permute-start | bytes 786440 | tf_op jit(solution)/shard_map/ppermute | solution.py:269
  143.3 14.4 %collective-permute-start.17 = (bf16[8,128,128]{2,1,0:T(8,128)(2,1)S(1)}, bf16[8,128,128]{2,1,0:T(8,128)(2,1)S(1)}, u32[]{:S(2)}, u32[]{:S(2)}) collective-permute-start(bf16[8,128,128]{2,1,0:T(8,128)(2,1)S(1)} %shard_map.100), channel_id=1, source_target_pairs={{2,6},{4,0},{3,7},{5,1},{10,14},{12,8},{11,15},{13,9},{18,22},{20,... | collective-permute-start | bytes 786440 | tf_op jit(solution)/shard_map/ppermute | solution.py:269

commit v4 on v3

--- a/solution.py
+++ b/solution.py
@@ -9,6 +9,7 @@
 
 
 UNROLL = 4
+GROUPS = 4
 VMEM_LIMIT = 8 * 1024 * 1024
 
 in_vmem = functools.partial(pltpu.with_memory_space_constraint, memory_space=pltpu.VMEM)
@@ -53,20 +54,25 @@
     lax.fori_loop(0, acc.shape[0], body, 0, unroll=4)
 
 
-def add_products(acc, x_ref, w_ref, place_ref, start, first, count):
+def add_row(acc, x, w_ref, tables, row):
+    scalars, cols_ref = tables
     _, entries, block, _ = w_ref.shape
-
+    group = acc.shape[0] // GROUPS
+    for k in range(0, entries, 2):
+        pair = jnp.concatenate([w_ref[row, k], w_ref[row, k + 1]], axis=1)
+        product = jnp.dot(x, pair, preferred_element_type=jnp.float32)
+        for half in range(2):
+            col = cols_ref[k + half, scalars[0] + row] - scalars[1]
+            which = sum((col >= i * group).astype(jnp.int32) for i in range(1, GROUPS))
+            to = col + scalars[2 + which]
+            acc[to] = acc[to] + product[:, half * block:(half + 1) * block]
+
+
+def add_products(acc, x_ref, w_ref, tables, start, first, count):
     def advance(step, carry):
         for i in range(UNROLL):
             at = first + step * UNROLL + i
-            row = start + at
-            x = x_ref[at]
-            for k in range(0, entries, 2):
-                pair = jnp.concatenate([w_ref[row, k], w_ref[row, k + 1]], axis=1)
-                product = jnp.dot(x, pair, preferred_element_type=jnp.float32)
-                for half in range(2):
-                    to = place_ref[row * entries + k + half]
-                    acc[to] = acc[to] + product[:, half * block:(half + 1) * block]
+            add_row(acc, x_ref[at], w_ref, tables, start + at)
         return carry
 
     lax.fori_loop(0, count // UNROLL, advance, 0)
@@ -84,62 +90,121 @@
         start += out.shape[0]
 
 
-def fold_kernel(parts, load, starts_ref, place_ref, *refs):
+def row_copies(w_ref, held_ref, sems, ranges):
+    copies = []
+    for start, count in ranges:
+        for first in range(0, count, UNROLL):
+            rows = pl.ds(start + first, UNROLL)
+            copies.append(pltpu.make_async_copy(w_ref.at[rows], held_ref.at[rows], sems.at[len(copies)]))
+    return copies
+
+
+def fold_kernel(parts, load, scalars, cols_ref, *refs):
     x_refs, w_ref, refs = refs[:parts], refs[parts], refs[parts + 1:]
+    tables = scalars, cols_ref
+    starts = [scalars[2 + GROUPS + i] for i in range(parts)]
     copies = []
     if load:
         *outs, held_ref, acc, sems = refs
-        for part, x_ref in enumerate(x_refs):
-            for first in range(0, x_ref.shape[0], UNROLL):
-                rows = pl.ds(starts_ref[part] + first, UNROLL)
-                copies.append(pltpu.make_async_copy(w_ref.at[rows], held_ref.at[rows], sems.at[len(copies)]))
+        copies = row_copies(w_ref, held_ref, sems, [(at, x.shape[0]) for at, x in zip(starts, x_refs)])
         w_ref = held_ref
     else:
         *outs, acc = refs
     for copy in copies:
         copy.start()
     clear(acc)
-    for part, x_ref in enumerate(x_refs):
+    for start, x_ref in zip(starts, x_refs):
         if load:
             for first in range(0, x_ref.shape[0], UNROLL):
                 copies.pop(0).wait()
-                add_products(acc, x_ref, w_ref, place_ref, starts_ref[part], first, UNROLL)
+                add_products(acc, x_ref, w_ref, tables, start, first, UNROLL)
         else:
-            add_products(acc, x_ref, w_ref, place_ref, starts_ref[part], 0, x_ref.shape[0])
+            add_products(acc, x_ref, w_ref, tables, start, 0, x_ref.shape[0])
     write_out(acc, outs)
 
 
-def fold(xs, weights, places, starts, segments, load=False, keep=False):
-    rows_in, entries, block, _ = weights.shape
-    rows = xs[0].shape[1]
-    total = sum(count for count, _ in segments)
+def own_fold_kernel(scalars, cols_ref, acts_ref, live_ref, w_ref, *refs):
+    *outs, held_ref, acc, x_ref, mask_ref, sems = refs
+    blocks = w_ref.shape[0]
+    width = x_ref.shape[1]
+    block = width // blocks
+    count = blocks // UNROLL
+    half = scalars[2 + GROUPS]
+    lanes = pl.ds(pl.multiple_of(half * width, width), width)
+    inputs = [
+        pltpu.make_async_copy(live_ref.at[pl.ds(half * blocks, blocks)], mask_ref, sems.at[count]),
+        pltpu.make_async_copy(acts_ref.at[:, lanes], x_ref, sems.at[count + 1]),
+    ]
+    copies = row_copies(w_ref, held_ref, sems, [(0, blocks)])
+    for copy in inputs + copies:
+        copy.start()
+    clear(acc)
+    for copy in inputs:
+        copy.wait()
+    live = mask_ref[...].astype(jnp.float32).T
+    for i, copy in enumerate(copies):
+        copy.wait()
+        for at in range(i * UNROLL, (i + 1) * UNROLL):
+            x = x_ref[:, at * block:(at + 1) * block].astype(jnp.float32) * live[:, at:at + 1]
+            add_row(acc, x.astype(jnp.bfloat16), held_ref, (scalars, cols_ref), at)
+    write_out(acc, outs)
+
+
+def fold_parts(rows, weights, segments):
+    block = weights.shape[-1]
+    outs = [pltpu.VMEM((count, rows, block), kind) for count, kind in segments]
+    acc = pltpu.VMEM((sum(count for count, _ in segments), rows, block), jnp.float32)
+    held = pltpu.VMEM(weights.shape, weights.dtype)
+    cost = pl.CostEstimate(flops=2 * rows * weights.size, bytes_accessed=2 * weights.size, transcendentals=0)
+    return outs, acc, held, weights.shape[0] // UNROLL, cost
+
+
+def own_fold(acts, act_mask, half, weights, cols, scalars, segments):
+    rows, width = acts.shape
+    outs, acc, held, count, cost = fold_parts(rows, weights, segments)
     smem = pl.BlockSpec(memory_space=pltpu.SMEM)
     vmem = pl.BlockSpec(memory_space=pltpu.VMEM)
     hbm = pl.BlockSpec(memory_space=pltpu.HBM)
-    out_shape = [pltpu.VMEM((count, rows, block), kind) for count, kind in segments]
-    scratch = [pltpu.VMEM((total, rows, block), jnp.float32)]
-    held = pltpu.VMEM(weights.shape, weights.dtype)
+    return pl.pallas_call(
+        own_fold_kernel,
+        out_shape=outs,
+        in_specs=[smem, smem, hbm, hbm, hbm],
+        out_specs=[vmem] * len(outs),
+        scratch_shapes=[
+            held,
+            acc,
+            pltpu.VMEM((rows, width // 2), acts.dtype),
+            pltpu.VMEM((weights.shape[0], rows), act_mask.dtype),
+            pltpu.SemaphoreType.DMA((count + 2,)),
+        ],
+        compiler_params=pltpu.CompilerParams(vmem_limit_bytes=2 * VMEM_LIMIT + 2 * 1024 * 1024),
+        cost_estimate=cost,
+    )(jnp.stack([*scalars, half]), cols.T, in_hbm(acts), in_hbm(act_mask.T), in_hbm(weights))
+
+
+def fold(xs, weights, cols, scalars, starts, segments, load=False, keep=False):
+    outs, acc, held, count, cost = fold_parts(xs[0].shape[1], weights, segments)
+    scratch = [acc]
+    smem = pl.BlockSpec(memory_space=pltpu.SMEM)
+    vmem = pl.BlockSpec(memory_space=pltpu.VMEM)
+    hbm = pl.BlockSpec(memory_space=pltpu.HBM)
     limit = VMEM_LIMIT
     if load:
-        scratch.append(pltpu.SemaphoreType.DMA((rows_in // UNROLL,)))
+        scratch.append(pltpu.SemaphoreType.DMA((count,)))
         if keep:
-            out_shape.append(held)
+            outs.append(held)
         else:
             scratch.insert(0, held)
             limit += weights.size * weights.dtype.itemsize
     return pl.pallas_call(
         functools.partial(fold_kernel, len(xs), load),
-        out_shape=out_shape,
+        out_shape=outs,
         in_specs=[smem, smem] + [vmem] * len(xs) + [hbm if load else vmem],
-        out_specs=[vmem] * len(out_shape),
+        out_specs=[vmem] * len(outs),
         scratch_shapes=scratch,
         compiler_params=pltpu.CompilerParams(vmem_limit_bytes=limit),
-        cost_estimate=pl.CostEstimate(
-            flops=2 * rows * rows_in * entries * block * block,
-            bytes_accessed=2 * weights.size,
-            transcendentals=0,
-        ),
-    )(jnp.stack(starts), places.reshape(-1), *map(in_vmem, xs), (in_hbm if load else in_vmem)(weights))
+        cost_estimate=cost,
+    )(jnp.stack([*scalars, *starts]), cols.T, *map(in_vmem, xs), (in_hbm if load else in_vmem)(weights))
 
 
 def add_kernel(*refs):
@@ -193,13 +258,11 @@
     over_depth = functools.partial(lax.ppermute, axis_name="depth", perm=[(0, 1), (1, 0)])
     over_core = functools.partial(lax.ppermute, axis_name="row", perm=[(i, i ^ 1) for i in range(size_row)])
     over_x = functools.partial(lax.ppermute, axis_name="row", perm=[(i, i ^ 2) for i in range(size_row)])
-    zero = jnp.int32(0)
 
     side = lax.rem(c, 2)
     eighth, fourth = half_in // 4, half_in // 2
     part_x = over_depth(masked(acts, act_mask, (1 - d) * 4 + side, eighth))
     rest_x = over_depth(masked(acts, act_mask, (1 - d) * 2 + 1, fourth))
-    own_x = masked(acts, act_mask, d * 2, half_in, steps=2)
     swapped_x = lax.ppermute(part_x, "col", [(i, i ^ 1) for i in range(size_col)])
     other_x = [part_x, swapped_x, rest_x]
     other_starts = [side * eighth, (1 - side) * eighth, jnp.int32(fourth)]
@@ -211,21 +274,18 @@
         bias1.reshape(col_blocks, 1, block), d * half_mid + core * quarter, quarter, 0
     )
 
-    to1 = lax.dynamic_slice_in_dim(cols1, d * half_in, half_in, 0) - c * col_blocks
-    to_depth = to1 // half_mid
-    to_core = (to1 // quarter) % 2
-    same_core = 1 - (to_core ^ core)
-    same_depth = 1 - (to_depth ^ d)
-    place1 = same_core * half_mid + same_depth * quarter + to1 % quarter
-
-    to2 = lax.dynamic_slice_in_dim(cols2, d * half_mid, half_mid, 0) - r * row_blocks
+    def shifts(places, size):
+        return [(place - i) * size for i, place in enumerate(places)]
+
+    places1 = [(1 - (which ^ core)) * 2 + 1 - (depth ^ d) for depth in range(2) for which in range(2)]
+    scalars1 = [d * half_in, c * col_blocks, *shifts(places1, quarter)]
+
     share = row_blocks // size_col
-    chunk = to2 // share
     far = jnp.where(c < size_col // 2, size_col - 1, 0)
-    slot = jnp.where(chunk == far, 0, jnp.where(chunk == (far ^ 1), 1, jnp.where(chunk == (c ^ 1), 2, 3)))
-    place2 = slot * share + to2 % share
-    own_x, place1, place2 = lax.optimization_barrier((own_x, place1, place2))
-
+    places2 = [
+        jnp.where(i == far, 0, jnp.where(i == (far ^ 1), 1, jnp.where(i == (c ^ 1), 2, 3))) for i in range(size_col)
+    ]
+    scalars2 = [d * half_mid, r * row_blocks, *shifts(places2, share)]
     segments = [(half_mid, bf16), (quarter, f32), (quarter, f32)]
 
     def core_sums(low, send, keep):
@@ -234,10 +294,10 @@
             ((send + low[:quarter].astype(f32)).astype(bf16), keep + low[quarter:].astype(f32))
         )
 
-    sums = fold([own_x], w1, place1, [zero], segments, load=True)
+    sums = own_fold(acts, act_mask, d, w1, cols1, scalars1, segments)
     send_own, keep_own = core_sums(*sums)
     got_other = over_depth(send_own)
-    sums = fold(other_x, w1, place1, other_starts, segments, load=True)
+    sums = fold(other_x, w1, cols1, scalars1, other_starts, segments, load=True)
     send_other, keep_other = core_sums(*sums)
     got_own = over_depth(send_other)
 
@@ -257,13 +317,13 @@
     hidden_other = hidden(*sums_other, mask_other)
     starts = [core * quarter, (1 - core) * quarter]
     cuts = [share // 2] * 4 + [share] * 2
-    *for_other, w2 = fold(hidden_other, w2, place2, starts, [(n, bf16) for n in cuts], load=True, keep=True)
+    *for_other, w2 = fold(hidden_other, w2, cols2, scalars2, starts, [(n, bf16) for n in cuts], load=True, keep=True)
     got = []
     for part in for_other:
         got.append(over_depth(part))
     part_own, low_own, w2 = lax.optimization_barrier((*sums_own, w2))
     hidden_own = hidden(part_own, low_own, mask_own)
-    mine = fold(hidden_own, w2, place2, starts, [(n, f32) for n in cuts])
+    mine = fold(hidden_own, w2, cols2, scalars2, starts, [(n, f32) for n in cuts])
 
     def over_col(parts, perm):
         return lax.ppermute(add(parts), "col", perm)

time: 159 us -> 155 us (0.975)
    pallas_call x0 -> x1, Pallas kernels: none -> 7.69 us  [own_fold(): pl.pallas_call(own_fold_kernel, out_shape=outs, in_specs=[smem, smem, hbm...]
    pallas_call x4 -> x3, Pallas kernels: 23.5 us -> 18.1 us  [fold(): pl.pallas_call(functools.partial(fold_kernel, len(xs), load), out_shape=o...]
    pallas_call x3 -> x2, Pallas kernels: 6.33 us -> 3.51 us  [masked(): pl.pallas_call(mask_kernel, out_shape=pltpu.VMEM((blocks, rows, block), j...]
  transfers between devices with their start and end apart: 27 -> 27, of which waited for: 13 -> 13; matrix products, arithmetic and copies ran while one was open for 5% -> 3% of each run, Pallas kernels for 18% -> 18%
where the time goes in v4:
time: 155 us
  waiting for transfers between devices  84.7 us (55%)
  starting transfers between devices  31.3 us (20%)
  Pallas kernels  31.2 us (20%)
  other arithmetic  6.29 us (4%)
    ppermute x9, waiting for transfers between devices, over_col(): return lax.ppermute(add(parts), 'col', perm)  26.3 us
    ppermute x6, waiting for transfers between devices, exchange_plan(): got.append(over_depth(part))  22 us
    pallas_call x3, Pallas kernels, fold(): pl.pallas_call(functools.partial(fold_kernel, len(xs), load), out_shape=o...  18.1 us
    ppermute x2, waiting for transfers between devices, x_sums(): return (part, over_x(low))  14.1 us
    ppermute x9, starting transfers between devices, over_col(): return lax.ppermute(add(parts), 'col', perm)  13.9 us
    ppermute x1, waiting for transfers between devices, exchange_plan(): got_other = over_depth(send_own)  11.7 us
    pallas_call x1, Pallas kernels, own_fold(): pl.pallas_call(own_fold_kernel, out_shape=outs, in_specs=[smem, smem, hbm...  7.69 us
    ppermute x1, waiting for transfers between devices, exchange_plan(): lax.ppermute(part_x, 'col', [(i, i ^ 1) for i in range(size_col)])  6.91 us
  transfers between devices with their start and end apart: 27, of which 13 were waited for; matrix products, arithmetic and copies ran while one was open for 3% of the time, Pallas kernels for 18%

profile of v4, /device:TPU:0, one launch (start us, length us, event | category | flops | bytes accessed | tf_op | source)
XLA Modules:
  0.0 154.9 jit_solution(2751852904604156812)
XLA Ops:
  0.0 2.0 %shard_map.92 = bf16[8,128,128]{2,1,0:T(8,128)(2,1)} custom-call(s32[1]{0:T(128)} %bitcast.19.half_ref, bf16[128,8192]{1,0:T(8,128)(2,1)} %acts_ref.5, s32[64,128]{1,0:T(8,128)} %bitcast.35), custom_call_target="tpu_custom_call" | custom-call | flops 1024 | bytes 524288 | tf_op jit(solution)/shard_map/pallas_call | solution.py:31
  2.0 3.0 %collective-permute-start.1 = (bf16[8,128,128]{2,1,0:T(8,128)(2,1)}, bf16[8,128,128]{2,1,0:T(8,128)(2,1)S(1)}, u32[]{:S(2)}, u32[]{:S(2)}) collective-permute-start(bf16[8,128,128]{2,1,0:T(8,128)(2,1)} %shard_map.92), channel_id=1, source_target_pairs={{0,1},{1,0},{2,3},{3,2},{4,5},{5,4},{6,7},{7,6},{8,9},{9,8},{10,11... | collective-permute-start | bytes 786440 | tf_op jit(solution)/shard_map/ppermute | solution.py:264
  5.0 1.5 shard_map.93
  6.7 0.7 copy-done.1
  7.4 7.7 %shard_map.91 = (bf16[32,128,128]{2,1,0:T(8,128)(2,1)}, f32[16,128,128]{2,1,0:T(8,128)S(1)}, f32[16,128,128]{2,1,0:T(8,128)S(1)}) custom-call(s32[7]{0:T(128)S(1)} %stack.88.scalars, s32[8,64]{1,0:T(8,128)S(1)} %bitcast.30, bf16[128,8192]{1,0:T(8,128)(2,1)} %acts_ref.5, s32[64,128]{1,0:T(8,128)} %bitcast.37, bf16[32,8,128,128]{3,2,1,0:T(8,128)(2,1)} %refs_3_.1), custom_call_target="tpu_custom_call" | custom-call | flops 1073741824 | bytes 8388608 | tf_op jit(solution)/shard_map/pallas_call | solution.py:168
  15.2 2.3 %collective-permute-start.2 = (bf16[8,128,128]{2,1,0:T(8,128)(2,1)S(1)}, bf16[8,128,128]{2,1,0:T(8,128)(2,1)}, u32[]{:S(2)}, u32[]{:S(2)}) collective-permute-start(bf16[8,128,128]{2,1,0:T(8,128)(2,1)S(1)} %collective-permute-done.1.refs_0_), channel_id=1, source_target_pairs={{0,2},{2,0},{4,6},{6,4},{1,3},{3,1},{5,7},{7,5},{8,10},{10,8},{12,... | collective-permute-start | bytes 786440 | tf_op jit(solution)/shard_map/ppermute | solution.py:266
  17.5 6.9 %collective-permute-done.2.refs_1_ = bf16[8,128,128]{2,1,0:T(8,128)(2,1)} collective-permute-done((bf16[8,128,128]{2,1,0:T(8,128)(2,1)S(1)}, bf16[8,128,128]{2,1,0:T(8,128)(2,1)}, u32[]{:S(2)}, u32[]{:S(2)}) %collective-permute-start.2) | collective-permute-done | bytes 262176 | tf_op jit(solution)/shard_map/ppermute | solution.py:266
  24.4 6.6 %shard_map.94 = (bf16[32,128,128]{2,1,0:T(8,128)(2,1)S(1)}, f32[16,128,128]{2,1,0:T(8,128)S(1)}, f32[16,128,128]{2,1,0:T(8,128)S(1)}) custom-call(s32[9]{0:T(128)S(1)} %stack.91.scalars, s32[8,64]{1,0:T(8,128)S(1)} %bitcast.31, bf16[8,128,128]{2,1,0:T(8,128)(2,1)S(1)} %collective-permute-done.1.refs_0_, bf16[8,128,128]{2,1,0:T(8,128)(2,1)} %collective-permute-done.2.refs_1_, ...), custom_call_target="tpu_custom_call" | custom-call | flops 1073741824 | bytes 8388608 | tf_op jit(solution)/shard_map/pallas_call | solution.py:199
  31.1 2.5 %convert_add_fusion.3 = (f32[16,128,128]{2,1,0:T(8,128)}, bf16[16,128,128]{2,1,0:T(8,128)(2,1)S(1)}) fusion(f32[16,128,128]{2,1,0:T(8,128)S(1)} %get-tuple-element.37, bf16[32,128,128]{2,1,0:T(8,128)(2,1)} %collective-permute-done, f32[16,128,128]{2,1,0:T(8,128)S(1)} %get-tuple-element.35), kind=kLoop, calls=%fused_computation.6 | loop fusion | flops 1310720 | bytes 4718592 | tf_op jit(solution)/shard_map/add | solution.py:294
  33.6 1.6 %collective-permute-start.7 = (bf16[16,128,128]{2,1,0:T(8,128)(2,1)S(1)}, bf16[16,128,128]{2,1,0:T(8,128)(2,1)S(1)}, u32[]{:S(2)}, u32[]{:S(2)}) collective-permute-start(bf16[16,128,128]{2,1,0:T(8,128)(2,1)S(1)} %get-tuple-element.46), channel_id=1, source_target_pairs={{0,1},{1,0},{2,3},{3,2},{4,5},{5,4},{6,7},{7,6},{8,9},{9,8},{10,11... | collective-permute-start | bytes 1572872 | tf_op jit(solution)/shard_map/ppermute | solution.py:299
  35.2 1.1 convert_add_fusion.2
  36.3 11.7 %collective-permute-done.7 = bf16[16,128,128]{2,1,0:T(8,128)(2,1)S(1)} collective-permute-done((bf16[16,128,128]{2,1,0:T(8,128)(2,1)S(1)}, bf16[16,128,128]{2,1,0:T(8,128)(2,1)S(1)}, u32[]{:S(2)}, u32[]{:S(2)}) %collective-permute-start.7) | collective-permute-done | bytes 524320 | tf_op jit(solution)/shard_map/ppermute | solution.py:299
  47.9 1.0 fusion
  48.9 1.5 collective-permute-start.8
  50.4 1.5 collective-permute-start.9
  52.0 0.5 collective-permute-start.5
  52.5 1.6 %collective-permute-done.9 = bf16[128,16]{0,1:T(8,128)(2,1)S(1)} collective-permute-done((bf16[128,16]{0,1:T(8,128)(2,1)S(1)}, bf16[128,16]{0,1:T(8,128)(2,1)S(1)}, u32[]{:S(2)}, u32[]{:S(2)}) %collective-permute-start.9) | collective-permute-done | bytes 4128 | tf_op jit(solution)/shard_map/ppermute | solution.py:270
  54.1 8.5 %collective-permute-done.8 = bf16[16,128,128]{2,1,0:T(8,128)(2,1)S(1)} collective-permute-done((bf16[16,128,128]{2,1,0:T(8,128)(2,1)}, bf16[16,128,128]{2,1,0:T(8,128)(2,1)S(1)}, u32[]{:S(2)}, u32[]{:S(2)}) %collective-permute-start.8) | collective-permute-done | bytes 524320 | tf_op jit(solution)/shard_map/ppermute | solution.py:307
  62.6 0.4 multiply_convert_fusion.1.refs_0_
  63.0 2.1 %collective-permute-done.5 = bf16[16,128,128]{2,1,0:T(8,128)(2,1)S(1)} collective-permute-done((bf16[16,128,128]{2,1,0:T(8,128)(2,1)}, bf16[16,128,128]{2,1,0:T(8,128)(2,1)S(1)}, u32[]{:S(2)}, u32[]{:S(2)}) %collective-permute-start.5) | collective-permute-done | bytes 524320 | tf_op jit(solution)/shard_map/ppermute | solution.py:302
  65.1 1.0 fusion.1
  66.1 0.5 collective-permute-start.6
  66.8 6.2 %shard_map.95 = (bf16[8,128,128]{2,1,0:T(8,128)(2,1)S(1)}, bf16[8,128,128]{2,1,0:T(8,128)(2,1)S(1)}, bf16[8,128,128]{2,1,0:T(8,128)(2,1)S(1)}, bf16[8,128,128]{2...) custom-call(s32[8]{0:T(128)S(1)} %stack.81.scalars, ...), custom_call_target="tpu_custom_call" | custom-call | flops 1073741824 | bytes 8388608 | tf_op jit(solution)/shard_map/pallas_call | solution.py:199
  73.0 5.6 %collective-permute-done.6 = bf16[16,128,128]{2,1,0:T(8,128)(2,1)S(1)} collective-permute-done((bf16[16,128,128]{2,1,0:T(8,128)(2,1)}, bf16[16,128,128]{2,1,0:T(8,128)(2,1)S(1)}, u32[]{:S(2)}, u32[]{:S(2)}) %collective-permute-start.6) | collective-permute-done | bytes 524320 | tf_op jit(solution)/shard_map/ppermute | solution.py:307
  78.6 0.4 multiply_convert_fusion.refs_0_
  79.0 1.6 %collective-permute-start.24 = (bf16[8,128,128]{2,1,0:T(8,128)(2,1)S(1)}, bf16[8,128,128]{2,1,0:T(8,128)(2,1)S(1)}, u32[]{:S(2)}, u32[]{:S(2)}) collective-permute-start(bf16[8,128,128]{2,1,0:T(8,128)(2,1)S(1)} %get-tuple-element.64), channel_id=1, source_target_pairs={{0,1},{1,0},{2,3},{3,2},{4,5},{5,4},{6,7},{7,6},{8,9},{9,8},{10,11... | collective-permute-start | bytes 786440 | tf_op jit(solution)/shard_map/ppermute | solution.py:323
  80.7 0.5 collective-permute-start.13
  81.1 1.6 %collective-permute-start.21 = (bf16[8,128,128]{2,1,0:T(8,128)(2,1)S(1)}, bf16[8,128,128]{2,1,0:T(8,128)(2,1)S(1)}, u32[]{:S(2)}, u32[]{:S(2)}) collective-permute-start(bf16[8,128,128]{2,1,0:T(8,128)(2,1)S(1)} %get-tuple-element.62), channel_id=1, source_target_pairs={{0,1},{1,0},{2,3},{3,2},{4,5},{5,4},{6,7},{7,6},{8,9},{9,8},{10,11... | collective-permute-start | bytes 786440 | tf_op jit(solution)/shard_map/ppermute | solution.py:323
  82.7 0.5 collective-permute-start.15
  83.2 1.6 %collective-permute-start.18 = (bf16[8,128,128]{2,1,0:T(8,128)(2,1)S(1)}, bf16[8,128,128]{2,1,0:T(8,128)(2,1)S(1)}, u32[]{:S(2)}, u32[]{:S(2)}) collective-permute-start(bf16[8,128,128]{2,1,0:T(8,128)(2,1)S(1)} %get-tuple-element.60), channel_id=1, source_target_pairs={{0,1},{1,0},{2,3},{3,2},{4,5},{5,4},{6,7},{7,6},{8,9},{9,8},{10,11... | collective-permute-start | bytes 786440 | tf_op jit(solution)/shard_map/ppermute | solution.py:323
  84.7 5.3 %shard_map.96 = (f32[8,128,128]{2,1,0:T(8,128)S(1)}, f32[8,128,128]{2,1,0:T(8,128)S(1)}, f32[8,128,128]{2,1,0:T(8,128)S(1)}, f32[8,128,128]{2,1,0:T(8,128)S(1)},...) custom-call(s32[8]{0:T(128)S(1)} %stack.81.scalars, s32[8,64]{1,0:T(8,128)S(1)} %bitcast.33, ...), custom_call_target="tpu_custom_call" | custom-call | flops 1073741824 | bytes 8388608 | tf_op jit(solution)/shard_map/pallas_call | solution.py:199
  90.0 0.5 collective-permute-start.12
  90.6 14.5 %collective-permute-done.21.refs_1_ = bf16[8,128,128]{2,1,0:T(8,128)(2,1)S(1)} collective-permute-done((bf16[8,128,128]{2,1,0:T(8,128)(2,1)S(1)}, bf16[8,128,128]{2,1,0:T(8,128)(2,1)S(1)}, u32[]{:S(2)}, u32[]{:S(2)}) %collective-permute-start.21) | collective-permute-done | bytes 262176 | tf_op jit(solution)/shard_map/ppermute | solution.py:323
  105.1 3.7 %collective-permute-start.25 = (bf16[8,128,128]{2,1,0:T(8,128)(2,1)S(1)}, bf16[8,128,128]{2,1,0:T(8,128)(2,1)S(1)}, u32[]{:S(2)}, u32[]{:S(2)}) collective-permute-start(bf16[8,128,128]{2,1,0:T(8,128)(2,1)S(1)} %shard_map.104), channel_id=1, source_target_pairs={{0,2},{6,4},{1,3},{7,5},{8,10},{14,12},{9,11},{15,13},{16,18},{22,... | collective-permute-start | bytes 786440 | tf_op jit(solution)/shard_map/ppermute | solution.py:329
  108.9 7.5 %collective-permute-done.18.refs_1_ = bf16[8,128,128]{2,1,0:T(8,128)(2,1)S(1)} collective-permute-done((bf16[8,128,128]{2,1,0:T(8,128)(2,1)S(1)}, bf16[8,128,128]{2,1,0:T(8,128)(2,1)S(1)}, u32[]{:S(2)}, u32[]{:S(2)}) %collective-permute-start.18) | collective-permute-done | bytes 262176 | tf_op jit(solution)/shard_map/ppermute | solution.py:323
  116.4 3.7 %collective-permute-start.22 = (bf16[8,128,128]{2,1,0:T(8,128)(2,1)S(1)}, bf16[8,128,128]{2,1,0:T(8,128)(2,1)S(1)}, u32[]{:S(2)}, u32[]{:S(2)}) collective-permute-start(bf16[8,128,128]{2,1,0:T(8,128)(2,1)S(1)} %shard_map.102), channel_id=1, source_target_pairs={{0,2},{6,4},{1,3},{7,5},{8,10},{14,12},{9,11},{15,13},{16,18},{22,... | collective-permute-start | bytes 786440 | tf_op jit(solution)/shard_map/ppermute | solution.py:329
  120.1 1.3 collective-permute-start.19
  121.5 1.3 collective-permute-start.16
  123.2 3.5 %collective-permute-done.22.refs_2_ = bf16[8,128,128]{2,1,0:T(8,128)(2,1)S(1)} collective-permute-done((bf16[8,128,128]{2,1,0:T(8,128)(2,1)S(1)}, bf16[8,128,128]{2,1,0:T(8,128)(2,1)S(1)}, u32[]{:S(2)}, u32[]{:S(2)}) %collective-permute-start.22) | collective-permute-done | bytes 262176 | tf_op jit(solution)/shard_map/ppermute | solution.py:329
  126.7 0.7 collective-permute-start.26
  127.5 4.8 %collective-permute-done.19.refs_2_ = bf16[8,128,128]{2,1,0:T(8,128)(2,1)S(1)} collective-permute-done((bf16[8,128,128]{2,1,0:T(8,128)(2,1)S(1)}, bf16[8,128,128]{2,1,0:T(8,128)(2,1)S(1)}, u32[]{:S(2)}, u32[]{:S(2)}) %collective-permute-start.19) | collective-permute-done | bytes 262176 | tf_op jit(solution)/shard_map/ppermute | solution.py:329
  132.3 0.7 collective-permute-start.23
  133.1 4.8 %collective-permute-done.16.refs_2_ = bf16[8,128,128]{2,1,0:T(8,128)(2,1)S(1)} collective-permute-done((bf16[8,128,128]{2,1,0:T(8,128)(2,1)S(1)}, bf16[8,128,128]{2,1,0:T(8,128)(2,1)S(1)}, u32[]{:S(2)}, u32[]{:S(2)}) %collective-permute-start.16) | collective-permute-done | bytes 262176 | tf_op jit(solution)/shard_map/ppermute | solution.py:329
  137.9 1.3 collective-permute-start.20
  139.3 1.3 collective-permute-start.17
  140.7 10.1 %collective-permute-done.20.refs_1_ = bf16[8,128,128]{2,1,0:T(8,128)(2,1)S(1)} collective-permute-done((bf16[8,128,128]{2,1,0:T(8,128)(2,1)S(1)}, bf16[8,128,128]{2,1,0:T(8,128)(2,1)S(1)}, u32[]{:S(2)}, u32[]{:S(2)}) %collective-permute-start.20) | collective-permute-done | bytes 262176 | tf_op jit(solution)/shard_map/ppermute | solution.py:329
  150.8 2.9 %collective-permute-done.17.refs_0_ = bf16[8,128,128]{2,1,0:T(8,128)(2,1)S(1)} collective-permute-done((bf16[8,128,128]{2,1,0:T(8,128)(2,1)S(1)}, bf16[8,128,128]{2,1,0:T(8,128)(2,1)S(1)}, u32[]{:S(2)}, u32[]{:S(2)}) %collective-permute-start.17) | collective-permute-done | bytes 262176 | tf_op jit(solution)/shard_map/ppermute | solution.py:329
  153.7 1.2 shard_map.106
  (48 shorter events, 1.5 us)
Async XLA Ops:
  0.0 52.5 %copy-start = (f32[8192]{0:T(1024)S(1)}, f32[8192]{0:T(1024)}, u32[]{:S(2)}) copy-start(f32[8192]{0:T(1024)} %param.13) | copy-start | bytes 98308
  0.0 24.4 %copy-start.2 = (s32[64,8]{0,1:T(8,128)S(1)}, s32[64,8]{0,1:T(8,128)}, u32[]{:S(2)}) copy-start(s32[64,8]{0,1:T(8,128)} %param.12) | copy-start | bytes 6148
  2.0 13.2 %collective-permute-start.1 = (bf16[8,128,128]{2,1,0:T(8,128)(2,1)}, bf16[8,128,128]{2,1,0:T(8,128)(2,1)S(1)}, u32[]{:S(2)}, u32[]{:S(2)}) collective-permute-start(bf16[8,128,128]{2,1,0:T(8,128)(2,1)} %shard_map.92), channel_id=1, source_target_pairs={{0,1},{1,0},{2,3},{3,2},{4,5},{5,4},{6,7},{7,6},{8,9},{9,8},{10,11... | collective-permute-start | bytes 786440 | tf_op jit(solution)/shard_map/ppermute | solution.py:264
  6.5 17.9 %collective-permute-start.3 = (bf16[16,128,128]{2,1,0:T(8,128)(2,1)S(1)}, bf16[16,128,128]{2,1,0:T(8,128)(2,1)S(1)}, u32[]{:S(2)}, u32[]{:S(2)}) collective-permute-start(bf16[16,128,128]{2,1,0:T(8,128)(2,1)S(1)} %shard_map.93), channel_id=1, source_target_pairs={{0,1},{1,0},{2,3},{3,2},{4,5},{5,4},{6,7},{7,6},{8,9},{9,8},{10,11... | collective-permute-start | bytes 1572872 | tf_op jit(solution)/shard_map/ppermute | solution.py:265
  6.7 0.7 copy-start.1
  15.1 16.0 %collective-permute-start = (bf16[32,128,128]{2,1,0:T(8,128)(2,1)}, bf16[32,128,128]{2,1,0:T(8,128)(2,1)}, u32[]{:S(2)}, u32[]{:S(2)}) collective-permute-start(bf16[32,128,128]{2,1,0:T(8,128)(2,1)} %get-tuple-element.36), channel_id=1, source_target_pairs={{0,8},{8,0},{16,24},{24,16},{1,9},{9,1},{17,25},{25,17},{2,10},{10... | collective-permute-start | bytes 3145736 | tf_op jit(solution)/shard_map/ppermute | solution.py:292
  15.2 9.2 %collective-permute-start.2 = (bf16[8,128,128]{2,1,0:T(8,128)(2,1)S(1)}, bf16[8,128,128]{2,1,0:T(8,128)(2,1)}, u32[]{:S(2)}, u32[]{:S(2)}) collective-permute-start(bf16[8,128,128]{2,1,0:T(8,128)(2,1)S(1)} %collective-permute-done.1.refs_0_), channel_id=1, source_target_pairs={{0,2},{2,0},{4,6},{6,4},{1,3},{3,1},{5,7},{7,5},{8,10},{10,8},{12,... | collective-permute-start | bytes 786440 | tf_op jit(solution)/shard_map/ppermute | solution.py:266
  31.0 19.4 %copy-start.6 = (s32[128,64]{0,1:T(8,128)S(1)}, s32[128,64]{0,1:T(8,128)}, u32[]{:S(2)}) copy-start(s32[128,64]{0,1:T(8,128)} %param.14) | copy-start | bytes 98308
  31.0 4.1 %collective-permute-start.4 = (bf16[32,128,128]{2,1,0:T(8,128)(2,1)S(1)}, bf16[32,128,128]{2,1,0:T(8,128)(2,1)S(1)}, u32[]{:S(2)}, u32[]{:S(2)}) collective-permute-start(bf16[32,128,128]{2,1,0:T(8,128)(2,1)S(1)} %get-tuple-element.40), channel_id=1, source_target_pairs={{0,8},{8,0},{16,24},{24,16},{1,9},{9,1},{17,25},{25,17},{2,10},{10... | collective-permute-start | bytes 3145736 | tf_op jit(solution)/shard_map/ppermute | solution.py:292
  31.1 35.6 %copy-start.3 = (s32[64,8]{0,1:T(8,128)S(1)}, s32[64,8]{0,1:T(8,128)}, u32[]{:S(2)}) copy-start(s32[64,8]{0,1:T(8,128)} %param.16) | copy-start | bytes 6148
  33.6 31.5 %copy-start.5 = (f32[16,128,128]{2,1,0:T(8,128)S(1)}, f32[16,128,128]{2,1,0:T(8,128)}, u32[]{:S(2)}) copy-start(f32[16,128,128]{2,1,0:T(8,128)} %get-tuple-element.38) | copy-start | bytes 3145732
  33.6 14.3 %collective-permute-start.7 = (bf16[16,128,128]{2,1,0:T(8,128)(2,1)S(1)}, bf16[16,128,128]{2,1,0:T(8,128)(2,1)S(1)}, u32[]{:S(2)}, u32[]{:S(2)}) collective-permute-start(bf16[16,128,128]{2,1,0:T(8,128)(2,1)S(1)} %get-tuple-element.46), channel_id=1, source_target_pairs={{0,1},{1,0},{2,3},{3,2},{4,5},{5,4},{6,7},{7,6},{8,9},{9,8},{10,11... | collective-permute-start | bytes 1572872 | tf_op jit(solution)/shard_map/ppermute | solution.py:299
  48.9 13.7 %collective-permute-start.8 = (bf16[16,128,128]{2,1,0:T(8,128)(2,1)}, bf16[16,128,128]{2,1,0:T(8,128)(2,1)S(1)}, u32[]{:S(2)}, u32[]{:S(2)}) collective-permute-start(bf16[16,128,128]{2,1,0:T(8,128)(2,1)} %get-tuple-element.48), channel_id=1, source_target_pairs={{0,16},{8,24},{16,0},{24,8},{1,17},{9,25},{17,1},{25,9},{2,18},{10... | collective-permute-start | bytes 1572872 | tf_op jit(solution)/shard_map/ppermute | solution.py:307
  50.4 3.6 %collective-permute-start.9 = (bf16[128,16]{0,1:T(8,128)(2,1)S(1)}, bf16[128,16]{0,1:T(8,128)(2,1)S(1)}, u32[]{:S(2)}, u32[]{:S(2)}) collective-permute-start(bf16[128,16]{0,1:T(8,128)(2,1)S(1)} %get-tuple-element.74), channel_id=1, source_target_pairs={{0,1},{1,0},{2,3},{3,2},{4,5},{5,4},{6,7},{7,6},{8,9},{9,8},{10,11... | collective-permute-start | bytes 12296 | tf_op jit(solution)/shard_map/ppermute | solution.py:270
  52.0 13.2 %collective-permute-start.5 = (bf16[16,128,128]{2,1,0:T(8,128)(2,1)}, bf16[16,128,128]{2,1,0:T(8,128)(2,1)S(1)}, u32[]{:S(2)}, u32[]{:S(2)}) collective-permute-start(bf16[16,128,128]{2,1,0:T(8,128)(2,1)} %get-tuple-element.42), channel_id=1, source_target_pairs={{0,1},{1,0},{2,3},{3,2},{4,5},{5,4},{6,7},{7,6},{8,9},{9,8},{10,11... | collective-permute-start | bytes 1572872 | tf_op jit(solution)/shard_map/ppermute | solution.py:302
  63.0 3.8 %collective-permute-start.10 = (bf16[16,128,128]{2,1,0:T(8,128)(2,1)S(1)}, bf16[16,128,128]{2,1,0:T(8,128)(2,1)S(1)}, u32[]{:S(2)}, u32[]{:S(2)}) collective-permute-start(bf16[16,128,128]{2,1,0:T(8,128)(2,1)S(1)} %multiply_convert_fusion.1.refs_0_), channel_id=1, source_target_pairs={{0,8},{8,0},{16,24},{24,16},{1,9},{9,1},{17,25},{25,17},{2,10},{10... | collective-permute-start | bytes 1572872 | tf_op jit(solution)/shard_map/ppermute | solution.py:313
  66.1 12.5 %collective-permute-start.6 = (bf16[16,128,128]{2,1,0:T(8,128)(2,1)}, bf16[16,128,128]{2,1,0:T(8,128)(2,1)S(1)}, u32[]{:S(2)}, u32[]{:S(2)}) collective-permute-start(bf16[16,128,128]{2,1,0:T(8,128)(2,1)} %get-tuple-element.44), channel_id=1, source_target_pairs={{0,16},{8,24},{16,0},{24,8},{1,17},{9,25},{17,1},{25,9},{2,18},{10... | collective-permute-start | bytes 1572872 | tf_op jit(solution)/shard_map/ppermute | solution.py:307
  79.0 4.2 %collective-permute-start.11 = (bf16[16,128,128]{2,1,0:T(8,128)(2,1)S(1)}, bf16[16,128,128]{2,1,0:T(8,128)(2,1)S(1)}, u32[]{:S(2)}, u32[]{:S(2)}) collective-permute-start(bf16[16,128,128]{2,1,0:T(8,128)(2,1)S(1)} %multiply_convert_fusion.refs_0_), channel_id=1, source_target_pairs={{0,8},{8,0},{16,24},{24,16},{1,9},{9,1},{17,25},{25,17},{2,10},{10... | collective-permute-start | bytes 1572872 | tf_op jit(solution)/shard_map/ppermute | solution.py:313
  79.0 11.0 %collective-permute-start.24 = (bf16[8,128,128]{2,1,0:T(8,128)(2,1)S(1)}, bf16[8,128,128]{2,1,0:T(8,128)(2,1)S(1)}, u32[]{:S(2)}, u32[]{:S(2)}) collective-permute-start(bf16[8,128,128]{2,1,0:T(8,128)(2,1)S(1)} %get-tuple-element.64), channel_id=1, source_target_pairs={{0,1},{1,0},{2,3},{3,2},{4,5},{5,4},{6,7},{7,6},{8,9},{9,8},{10,11... | collective-permute-start | bytes 786440 | tf_op jit(solution)/shard_map/ppermute | solution.py:323
  80.7 40.9 %collective-permute-start.13 = (bf16[16,128,128]{2,1,0:T(8,128)(2,1)S(1)}, bf16[16,128,128]{2,1,0:T(8,128)(2,1)S(1)}, u32[]{:S(2)}, u32[]{:S(2)}) collective-permute-start(bf16[16,128,128]{2,1,0:T(8,128)(2,1)S(1)} %get-tuple-element.56), channel_id=1, source_target_pairs={{0,1},{1,0},{2,3},{3,2},{4,5},{5,4},{6,7},{7,6},{8,9},{9,8},{10,11... | collective-permute-start | bytes 1572872 | tf_op jit(solution)/shard_map/ppermute | solution.py:323
  81.1 24.0 %collective-permute-start.21 = (bf16[8,128,128]{2,1,0:T(8,128)(2,1)S(1)}, bf16[8,128,128]{2,1,0:T(8,128)(2,1)S(1)}, u32[]{:S(2)}, u32[]{:S(2)}) collective-permute-start(bf16[8,128,128]{2,1,0:T(8,128)(2,1)S(1)} %get-tuple-element.62), channel_id=1, source_target_pairs={{0,1},{1,0},{2,3},{3,2},{4,5},{5,4},{6,7},{7,6},{8,9},{9,8},{10,11... | collective-permute-start | bytes 786440 | tf_op jit(solution)/shard_map/ppermute | solution.py:323
  82.7 37.4 %collective-permute-start.15 = (bf16[8,128,128]{2,1,0:T(8,128)(2,1)S(1)}, bf16[8,128,128]{2,1,0:T(8,128)(2,1)S(1)}, u32[]{:S(2)}, u32[]{:S(2)}) collective-permute-start(bf16[8,128,128]{2,1,0:T(8,128)(2,1)S(1)} %get-tuple-element.58), channel_id=1, source_target_pairs={{0,1},{1,0},{2,3},{3,2},{4,5},{5,4},{6,7},{7,6},{8,9},{9,8},{10,11... | collective-permute-start | bytes 786440 | tf_op jit(solution)/shard_map/ppermute | solution.py:323
  83.2 70.6 %copy-start.4 = (f32[2048]{0:T(1024)S(1)}, f32[2048]{0:T(1024)}, u32[]{:S(2)}) copy-start(f32[2048]{0:T(1024)} %param.17) | copy-start | bytes 24580
  83.2 33.2 %collective-permute-start.18 = (bf16[8,128,128]{2,1,0:T(8,128)(2,1)S(1)}, bf16[8,128,128]{2,1,0:T(8,128)(2,1)S(1)}, u32[]{:S(2)}, u32[]{:S(2)}) collective-permute-start(bf16[8,128,128]{2,1,0:T(8,128)(2,1)S(1)} %get-tuple-element.60), channel_id=1, source_target_pairs={{0,1},{1,0},{2,3},{3,2},{4,5},{5,4},{6,7},{7,6},{8,9},{9,8},{10,11... | collective-permute-start | bytes 786440 | tf_op jit(solution)/shard_map/ppermute | solution.py:323
  90.0 49.3 %collective-permute-start.12 = (bf16[16,128,128]{2,1,0:T(8,128)(2,1)S(1)}, bf16[16,128,128]{2,1,0:T(8,128)(2,1)S(1)}, u32[]{:S(2)}, u32[]{:S(2)}) collective-permute-start(bf16[16,128,128]{2,1,0:T(8,128)(2,1)S(1)} %get-tuple-element.54), channel_id=1, source_target_pairs={{0,1},{1,0},{2,3},{3,2},{4,5},{5,4},{6,7},{7,6},{8,9},{9,8},{10,11... | collective-permute-start | bytes 1572872 | tf_op jit(solution)/shard_map/ppermute | solution.py:323
  105.1 17.8 %collective-permute-start.25 = (bf16[8,128,128]{2,1,0:T(8,128)(2,1)S(1)}, bf16[8,128,128]{2,1,0:T(8,128)(2,1)S(1)}, u32[]{:S(2)}, u32[]{:S(2)}) collective-permute-start(bf16[8,128,128]{2,1,0:T(8,128)(2,1)S(1)} %shard_map.104), channel_id=1, source_target_pairs={{0,2},{6,4},{1,3},{7,5},{8,10},{14,12},{9,11},{15,13},{16,18},{22,... | collective-permute-start | bytes 786440 | tf_op jit(solution)/shard_map/ppermute | solution.py:329
  116.4 10.3 %collective-permute-start.22 = (bf16[8,128,128]{2,1,0:T(8,128)(2,1)S(1)}, bf16[8,128,128]{2,1,0:T(8,128)(2,1)S(1)}, u32[]{:S(2)}, u32[]{:S(2)}) collective-permute-start(bf16[8,128,128]{2,1,0:T(8,128)(2,1)S(1)} %shard_map.102), channel_id=1, source_target_pairs={{0,2},{6,4},{1,3},{7,5},{8,10},{14,12},{9,11},{15,13},{16,18},{22,... | collective-permute-start | bytes 786440 | tf_op jit(solution)/shard_map/ppermute | solution.py:329
  120.1 12.2 %collective-permute-start.19 = (bf16[8,128,128]{2,1,0:T(8,128)(2,1)S(1)}, bf16[8,128,128]{2,1,0:T(8,128)(2,1)S(1)}, u32[]{:S(2)}, u32[]{:S(2)}) collective-permute-start(bf16[8,128,128]{2,1,0:T(8,128)(2,1)S(1)} %shard_map.100), channel_id=1, source_target_pairs={{0,2},{6,4},{1,3},{7,5},{8,10},{14,12},{9,11},{15,13},{16,18},{22,... | collective-permute-start | bytes 786440 | tf_op jit(solution)/shard_map/ppermute | solution.py:329
  121.5 16.4 %collective-permute-start.16 = (bf16[8,128,128]{2,1,0:T(8,128)(2,1)S(1)}, bf16[8,128,128]{2,1,0:T(8,128)(2,1)S(1)}, u32[]{:S(2)}, u32[]{:S(2)}) collective-permute-start(bf16[8,128,128]{2,1,0:T(8,128)(2,1)S(1)} %shard_map.98), channel_id=1, source_target_pairs={{0,2},{6,4},{1,3},{7,5},{8,10},{14,12},{9,11},{15,13},{16,18},{22,... | collective-permute-start | bytes 786440 | tf_op jit(solution)/shard_map/ppermute | solution.py:329
  123.0 30.8 %collective-permute-start.14 = (bf16[16,128,128]{2,1,0:T(8,128)(2,1)S(1)}, bf16[16,128,128]{2,1,0:T(8,128)(2,1)S(1)}, u32[]{:S(2)}, u32[]{:S(2)}) collective-permute-start(bf16[16,128,128]{2,1,0:T(8,128)(2,1)S(1)} %shard_map.97), channel_id=1, source_target_pairs={{0,2},{2,0},{4,6},{6,4},{1,3},{3,1},{5,7},{7,5},{8,10},{10,8},{12,... | collective-permute-start | bytes 1572872 | tf_op jit(solution)/shard_map/ppermute | solution.py:329
  126.7 13.9 %collective-permute-start.26 = (bf16[8,128,128]{2,1,0:T(8,128)(2,1)S(1)}, bf16[8,128,128]{2,1,0:T(8,128)(2,1)S(1)}, u32[]{:S(2)}, u32[]{:S(2)}) collective-permute-start(bf16[8,128,128]{2,1,0:T(8,128)(2,1)S(1)} %shard_map.105), channel_id=1, source_target_pairs={{2,4},{4,2},{3,5},{5,3},{10,12},{12,10},{11,13},{13,11},{18,20},{2... | collective-permute-start | bytes 786440 | tf_op jit(solution)/shard_map/ppermute | solution.py:329
  132.3 8.3 %collective-permute-start.23 = (bf16[8,128,128]{2,1,0:T(8,128)(2,1)S(1)}, bf16[8,128,128]{2,1,0:T(8,128)(2,1)S(1)}, u32[]{:S(2)}, u32[]{:S(2)}) collective-permute-start(bf16[8,128,128]{2,1,0:T(8,128)(2,1)S(1)} %shard_map.103), channel_id=1, source_target_pairs={{2,4},{4,2},{3,5},{5,3},{10,12},{12,10},{11,13},{13,11},{18,20},{2... | collective-permute-start | bytes 786440 | tf_op jit(solution)/shard_map/ppermute | solution.py:329
  137.9 12.9 %collective-permute-start.20 = (bf16[8,128,128]{2,1,0:T(8,128)(2,1)S(1)}, bf16[8,128,128]{2,1,0:T(8,128)(2,1)S(1)}, u32[]{:S(2)}, u32[]{:S(2)}) collective-permute-start(bf16[8,128,128]{2,1,0:T(8,128)(2,1)S(1)} %shard_map.101), channel_id=1, source_target_pairs={{2,6},{4,0},{3,7},{5,1},{10,14},{12,8},{11,15},{13,9},{18,22},{20,... | collective-permute-start | bytes 786440 | tf_op jit(solution)/shard_map/ppermute | solution.py:329
  139.3 14.4 %collective-permute-start.17 = (bf16[8,128,128]{2,1,0:T(8,128)(2,1)S(1)}, bf16[8,128,128]{2,1,0:T(8,128)(2,1)S(1)}, u32[]{:S(2)}, u32[]{:S(2)}) collective-permute-start(bf16[8,128,128]{2,1,0:T(8,128)(2,1)S(1)} %shard_map.99), channel_id=1, source_target_pairs={{2,6},{4,0},{3,7},{5,1},{10,14},{12,8},{11,15},{13,9},{18,22},{20,... | collective-permute-start | bytes 786440 | tf_op jit(solution)/shard_map/ppermute | solution.py:329

commit v5 on v4

--- a/solution.py
+++ b/solution.py
@@ -62,20 +62,25 @@
         pair = jnp.concatenate([w_ref[row, k], w_ref[row, k + 1]], axis=1)
         product = jnp.dot(x, pair, preferred_element_type=jnp.float32)
         for half in range(2):
-            col = cols_ref[k + half, scalars[0] + row] - scalars[1]
-            which = sum((col >= i * group).astype(jnp.int32) for i in range(1, GROUPS))
-            to = col + scalars[2 + which]
+            col = cols_ref[k + half, scalars[0] + row]
+            if group & (group - 1):
+                which = lax.rem(lax.div(col, group), GROUPS)
+            else:
+                which = (col >> (group.bit_length() - 1)) & (GROUPS - 1)
+            to = col + scalars[1 + which]
             acc[to] = acc[to] + product[:, half * block:(half + 1) * block]
 
 
 def add_products(acc, x_ref, w_ref, tables, start, first, count):
+    unroll = 2 * UNROLL if count % (2 * UNROLL) == 0 else UNROLL
+
     def advance(step, carry):
-        for i in range(UNROLL):
-            at = first + step * UNROLL + i
+        for i in range(unroll):
+            at = first + step * unroll + i
             add_row(acc, x_ref[at], w_ref, tables, start + at)
         return carry
 
-    lax.fori_loop(0, count // UNROLL, advance, 0)
+    lax.fori_loop(0, count // unroll, advance, 0)
 
 
 def write_out(acc, outs):
@@ -92,17 +97,23 @@
 
 def row_copies(w_ref, held_ref, sems, ranges):
     copies = []
+    sem = done = 0
     for start, count in ranges:
-        for first in range(0, count, UNROLL):
-            rows = pl.ds(start + first, UNROLL)
-            copies.append(pltpu.make_async_copy(w_ref.at[rows], held_ref.at[rows], sems.at[len(copies)]))
+        pieces = []
+        first = 0
+        while first < count:
+            size = min(count - first, max(done, UNROLL))
+            rows = pl.ds(start + first, size)
+            pieces.append((first, size, pltpu.make_async_copy(w_ref.at[rows], held_ref.at[rows], sems.at[sem])))
+            sem, done, first = sem + 1, done + size, first + size
+        copies.append(pieces)
     return copies
 
 
 def fold_kernel(parts, load, scalars, cols_ref, *refs):
     x_refs, w_ref, refs = refs[:parts], refs[parts], refs[parts + 1:]
     tables = scalars, cols_ref
-    starts = [scalars[2 + GROUPS + i] for i in range(parts)]
+    starts = [scalars[1 + GROUPS + i] for i in range(parts)]
     copies = []
     if load:
         *outs, held_ref, acc, sems = refs
@@ -110,14 +121,15 @@
         w_ref = held_ref
     else:
         *outs, acc = refs
-    for copy in copies:
-        copy.start()
+    for pieces in copies:
+        for _, _, copy in pieces:
+            copy.start()
     clear(acc)
     for start, x_ref in zip(starts, x_refs):
         if load:
-            for first in range(0, x_ref.shape[0], UNROLL):
-                copies.pop(0).wait()
-                add_products(acc, x_ref, w_ref, tables, start, first, UNROLL)
+            for first, size, copy in copies.pop(0):
+                copy.wait()
+                add_products(acc, x_ref, w_ref, tables, start, first, size)
         else:
             add_products(acc, x_ref, w_ref, tables, start, 0, x_ref.shape[0])
     write_out(acc, outs)
@@ -129,22 +141,22 @@
     width = x_ref.shape[1]
     block = width // blocks
     count = blocks // UNROLL
-    half = scalars[2 + GROUPS]
+    half = scalars[1 + GROUPS]
     lanes = pl.ds(pl.multiple_of(half * width, width), width)
     inputs = [
         pltpu.make_async_copy(live_ref.at[pl.ds(half * blocks, blocks)], mask_ref, sems.at[count]),
         pltpu.make_async_copy(acts_ref.at[:, lanes], x_ref, sems.at[count + 1]),
     ]
-    copies = row_copies(w_ref, held_ref, sems, [(0, blocks)])
-    for copy in inputs + copies:
+    (pieces,) = row_copies(w_ref, held_ref, sems, [(0, blocks)])
+    for copy in inputs + [piece[2] for piece in pieces]:
         copy.start()
     clear(acc)
     for copy in inputs:
         copy.wait()
     live = mask_ref[...].astype(jnp.float32).T
-    for i, copy in enumerate(copies):
+    for first, size, copy in pieces:
         copy.wait()
-        for at in range(i * UNROLL, (i + 1) * UNROLL):
+        for at in range(first, first + size):
             x = x_ref[:, at * block:(at + 1) * block].astype(jnp.float32) * live[:, at:at + 1]
             add_row(acc, x.astype(jnp.bfloat16), held_ref, (scalars, cols_ref), at)
     write_out(acc, outs)
@@ -274,18 +286,18 @@
         bias1.reshape(col_blocks, 1, block), d * half_mid + core * quarter, quarter, 0
     )
 
-    def shifts(places, size):
-        return [(place - i) * size for i, place in enumerate(places)]
+    def shifts(places, size, first):
+        return [(place - i) * size - first for i, place in enumerate(places)]
 
     places1 = [(1 - (which ^ core)) * 2 + 1 - (depth ^ d) for depth in range(2) for which in range(2)]
-    scalars1 = [d * half_in, c * col_blocks, *shifts(places1, quarter)]
+    scalars1 = [d * half_in, *shifts(places1, quarter, c * col_blocks)]
 
     share = row_blocks // size_col
     far = jnp.where(c < size_col // 2, size_col - 1, 0)
     places2 = [
         jnp.where(i == far, 0, jnp.where(i == (far ^ 1), 1, jnp.where(i == (c ^ 1), 2, 3))) for i in range(size_col)
     ]
-    scalars2 = [d * half_mid, r * row_blocks, *shifts(places2, share)]
+    scalars2 = [d * half_mid, *shifts(places2, share, r * row_blocks)]
     segments = [(half_mid, bf16), (quarter, f32), (quarter, f32)]
 
     def core_sums(low, send, keep):

time: 155 us -> 155 us (level)
  Pallas kernels: 31.2 us -> 29.6 us
  transfers between devices with their start and end apart: 27 -> 27, of which waited for: 13 -> 13; matrix products, arithmetic and copies ran while one was open for 3% -> 3% of each run, Pallas kernels for 18% -> 17%
where the time goes in v5:
time: 155 us; the launch traced here: 154 us
  waiting for transfers between devices  85.3 us (55%)
  starting transfers between devices  31.6 us (20%)
  Pallas kernels  29.6 us (19%)
  other arithmetic  6.29 us (4%)
    ppermute x9, waiting for transfers between devices, over_col(): return lax.ppermute(add(parts), 'col', perm)  26.3 us
    ppermute x6, waiting for transfers between devices, exchange_plan(): got.append(over_depth(part))  22.6 us
    pallas_call x3, Pallas kernels, fold(): pl.pallas_call(functools.partial(fold_kernel, len(xs), load), out_shape=o...  16.9 us
    ppermute x2, waiting for transfers between devices, x_sums(): return (part, over_x(low))  14.1 us
    ppermute x9, starting transfers between devices, over_col(): return lax.ppermute(add(parts), 'col', perm)  13.9 us
    ppermute x1, waiting for transfers between devices, exchange_plan(): got_other = over_depth(send_own)  11.5 us
    pallas_call x1, Pallas kernels, own_fold(): pl.pallas_call(own_fold_kernel, out_shape=outs, in_specs=[smem, smem, hbm...  7.35 us
    ppermute x1, waiting for transfers between devices, exchange_plan(): lax.ppermute(part_x, 'col', [(i, i ^ 1) for i in range(size_col)])  6.91 us
  transfers between devices with their start and end apart: 27, of which 13 were waited for; matrix products, arithmetic and copies ran while one was open for 3% of the time, Pallas kernels for 17%

profile of v5, /device:TPU:0, one launch (start us, length us, event | category | flops | bytes accessed | tf_op | source)
XLA Modules:
  0.0 154.2 jit_solution(9251104554128677146)
XLA Ops:
  0.0 2.0 %shard_map.92 = bf16[8,128,128]{2,1,0:T(8,128)(2,1)} custom-call(s32[1]{0:T(128)} %bitcast.17.half_ref, bf16[128,8192]{1,0:T(8,128)(2,1)} %acts_ref.5, s32[64,128]{1,0:T(8,128)} %bitcast.33), custom_call_target="tpu_custom_call" | custom-call | flops 1024 | bytes 524288 | tf_op jit(solution)/shard_map/pallas_call | solution.py:31
  2.0 3.0 %collective-permute-start.1 = (bf16[8,128,128]{2,1,0:T(8,128)(2,1)}, bf16[8,128,128]{2,1,0:T(8,128)(2,1)S(1)}, u32[]{:S(2)}, u32[]{:S(2)}) collective-permute-start(bf16[8,128,128]{2,1,0:T(8,128)(2,1)} %shard_map.92), channel_id=1, source_target_pairs={{0,1},{1,0},{2,3},{3,2},{4,5},{5,4},{6,7},{7,6},{8,9},{9,8},{10,11... | collective-permute-start | bytes 786440 | tf_op jit(solution)/shard_map/ppermute | solution.py:276
  5.0 1.5 shard_map.93
  6.7 0.7 copy-done.1
  7.4 7.3 %shard_map.91 = (bf16[32,128,128]{2,1,0:T(8,128)(2,1)}, f32[16,128,128]{2,1,0:T(8,128)S(1)}, f32[16,128,128]{2,1,0:T(8,128)S(1)}) custom-call(s32[6]{0:T(128)S(1)} %stack.78.scalars, s32[8,64]{1,0:T(8,128)S(1)} %bitcast.28, bf16[128,8192]{1,0:T(8,128)(2,1)} %acts_ref.5, s32[64,128]{1,0:T(8,128)} %bitcast.35, bf16[32,8,128,128]{3,2,1,0:T(8,128)(2,1)} %refs_3_.1), custom_call_target="tpu_custom_call" | custom-call | flops 1073741824 | bytes 8388608 | tf_op jit(solution)/shard_map/pallas_call | solution.py:180
  14.8 2.1 %collective-permute-start.2 = (bf16[8,128,128]{2,1,0:T(8,128)(2,1)S(1)}, bf16[8,128,128]{2,1,0:T(8,128)(2,1)}, u32[]{:S(2)}, u32[]{:S(2)}) collective-permute-start(bf16[8,128,128]{2,1,0:T(8,128)(2,1)S(1)} %collective-permute-done.1.refs_0_), channel_id=1, source_target_pairs={{0,2},{2,0},{4,6},{6,4},{1,3},{3,1},{5,7},{7,5},{8,10},{10,8},{12,... | collective-permute-start | bytes 786440 | tf_op jit(solution)/shard_map/ppermute | solution.py:278
  17.0 6.9 %collective-permute-done.2.refs_1_ = bf16[8,128,128]{2,1,0:T(8,128)(2,1)} collective-permute-done((bf16[8,128,128]{2,1,0:T(8,128)(2,1)S(1)}, bf16[8,128,128]{2,1,0:T(8,128)(2,1)}, u32[]{:S(2)}, u32[]{:S(2)}) %collective-permute-start.2) | collective-permute-done | bytes 262176 | tf_op jit(solution)/shard_map/ppermute | solution.py:278
  23.9 6.3 %shard_map.94 = (bf16[32,128,128]{2,1,0:T(8,128)(2,1)S(1)}, f32[16,128,128]{2,1,0:T(8,128)S(1)}, f32[16,128,128]{2,1,0:T(8,128)S(1)}) custom-call(s32[8]{0:T(128)S(1)} %stack.81.scalars, s32[8,64]{1,0:T(8,128)S(1)} %bitcast.29, bf16[8,128,128]{2,1,0:T(8,128)(2,1)S(1)} %collective-permute-done.1.refs_0_, bf16[8,128,128]{2,1,0:T(8,128)(2,1)} %collective-permute-done.2.refs_1_, ...), custom_call_target="tpu_custom_call" | custom-call | flops 1073741824 | bytes 8388608 | tf_op jit(solution)/shard_map/pallas_call | solution.py:211
  30.4 2.5 %convert_add_fusion.3 = (f32[16,128,128]{2,1,0:T(8,128)}, bf16[16,128,128]{2,1,0:T(8,128)(2,1)S(1)}) fusion(f32[16,128,128]{2,1,0:T(8,128)S(1)} %get-tuple-element.37, bf16[32,128,128]{2,1,0:T(8,128)(2,1)} %collective-permute-done, f32[16,128,128]{2,1,0:T(8,128)S(1)} %get-tuple-element.35), kind=kLoop, calls=%fused_computation.6 | loop fusion | flops 1310720 | bytes 4718592 | tf_op jit(solution)/shard_map/add | solution.py:306
  32.9 1.7 %collective-permute-start.7 = (bf16[16,128,128]{2,1,0:T(8,128)(2,1)S(1)}, bf16[16,128,128]{2,1,0:T(8,128)(2,1)S(1)}, u32[]{:S(2)}, u32[]{:S(2)}) collective-permute-start(bf16[16,128,128]{2,1,0:T(8,128)(2,1)S(1)} %get-tuple-element.46), channel_id=1, source_target_pairs={{0,1},{1,0},{2,3},{3,2},{4,5},{5,4},{6,7},{7,6},{8,9},{9,8},{10,11... | collective-permute-start | bytes 1572872 | tf_op jit(solution)/shard_map/ppermute | solution.py:311
  34.6 1.1 convert_add_fusion.2
  35.7 11.5 %collective-permute-done.7 = bf16[16,128,128]{2,1,0:T(8,128)(2,1)S(1)} collective-permute-done((bf16[16,128,128]{2,1,0:T(8,128)(2,1)S(1)}, bf16[16,128,128]{2,1,0:T(8,128)(2,1)S(1)}, u32[]{:S(2)}, u32[]{:S(2)}) %collective-permute-start.7) | collective-permute-done | bytes 524320 | tf_op jit(solution)/shard_map/ppermute | solution.py:311
  47.2 1.0 fusion
  48.2 1.7 %collective-permute-start.8 = (bf16[16,128,128]{2,1,0:T(8,128)(2,1)}, bf16[16,128,128]{2,1,0:T(8,128)(2,1)S(1)}, u32[]{:S(2)}, u32[]{:S(2)}) collective-permute-start(bf16[16,128,128]{2,1,0:T(8,128)(2,1)} %get-tuple-element.48), channel_id=1, source_target_pairs={{0,16},{8,24},{16,0},{24,8},{1,17},{9,25},{17,1},{25,9},{2,18},{10... | collective-permute-start | bytes 1572872 | tf_op jit(solution)/shard_map/ppermute | solution.py:319
  49.8 1.5 collective-permute-start.9
  51.4 0.5 collective-permute-start.5
  51.9 1.6 %collective-permute-done.9 = bf16[128,16]{0,1:T(8,128)(2,1)S(1)} collective-permute-done((bf16[128,16]{0,1:T(8,128)(2,1)S(1)}, bf16[128,16]{0,1:T(8,128)(2,1)S(1)}, u32[]{:S(2)}, u32[]{:S(2)}) %collective-permute-start.9) | collective-permute-done | bytes 4128 | tf_op jit(solution)/shard_map/ppermute | solution.py:282
  53.5 8.4 %collective-permute-done.8 = bf16[16,128,128]{2,1,0:T(8,128)(2,1)S(1)} collective-permute-done((bf16[16,128,128]{2,1,0:T(8,128)(2,1)}, bf16[16,128,128]{2,1,0:T(8,128)(2,1)S(1)}, u32[]{:S(2)}, u32[]{:S(2)}) %collective-permute-start.8) | collective-permute-done | bytes 524320 | tf_op jit(solution)/shard_map/ppermute | solution.py:319
  61.8 0.4 multiply_convert_fusion.1.refs_0_
  62.3 2.2 %collective-permute-done.5 = bf16[16,128,128]{2,1,0:T(8,128)(2,1)S(1)} collective-permute-done((bf16[16,128,128]{2,1,0:T(8,128)(2,1)}, bf16[16,128,128]{2,1,0:T(8,128)(2,1)S(1)}, u32[]{:S(2)}, u32[]{:S(2)}) %collective-permute-start.5) | collective-permute-done | bytes 524320 | tf_op jit(solution)/shard_map/ppermute | solution.py:314
  64.5 1.0 fusion.1
  65.5 0.5 collective-permute-start.6
  66.1 6.0 %shard_map.95 = (bf16[8,128,128]{2,1,0:T(8,128)(2,1)S(1)}, bf16[8,128,128]{2,1,0:T(8,128)(2,1)S(1)}, bf16[8,128,128]{2,1,0:T(8,128)(2,1)S(1)}, bf16[8,128,128]{2...) custom-call(s32[7]{0:T(128)S(1)} %stack.72.scalars, ...), custom_call_target="tpu_custom_call" | custom-call | flops 1073741824 | bytes 8388608 | tf_op jit(solution)/shard_map/pallas_call | solution.py:211
  72.1 5.7 %collective-permute-done.6 = bf16[16,128,128]{2,1,0:T(8,128)(2,1)S(1)} collective-permute-done((bf16[16,128,128]{2,1,0:T(8,128)(2,1)}, bf16[16,128,128]{2,1,0:T(8,128)(2,1)S(1)}, u32[]{:S(2)}, u32[]{:S(2)}) %collective-permute-start.6) | collective-permute-done | bytes 524320 | tf_op jit(solution)/shard_map/ppermute | solution.py:319
  77.8 0.4 multiply_convert_fusion.refs_0_
  78.3 1.8 %collective-permute-start.24 = (bf16[8,128,128]{2,1,0:T(8,128)(2,1)S(1)}, bf16[8,128,128]{2,1,0:T(8,128)(2,1)S(1)}, u32[]{:S(2)}, u32[]{:S(2)}) collective-permute-start(bf16[8,128,128]{2,1,0:T(8,128)(2,1)S(1)} %get-tuple-element.64), channel_id=1, source_target_pairs={{0,1},{1,0},{2,3},{3,2},{4,5},{5,4},{6,7},{7,6},{8,9},{9,8},{10,11... | collective-permute-start | bytes 786440 | tf_op jit(solution)/shard_map/ppermute | solution.py:335
  80.1 0.3 collective-permute-start.13
  80.4 1.7 %collective-permute-start.21 = (bf16[8,128,128]{2,1,0:T(8,128)(2,1)S(1)}, bf16[8,128,128]{2,1,0:T(8,128)(2,1)S(1)}, u32[]{:S(2)}, u32[]{:S(2)}) collective-permute-start(bf16[8,128,128]{2,1,0:T(8,128)(2,1)S(1)} %get-tuple-element.62), channel_id=1, source_target_pairs={{0,1},{1,0},{2,3},{3,2},{4,5},{5,4},{6,7},{7,6},{8,9},{9,8},{10,11... | collective-permute-start | bytes 786440 | tf_op jit(solution)/shard_map/ppermute | solution.py:335
  82.1 0.3 collective-permute-start.15
  82.4 1.7 %collective-permute-start.18 = (bf16[8,128,128]{2,1,0:T(8,128)(2,1)S(1)}, bf16[8,128,128]{2,1,0:T(8,128)(2,1)S(1)}, u32[]{:S(2)}, u32[]{:S(2)}) collective-permute-start(bf16[8,128,128]{2,1,0:T(8,128)(2,1)S(1)} %get-tuple-element.60), channel_id=1, source_target_pairs={{0,1},{1,0},{2,3},{3,2},{4,5},{5,4},{6,7},{7,6},{8,9},{9,8},{10,11... | collective-permute-start | bytes 786440 | tf_op jit(solution)/shard_map/ppermute | solution.py:335
  84.1 4.5 %shard_map.96 = (f32[8,128,128]{2,1,0:T(8,128)S(1)}, f32[8,128,128]{2,1,0:T(8,128)S(1)}, f32[8,128,128]{2,1,0:T(8,128)S(1)}, f32[8,128,128]{2,1,0:T(8,128)S(1)},...) custom-call(s32[7]{0:T(128)S(1)} %stack.72.scalars, s32[8,64]{1,0:T(8,128)S(1)} %bitcast.31, ...), custom_call_target="tpu_custom_call" | custom-call | flops 1073741824 | bytes 8388608 | tf_op jit(solution)/shard_map/pallas_call | solution.py:211
  88.7 0.6 collective-permute-start.12
  89.3 15.1 %collective-permute-done.21.refs_1_ = bf16[8,128,128]{2,1,0:T(8,128)(2,1)S(1)} collective-permute-done((bf16[8,128,128]{2,1,0:T(8,128)(2,1)S(1)}, bf16[8,128,128]{2,1,0:T(8,128)(2,1)S(1)}, u32[]{:S(2)}, u32[]{:S(2)}) %collective-permute-start.21) | collective-permute-done | bytes 262176 | tf_op jit(solution)/shard_map/ppermute | solution.py:335
  104.4 3.6 %collective-permute-start.25 = (bf16[8,128,128]{2,1,0:T(8,128)(2,1)S(1)}, bf16[8,128,128]{2,1,0:T(8,128)(2,1)S(1)}, u32[]{:S(2)}, u32[]{:S(2)}) collective-permute-start(bf16[8,128,128]{2,1,0:T(8,128)(2,1)S(1)} %shard_map.104), channel_id=1, source_target_pairs={{0,2},{6,4},{1,3},{7,5},{8,10},{14,12},{9,11},{15,13},{16,18},{22,... | collective-permute-start | bytes 786440 | tf_op jit(solution)/shard_map/ppermute | solution.py:341
  108.1 7.5 %collective-permute-done.18.refs_1_ = bf16[8,128,128]{2,1,0:T(8,128)(2,1)S(1)} collective-permute-done((bf16[8,128,128]{2,1,0:T(8,128)(2,1)S(1)}, bf16[8,128,128]{2,1,0:T(8,128)(2,1)S(1)}, u32[]{:S(2)}, u32[]{:S(2)}) %collective-permute-start.18) | collective-permute-done | bytes 262176 | tf_op jit(solution)/shard_map/ppermute | solution.py:335
  115.6 3.6 %collective-permute-start.22 = (bf16[8,128,128]{2,1,0:T(8,128)(2,1)S(1)}, bf16[8,128,128]{2,1,0:T(8,128)(2,1)S(1)}, u32[]{:S(2)}, u32[]{:S(2)}) collective-permute-start(bf16[8,128,128]{2,1,0:T(8,128)(2,1)S(1)} %shard_map.102), channel_id=1, source_target_pairs={{0,2},{6,4},{1,3},{7,5},{8,10},{14,12},{9,11},{15,13},{16,18},{22,... | collective-permute-start | bytes 786440 | tf_op jit(solution)/shard_map/ppermute | solution.py:341
  119.4 1.3 collective-permute-start.19
  120.8 1.3 collective-permute-start.16
  122.4 3.5 %collective-permute-done.22.refs_2_ = bf16[8,128,128]{2,1,0:T(8,128)(2,1)S(1)} collective-permute-done((bf16[8,128,128]{2,1,0:T(8,128)(2,1)S(1)}, bf16[8,128,128]{2,1,0:T(8,128)(2,1)S(1)}, u32[]{:S(2)}, u32[]{:S(2)}) %collective-permute-start.22) | collective-permute-done | bytes 262176 | tf_op jit(solution)/shard_map/ppermute | solution.py:341
  126.0 0.7 collective-permute-start.26
  126.7 4.8 %collective-permute-done.19.refs_2_ = bf16[8,128,128]{2,1,0:T(8,128)(2,1)S(1)} collective-permute-done((bf16[8,128,128]{2,1,0:T(8,128)(2,1)S(1)}, bf16[8,128,128]{2,1,0:T(8,128)(2,1)S(1)}, u32[]{:S(2)}, u32[]{:S(2)}) %collective-permute-start.19) | collective-permute-done | bytes 262176 | tf_op jit(solution)/shard_map/ppermute | solution.py:341
  131.6 0.7 collective-permute-start.23
  132.3 4.8 %collective-permute-done.16.refs_2_ = bf16[8,128,128]{2,1,0:T(8,128)(2,1)S(1)} collective-permute-done((bf16[8,128,128]{2,1,0:T(8,128)(2,1)S(1)}, bf16[8,128,128]{2,1,0:T(8,128)(2,1)S(1)}, u32[]{:S(2)}, u32[]{:S(2)}) %collective-permute-start.16) | collective-permute-done | bytes 262176 | tf_op jit(solution)/shard_map/ppermute | solution.py:341
  137.2 1.3 collective-permute-start.20
  138.6 1.3 collective-permute-start.17
  139.9 10.1 %collective-permute-done.20.refs_1_ = bf16[8,128,128]{2,1,0:T(8,128)(2,1)S(1)} collective-permute-done((bf16[8,128,128]{2,1,0:T(8,128)(2,1)S(1)}, bf16[8,128,128]{2,1,0:T(8,128)(2,1)S(1)}, u32[]{:S(2)}, u32[]{:S(2)}) %collective-permute-start.20) | collective-permute-done | bytes 262176 | tf_op jit(solution)/shard_map/ppermute | solution.py:341
  150.0 2.9 %collective-permute-done.17.refs_0_ = bf16[8,128,128]{2,1,0:T(8,128)(2,1)S(1)} collective-permute-done((bf16[8,128,128]{2,1,0:T(8,128)(2,1)S(1)}, bf16[8,128,128]{2,1,0:T(8,128)(2,1)S(1)}, u32[]{:S(2)}, u32[]{:S(2)}) %collective-permute-start.17) | collective-permute-done | bytes 262176 | tf_op jit(solution)/shard_map/ppermute | solution.py:341
  153.0 1.2 shard_map.106
  (48 shorter events, 1.5 us)
Async XLA Ops:
  0.0 51.9 %copy-start = (f32[8192]{0:T(1024)S(1)}, f32[8192]{0:T(1024)}, u32[]{:S(2)}) copy-start(f32[8192]{0:T(1024)} %param.13) | copy-start | bytes 98308
  0.0 23.9 %copy-start.2 = (s32[64,8]{0,1:T(8,128)S(1)}, s32[64,8]{0,1:T(8,128)}, u32[]{:S(2)}) copy-start(s32[64,8]{0,1:T(8,128)} %param.12) | copy-start | bytes 6148
  2.0 12.8 %collective-permute-start.1 = (bf16[8,128,128]{2,1,0:T(8,128)(2,1)}, bf16[8,128,128]{2,1,0:T(8,128)(2,1)S(1)}, u32[]{:S(2)}, u32[]{:S(2)}) collective-permute-start(bf16[8,128,128]{2,1,0:T(8,128)(2,1)} %shard_map.92), channel_id=1, source_target_pairs={{0,1},{1,0},{2,3},{3,2},{4,5},{5,4},{6,7},{7,6},{8,9},{9,8},{10,11... | collective-permute-start | bytes 786440 | tf_op jit(solution)/shard_map/ppermute | solution.py:276
  6.5 17.4 %collective-permute-start.3 = (bf16[16,128,128]{2,1,0:T(8,128)(2,1)S(1)}, bf16[16,128,128]{2,1,0:T(8,128)(2,1)S(1)}, u32[]{:S(2)}, u32[]{:S(2)}) collective-permute-start(bf16[16,128,128]{2,1,0:T(8,128)(2,1)S(1)} %shard_map.93), channel_id=1, source_target_pairs={{0,1},{1,0},{2,3},{3,2},{4,5},{5,4},{6,7},{7,6},{8,9},{9,8},{10,11... | collective-permute-start | bytes 1572872 | tf_op jit(solution)/shard_map/ppermute | solution.py:277
  6.7 0.7 copy-start.1
  14.8 15.6 %collective-permute-start = (bf16[32,128,128]{2,1,0:T(8,128)(2,1)}, bf16[32,128,128]{2,1,0:T(8,128)(2,1)}, u32[]{:S(2)}, u32[]{:S(2)}) collective-permute-start(bf16[32,128,128]{2,1,0:T(8,128)(2,1)} %get-tuple-element.36), channel_id=1, source_target_pairs={{0,8},{8,0},{16,24},{24,16},{1,9},{9,1},{17,25},{25,17},{2,10},{10... | collective-permute-start | bytes 3145736 | tf_op jit(solution)/shard_map/ppermute | solution.py:304
  14.8 9.1 %collective-permute-start.2 = (bf16[8,128,128]{2,1,0:T(8,128)(2,1)S(1)}, bf16[8,128,128]{2,1,0:T(8,128)(2,1)}, u32[]{:S(2)}, u32[]{:S(2)}) collective-permute-start(bf16[8,128,128]{2,1,0:T(8,128)(2,1)S(1)} %collective-permute-done.1.refs_0_), channel_id=1, source_target_pairs={{0,2},{2,0},{4,6},{6,4},{1,3},{3,1},{5,7},{7,5},{8,10},{10,8},{12,... | collective-permute-start | bytes 786440 | tf_op jit(solution)/shard_map/ppermute | solution.py:278
  30.3 19.5 %copy-start.6 = (s32[128,64]{0,1:T(8,128)S(1)}, s32[128,64]{0,1:T(8,128)}, u32[]{:S(2)}) copy-start(s32[128,64]{0,1:T(8,128)} %param.14) | copy-start | bytes 98308
  30.3 4.3 %collective-permute-start.4 = (bf16[32,128,128]{2,1,0:T(8,128)(2,1)S(1)}, bf16[32,128,128]{2,1,0:T(8,128)(2,1)S(1)}, u32[]{:S(2)}, u32[]{:S(2)}) collective-permute-start(bf16[32,128,128]{2,1,0:T(8,128)(2,1)S(1)} %get-tuple-element.40), channel_id=1, source_target_pairs={{0,8},{8,0},{16,24},{24,16},{1,9},{9,1},{17,25},{25,17},{2,10},{10... | collective-permute-start | bytes 3145736 | tf_op jit(solution)/shard_map/ppermute | solution.py:304
  30.4 35.8 %copy-start.3 = (s32[64,8]{0,1:T(8,128)S(1)}, s32[64,8]{0,1:T(8,128)}, u32[]{:S(2)}) copy-start(s32[64,8]{0,1:T(8,128)} %param.16) | copy-start | bytes 6148
  32.9 31.6 %copy-start.5 = (f32[16,128,128]{2,1,0:T(8,128)S(1)}, f32[16,128,128]{2,1,0:T(8,128)}, u32[]{:S(2)}) copy-start(f32[16,128,128]{2,1,0:T(8,128)} %get-tuple-element.38) | copy-start | bytes 3145732
  32.9 14.3 %collective-permute-start.7 = (bf16[16,128,128]{2,1,0:T(8,128)(2,1)S(1)}, bf16[16,128,128]{2,1,0:T(8,128)(2,1)S(1)}, u32[]{:S(2)}, u32[]{:S(2)}) collective-permute-start(bf16[16,128,128]{2,1,0:T(8,128)(2,1)S(1)} %get-tuple-element.46), channel_id=1, source_target_pairs={{0,1},{1,0},{2,3},{3,2},{4,5},{5,4},{6,7},{7,6},{8,9},{9,8},{10,11... | collective-permute-start | bytes 1572872 | tf_op jit(solution)/shard_map/ppermute | solution.py:311
  48.2 13.7 %collective-permute-start.8 = (bf16[16,128,128]{2,1,0:T(8,128)(2,1)}, bf16[16,128,128]{2,1,0:T(8,128)(2,1)S(1)}, u32[]{:S(2)}, u32[]{:S(2)}) collective-permute-start(bf16[16,128,128]{2,1,0:T(8,128)(2,1)} %get-tuple-element.48), channel_id=1, source_target_pairs={{0,16},{8,24},{16,0},{24,8},{1,17},{9,25},{17,1},{25,9},{2,18},{10... | collective-permute-start | bytes 1572872 | tf_op jit(solution)/shard_map/ppermute | solution.py:319
  49.8 3.6 %collective-permute-start.9 = (bf16[128,16]{0,1:T(8,128)(2,1)S(1)}, bf16[128,16]{0,1:T(8,128)(2,1)S(1)}, u32[]{:S(2)}, u32[]{:S(2)}) collective-permute-start(bf16[128,16]{0,1:T(8,128)(2,1)S(1)} %get-tuple-element.74), channel_id=1, source_target_pairs={{0,1},{1,0},{2,3},{3,2},{4,5},{5,4},{6,7},{7,6},{8,9},{9,8},{10,11... | collective-permute-start | bytes 12296 | tf_op jit(solution)/shard_map/ppermute | solution.py:282
  51.4 13.2 %collective-permute-start.5 = (bf16[16,128,128]{2,1,0:T(8,128)(2,1)}, bf16[16,128,128]{2,1,0:T(8,128)(2,1)S(1)}, u32[]{:S(2)}, u32[]{:S(2)}) collective-permute-start(bf16[16,128,128]{2,1,0:T(8,128)(2,1)} %get-tuple-element.42), channel_id=1, source_target_pairs={{0,1},{1,0},{2,3},{3,2},{4,5},{5,4},{6,7},{7,6},{8,9},{9,8},{10,11... | collective-permute-start | bytes 1572872 | tf_op jit(solution)/shard_map/ppermute | solution.py:314
  62.2 3.9 %collective-permute-start.10 = (bf16[16,128,128]{2,1,0:T(8,128)(2,1)S(1)}, bf16[16,128,128]{2,1,0:T(8,128)(2,1)S(1)}, u32[]{:S(2)}, u32[]{:S(2)}) collective-permute-start(bf16[16,128,128]{2,1,0:T(8,128)(2,1)S(1)} %multiply_convert_fusion.1.refs_0_), channel_id=1, source_target_pairs={{0,8},{8,0},{16,24},{24,16},{1,9},{9,1},{17,25},{25,17},{2,10},{10... | collective-permute-start | bytes 1572872 | tf_op jit(solution)/shard_map/ppermute | solution.py:325
  65.5 12.3 %collective-permute-start.6 = (bf16[16,128,128]{2,1,0:T(8,128)(2,1)}, bf16[16,128,128]{2,1,0:T(8,128)(2,1)S(1)}, u32[]{:S(2)}, u32[]{:S(2)}) collective-permute-start(bf16[16,128,128]{2,1,0:T(8,128)(2,1)} %get-tuple-element.44), channel_id=1, source_target_pairs={{0,16},{8,24},{16,0},{24,8},{1,17},{9,25},{17,1},{25,9},{2,18},{10... | collective-permute-start | bytes 1572872 | tf_op jit(solution)/shard_map/ppermute | solution.py:319
  78.2 4.2 %collective-permute-start.11 = (bf16[16,128,128]{2,1,0:T(8,128)(2,1)S(1)}, bf16[16,128,128]{2,1,0:T(8,128)(2,1)S(1)}, u32[]{:S(2)}, u32[]{:S(2)}) collective-permute-start(bf16[16,128,128]{2,1,0:T(8,128)(2,1)S(1)} %multiply_convert_fusion.refs_0_), channel_id=1, source_target_pairs={{0,8},{8,0},{16,24},{24,16},{1,9},{9,1},{17,25},{25,17},{2,10},{10... | collective-permute-start | bytes 1572872 | tf_op jit(solution)/shard_map/ppermute | solution.py:325
  78.3 10.4 %collective-permute-start.24 = (bf16[8,128,128]{2,1,0:T(8,128)(2,1)S(1)}, bf16[8,128,128]{2,1,0:T(8,128)(2,1)S(1)}, u32[]{:S(2)}, u32[]{:S(2)}) collective-permute-start(bf16[8,128,128]{2,1,0:T(8,128)(2,1)S(1)} %get-tuple-element.64), channel_id=1, source_target_pairs={{0,1},{1,0},{2,3},{3,2},{4,5},{5,4},{6,7},{7,6},{8,9},{9,8},{10,11... | collective-permute-start | bytes 786440 | tf_op jit(solution)/shard_map/ppermute | solution.py:335
  80.1 40.7 %collective-permute-start.13 = (bf16[16,128,128]{2,1,0:T(8,128)(2,1)S(1)}, bf16[16,128,128]{2,1,0:T(8,128)(2,1)S(1)}, u32[]{:S(2)}, u32[]{:S(2)}) collective-permute-start(bf16[16,128,128]{2,1,0:T(8,128)(2,1)S(1)} %get-tuple-element.56), channel_id=1, source_target_pairs={{0,1},{1,0},{2,3},{3,2},{4,5},{5,4},{6,7},{7,6},{8,9},{9,8},{10,11... | collective-permute-start | bytes 1572872 | tf_op jit(solution)/shard_map/ppermute | solution.py:335
  80.4 24.0 %collective-permute-start.21 = (bf16[8,128,128]{2,1,0:T(8,128)(2,1)S(1)}, bf16[8,128,128]{2,1,0:T(8,128)(2,1)S(1)}, u32[]{:S(2)}, u32[]{:S(2)}) collective-permute-start(bf16[8,128,128]{2,1,0:T(8,128)(2,1)S(1)} %get-tuple-element.62), channel_id=1, source_target_pairs={{0,1},{1,0},{2,3},{3,2},{4,5},{5,4},{6,7},{7,6},{8,9},{9,8},{10,11... | collective-permute-start | bytes 786440 | tf_op jit(solution)/shard_map/ppermute | solution.py:335
  82.1 37.3 %collective-permute-start.15 = (bf16[8,128,128]{2,1,0:T(8,128)(2,1)S(1)}, bf16[8,128,128]{2,1,0:T(8,128)(2,1)S(1)}, u32[]{:S(2)}, u32[]{:S(2)}) collective-permute-start(bf16[8,128,128]{2,1,0:T(8,128)(2,1)S(1)} %get-tuple-element.58), channel_id=1, source_target_pairs={{0,1},{1,0},{2,3},{3,2},{4,5},{5,4},{6,7},{7,6},{8,9},{9,8},{10,11... | collective-permute-start | bytes 786440 | tf_op jit(solution)/shard_map/ppermute | solution.py:335
  82.4 70.6 %copy-start.4 = (f32[2048]{0:T(1024)S(1)}, f32[2048]{0:T(1024)}, u32[]{:S(2)}) copy-start(f32[2048]{0:T(1024)} %param.17) | copy-start | bytes 24580
  82.4 33.2 %collective-permute-start.18 = (bf16[8,128,128]{2,1,0:T(8,128)(2,1)S(1)}, bf16[8,128,128]{2,1,0:T(8,128)(2,1)S(1)}, u32[]{:S(2)}, u32[]{:S(2)}) collective-permute-start(bf16[8,128,128]{2,1,0:T(8,128)(2,1)S(1)} %get-tuple-element.60), channel_id=1, source_target_pairs={{0,1},{1,0},{2,3},{3,2},{4,5},{5,4},{6,7},{7,6},{8,9},{9,8},{10,11... | collective-permute-start | bytes 786440 | tf_op jit(solution)/shard_map/ppermute | solution.py:335
  88.7 49.9 %collective-permute-start.12 = (bf16[16,128,128]{2,1,0:T(8,128)(2,1)S(1)}, bf16[16,128,128]{2,1,0:T(8,128)(2,1)S(1)}, u32[]{:S(2)}, u32[]{:S(2)}) collective-permute-start(bf16[16,128,128]{2,1,0:T(8,128)(2,1)S(1)} %get-tuple-element.54), channel_id=1, source_target_pairs={{0,1},{1,0},{2,3},{3,2},{4,5},{5,4},{6,7},{7,6},{8,9},{9,8},{10,11... | collective-permute-start | bytes 1572872 | tf_op jit(solution)/shard_map/ppermute | solution.py:335
  104.4 17.8 %collective-permute-start.25 = (bf16[8,128,128]{2,1,0:T(8,128)(2,1)S(1)}, bf16[8,128,128]{2,1,0:T(8,128)(2,1)S(1)}, u32[]{:S(2)}, u32[]{:S(2)}) collective-permute-start(bf16[8,128,128]{2,1,0:T(8,128)(2,1)S(1)} %shard_map.104), channel_id=1, source_target_pairs={{0,2},{6,4},{1,3},{7,5},{8,10},{14,12},{9,11},{15,13},{16,18},{22,... | collective-permute-start | bytes 786440 | tf_op jit(solution)/shard_map/ppermute | solution.py:341
  115.6 10.3 %collective-permute-start.22 = (bf16[8,128,128]{2,1,0:T(8,128)(2,1)S(1)}, bf16[8,128,128]{2,1,0:T(8,128)(2,1)S(1)}, u32[]{:S(2)}, u32[]{:S(2)}) collective-permute-start(bf16[8,128,128]{2,1,0:T(8,128)(2,1)S(1)} %shard_map.102), channel_id=1, source_target_pairs={{0,2},{6,4},{1,3},{7,5},{8,10},{14,12},{9,11},{15,13},{16,18},{22,... | collective-permute-start | bytes 786440 | tf_op jit(solution)/shard_map/ppermute | solution.py:341
  119.4 12.2 %collective-permute-start.19 = (bf16[8,128,128]{2,1,0:T(8,128)(2,1)S(1)}, bf16[8,128,128]{2,1,0:T(8,128)(2,1)S(1)}, u32[]{:S(2)}, u32[]{:S(2)}) collective-permute-start(bf16[8,128,128]{2,1,0:T(8,128)(2,1)S(1)} %shard_map.100), channel_id=1, source_target_pairs={{0,2},{6,4},{1,3},{7,5},{8,10},{14,12},{9,11},{15,13},{16,18},{22,... | collective-permute-start | bytes 786440 | tf_op jit(solution)/shard_map/ppermute | solution.py:341
  120.8 16.4 %collective-permute-start.16 = (bf16[8,128,128]{2,1,0:T(8,128)(2,1)S(1)}, bf16[8,128,128]{2,1,0:T(8,128)(2,1)S(1)}, u32[]{:S(2)}, u32[]{:S(2)}) collective-permute-start(bf16[8,128,128]{2,1,0:T(8,128)(2,1)S(1)} %shard_map.98), channel_id=1, source_target_pairs={{0,2},{6,4},{1,3},{7,5},{8,10},{14,12},{9,11},{15,13},{16,18},{22,... | collective-permute-start | bytes 786440 | tf_op jit(solution)/shard_map/ppermute | solution.py:341
  122.2 30.8 %collective-permute-start.14 = (bf16[16,128,128]{2,1,0:T(8,128)(2,1)S(1)}, bf16[16,128,128]{2,1,0:T(8,128)(2,1)S(1)}, u32[]{:S(2)}, u32[]{:S(2)}) collective-permute-start(bf16[16,128,128]{2,1,0:T(8,128)(2,1)S(1)} %shard_map.97), channel_id=1, source_target_pairs={{0,2},{2,0},{4,6},{6,4},{1,3},{3,1},{5,7},{7,5},{8,10},{10,8},{12,... | collective-permute-start | bytes 1572872 | tf_op jit(solution)/shard_map/ppermute | solution.py:341
  126.0 13.9 %collective-permute-start.26 = (bf16[8,128,128]{2,1,0:T(8,128)(2,1)S(1)}, bf16[8,128,128]{2,1,0:T(8,128)(2,1)S(1)}, u32[]{:S(2)}, u32[]{:S(2)}) collective-permute-start(bf16[8,128,128]{2,1,0:T(8,128)(2,1)S(1)} %shard_map.105), channel_id=1, source_target_pairs={{2,4},{4,2},{3,5},{5,3},{10,12},{12,10},{11,13},{13,11},{18,20},{2... | collective-permute-start | bytes 786440 | tf_op jit(solution)/shard_map/ppermute | solution.py:341
  131.6 8.3 %collective-permute-start.23 = (bf16[8,128,128]{2,1,0:T(8,128)(2,1)S(1)}, bf16[8,128,128]{2,1,0:T(8,128)(2,1)S(1)}, u32[]{:S(2)}, u32[]{:S(2)}) collective-permute-start(bf16[8,128,128]{2,1,0:T(8,128)(2,1)S(1)} %shard_map.103), channel_id=1, source_target_pairs={{2,4},{4,2},{3,5},{5,3},{10,12},{12,10},{11,13},{13,11},{18,20},{2... | collective-permute-start | bytes 786440 | tf_op jit(solution)/shard_map/ppermute | solution.py:341
  137.2 12.9 %collective-permute-start.20 = (bf16[8,128,128]{2,1,0:T(8,128)(2,1)S(1)}, bf16[8,128,128]{2,1,0:T(8,128)(2,1)S(1)}, u32[]{:S(2)}, u32[]{:S(2)}) collective-permute-start(bf16[8,128,128]{2,1,0:T(8,128)(2,1)S(1)} %shard_map.101), channel_id=1, source_target_pairs={{2,6},{4,0},{3,7},{5,1},{10,14},{12,8},{11,15},{13,9},{18,22},{20,... | collective-permute-start | bytes 786440 | tf_op jit(solution)/shard_map/ppermute | solution.py:341
  138.6 14.4 %collective-permute-start.17 = (bf16[8,128,128]{2,1,0:T(8,128)(2,1)S(1)}, bf16[8,128,128]{2,1,0:T(8,128)(2,1)S(1)}, u32[]{:S(2)}, u32[]{:S(2)}) collective-permute-start(bf16[8,128,128]{2,1,0:T(8,128)(2,1)S(1)} %shard_map.99), channel_id=1, source_target_pairs={{2,6},{4,0},{3,7},{5,1},{10,14},{12,8},{11,15},{13,9},{18,22},{20,... | collective-permute-start | bytes 786440 | tf_op jit(solution)/shard_map/ppermute | solution.py:341
